TPU v7x, 32 devices: a whole 2x2x4 slice. The times are simulated.
32 devices in a mesh: cell: 8 (over z, y), spot: 4 (over x, core).
Axes of the slice: x: 2, y: 2, z: 4, core: 2. Of those that a mesh axis runs over, the one named last changes fastest.
Arguments:
- logits: float32 [2, 22528, 2048], P(None, 'cell', 'spot'), may hold values from -9 to 12.5
- filter_logits: float32 [2, 22528], P(None, 'cell'), may hold values from -6 to 9
- expression: float32 [22528, 2048], P('cell', 'spot'), may hold values from 0.1 to 10
- observed: float32 [2, 2048, 2048], P(None, 'cell', 'spot'), may hold values from 0.1 to 30
- gene_mask: int32 [4, 2048], P(None, 'cell'), may hold values 0 or 1
- slide_ids: int32 [2048], P('spot'), may hold values from 0 to 3
- true_counts: int32 [4], replicated, may hold values from 128 to 511
Outputs:
- grad_logits: float32 [2, 22528, 2048], P(None, 'cell', 'spot')
- grad_filter: float32 [2, 22528], P(None, 'cell')
- count_terms: float32 [2, 4], replicated
- loss: float32 [], replicated
All inputs are finite; a program needn't handle non-finite values. No bound on the sum of `gene_mask` on one device may be relied on, other than what follows from the above.
Results may differ from a plain program's by a relative error of at most 0.0003.
Values sent between devices are 32-bit elements; how exact they have to be, the bound alone decides.
No kernel may reach another device: no remote copies, remote signals or barrier semaphores. Data moves between devices by JAX's collectives and lax.ppermute only.
A program may use at most 128 MiB of HBM per device.

v0:
```python
import jax
import jax.numpy as jnp
from jax import lax
from jax.sharding import PartitionSpec as P

G = 2048
SLIDES = 4


count_weight = 0.0625
entropy_weight = 1.0
epsilon = 1e-06
HIGH = lax.Precision.HIGHEST


def on_device(logits, filter_logits, expression, observed, gene_mask, slide_ids, true_counts):
    layers, cell_rows, spot_cols = logits.shape
    cells_all = cell_rows * lax.axis_size("cell")
    gene_rows = G // lax.axis_size("cell")
    kept = jax.nn.sigmoid(filter_logits)
    local_top = jnp.max(logits, axis=1)
    column_top = lax.pmax(local_top, "cell")
    exponent = jnp.exp(logits - column_top[:, None, :])
    column_total, column_kept = lax.psum(
        (jnp.sum(exponent, axis=1), jnp.sum(kept[:, :, None] * exponent, axis=1)), "cell"
    )
    mapping = exponent / column_total[:, None, :]
    column_mass = column_kept / column_total
    weighted = kept[:, :, None] * mapping
    joined = weighted.transpose(1, 0, 2).reshape(cell_rows, layers * spot_cols)
    full_expr = lax.all_gather(expression, "spot", axis=1, tiled=True)
    columns = full_expr
    proj_rows = lax.psum_scatter(
        lax.dot_general(
            columns,
            joined,
            (((0,), (0,)), ((), ())),
            precision=HIGH,
            preferred_element_type=jnp.float32,
        ),
        "cell",
        scatter_dimension=0,
        tiled=True,
    )
    projected = proj_rows.reshape(gene_rows, layers, spot_cols).transpose(1, 0, 2)
    onehot = (slide_ids[:, None] == jnp.arange(SLIDES, dtype=jnp.int32)[None, :]).astype(
        jnp.float32
    )
    flat_proj = projected.reshape(layers * gene_rows, spot_cols)
    flat_obs = observed.reshape(layers * gene_rows, spot_cols)
    stats_local = jnp.stack(
        [
            jnp.dot(flat_proj * flat_obs, onehot, precision=HIGH),
            jnp.dot(flat_proj * flat_proj, onehot, precision=HIGH),
            jnp.dot(flat_obs * flat_obs, onehot, precision=HIGH),
        ]
    )
    mass_local = jnp.dot(column_mass, onehot, precision=HIGH)
    stats, slide_mass = lax.psum((stats_local, mass_local), "spot")
    cross = stats[0].reshape(layers, gene_rows, SLIDES)
    inv_proj = lax.rsqrt(stats[1].reshape(layers, gene_rows, SLIDES) + epsilon)
    inv_obs = lax.rsqrt(stats[2].reshape(layers, gene_rows, SLIDES) + epsilon)
    cosine = cross * inv_proj * inv_obs
    weight_mask = gene_mask.T.astype(jnp.float32)
    gene_local = -jnp.sum(weight_mask[None] * cosine, axis=(1, 2)) / G
    entropy_local = jnp.sum(
        kept * jax.nn.softplus(-filter_logits) + (1.0 - kept) * jax.nn.softplus(filter_logits),
        axis=1,
    )
    gene_sum, entropy_sum = lax.psum((gene_local, entropy_local), "cell")
    counts = true_counts.astype(jnp.float32)
    count_terms = count_weight * ((slide_mass - counts[None]) / counts[None]) ** 2
    loss = (
        jnp.sum(gene_sum) + jnp.sum(count_terms) + entropy_weight * jnp.sum(entropy_sum) / cells_all
    )
    gene_weight = -weight_mask[None] / G
    coef_first = gene_weight * inv_proj * inv_obs
    coef_second = gene_weight * cross * inv_proj**3 * inv_obs
    spread_first = jnp.einsum("lgk,sk->lgs", coef_first, onehot, precision=HIGH)
    spread_second = jnp.einsum("lgk,sk->lgs", coef_second, onehot, precision=HIGH)
    grad_projected = spread_first * observed - spread_second * projected
    grad_count = 2.0 * count_weight * (slide_mass - counts[None]) / (counts[None] * counts[None])
    grad_mass = jnp.dot(grad_count, onehot.T, precision=HIGH)
    grad_rows = grad_projected.transpose(1, 0, 2).reshape(gene_rows, layers * spot_cols)
    columns = full_expr
    grad_joined = jnp.dot(
        columns,
        lax.all_gather(grad_rows, "cell", axis=0, tiled=True),
        precision=HIGH,
        preferred_element_type=jnp.float32,
    )
    grad_weighted = (
        grad_joined.reshape(cell_rows, layers, spot_cols).transpose(1, 0, 2) + grad_mass[:, None, :]
    )
    filter_local = jnp.sum(mapping * grad_weighted, axis=2)
    grad_map = kept[:, :, None] * grad_weighted
    column_local = jnp.sum(mapping * grad_map, axis=1)
    column_back = lax.psum(column_local, "cell")
    grad_kept = lax.psum(filter_local, "spot")
    grad_logits = cells_all * G * (mapping * (grad_map - column_back[:, None, :]))
    slope = kept * (1.0 - kept)
    grad_filter = cells_all * (
        grad_kept * slope - entropy_weight * slope * filter_logits / cells_all
    )
    return (grad_logits, grad_filter, count_terms, loss)


def solution(mesh):
    in_specs = (
        P(None, "cell", "spot"),
        P(None, "cell"),
        P("cell", "spot"),
        P(None, "cell", "spot"),
        P(None, "cell"),
        P("spot"),
        P(),
    )
    out_specs = (P(None, "cell", "spot"), P(None, "cell"), P(), P())
    return jax.shard_map(
        on_device, mesh=mesh, in_specs=in_specs, out_specs=out_specs, check_vma=False
    )
```

profile of v0, /device:TPU:0, one launch (start us, length us, event | category | flops | bytes accessed | tf_op | source)
XLA Modules:
  0.0 692.8 jit_solution(13120452524185625037)
XLA Ops:
  7.2 0.0 all-gather.3.cloned.1.call-start
  7.2 0.7 all-gather.3.cloned.1.call-update
  7.9 0.0 reduce-scatter.2.cloned.1.call-start
  7.9 12.1 %copy.31 = f32[2,2816,512]{1,2,0:T(8,128)} copy(f32[2,2816,512]{2,1,0:T(8,128)} %param.7) | data formatting | bytes 23068672 | tf_op args[0]
  20.0 0.0 copy-start.3
  20.0 7.6 %reduce_max.9 = f32[2,512]{1,0:T(2,128)S(1)} reduce(f32[2,2816,512]{2,1,0:T(8,128)} %param.7, f32[]{:T(128)} %constant.10.clone.1), dimensions={1}, to_apply=%region_0.0 | reduce | flops 2882560 | bytes 11538436 | tf_op jit(solution)/shard_map/reduce_max | solution.py:21
  27.6 22.8 %pmax.7 = f32[2,512]{1,0:T(2,128)S(1)} all-reduce(f32[2,512]{1,0:T(2,128)S(1)} %reduce_max.9), channel_id=1, replica_groups=mesh['cell'=8,'spot'=4] {'cell'}, use_global_device_ids=true, to_apply=%region_1.0 | all-reduce | flops 1024 | bytes 8192 | tf_op jit(solution)/shard_map/pmax | solution.py:22
  50.5 0.0 copy-done.3
  50.5 0.2 fusion.9
  50.7 7.0 %multiply_reduce_fusion.1 = (f32[2,512]{1,0:T(2,128)S(1)}, f32[2,512]{1,0:T(2,128)S(1)}) fusion(f32[2,2816,512]{1,2,0:T(8,128)} %copy.31, f32[2,2816]{1,0:T(2,128)S(1)} %get-tuple-element.26, f32[2,512]{1,0:T(2,128)S(1)} %pmax.7), kind=kLoop, calls=%fused_computation.5 | loop fusion | flops 11532288 | bytes 11569152 | tf_op jit(solution)/shard_map/reduce_sum | solution.py:25
  57.7 17.6 %all-reduce.1 = (f32[2,512]{1,0:T(2,128)S(1)}, f32[2,512]{1,0:T(2,128)S(1)}) all-reduce(f32[2,512]{1,0:T(2,128)S(1)} %get-tuple-element.15, f32[2,512]{1,0:T(2,128)S(1)} %get-tuple-element.14), channel_id=1, replica_groups=mesh['cell'=8,'spot'=4] {'cell'}, use_global_device_ids=true, to_apply=%region_3.0 | all-reduce | flops 2048 | bytes 16384 | tf_op jit(solution)/shard_map/psum | solution.py:24
  75.3 10.4 %broadcast_multiply_fusion = f32[2,2816,512]{1,2,0:T(8,128)} fusion(f32[2,2816]{1,0:T(2,128)S(1)} %get-tuple-element.26, f32[2,512]{1,0:T(2,128)S(1)} %get-tuple-element.19, f32[2,2816,512]{1,2,0:T(8,128)} %copy.31, f32[2,512]{1,0:T(2,128)S(1)} %pmax.7), kind=kLoop, calls=%fused_computation.9 | loop fusion | flops 8650752 | bytes 23099392 | tf_op jit(solution)/shard_map/mul | solution.py:29
  85.7 69.8 %all-gather.3.cloned.1.call-done = f32[2816,2048]{1,0:T(8,128)} async-done(((f32[2816,512]{1,0:T(8,128)}), f32[2816,2048]{1,0:T(8,128)}) %all-gather.3.cloned.1.call-update) | async-done | bytes 23068688 | tf_op jit(solution)/shard_map/all_gather | solution.py:31
  155.5 0.0 copy-start.4
  155.5 0.0 copy-start.2
  155.5 0.0 copy-start.1
  155.5 80.5 %convolution_bitcast_fusion = f32[2048,1024]{0,1:T(8,128)} fusion(f32[2816,1024]{0,1:T(8,128)} %bitcast.60, f32[2816,2048]{1,0:T(8,128)} %all-gather.3.cloned.1.call-done), kind=kOutput, calls=%fused_computation.10 | convolution fusion | flops 70866960384 | bytes 42991616 | tf_op jit(solution)/shard_map/dot_general | solution.py:34
  236.0 0.0 reduce-scatter.2.cloned.1.call-update
  236.1 0.0 copy-start.5
  236.1 0.0 all-gather.5.cloned.1.call-start
  236.1 0.0 copy-done.4
  236.2 0.0 copy-done.2
  236.2 0.1 fusion.18
  236.3 147.8 %reduce-scatter.2.cloned.1.call-done = f32[256,1024]{0,1:T(8,128)} async-done(((f32[2048,1024]{0,1:T(8,128)}), f32[256,1024]{0,1:T(8,128)}) %reduce-scatter.2.cloned.1.call-update) | async-done | bytes 1048592 | tf_op jit(solution)/shard_map/reduce_scatter | solution.py:33
  384.1 1.6 copy.32
  385.7 0.0 copy-done.1
  385.7 0.4 bitcast_multiply_fusion.3
  386.1 0.6 convolution_bitcast_fusion.1
  386.7 0.6 convolution_bitcast_fusion.2
  387.3 0.6 convolution_bitcast_fusion.3
  387.9 10.7 %all-reduce.2 = (f32[3,512,4]{1,2,0:T(4,128)S(1)}, f32[2,4]{1,0:T(2,128)S(1)}) all-reduce(f32[3,512,4]{1,2,0:T(4,128)S(1)} %pad_maximum_fusion, f32[2,4]{1,0:T(2,128)S(1)} %fusion.18), channel_id=1, replica_groups=mesh['cell'=8,'spot'=4] {'spot'}, use_global_device_ids=true, to_apply=%region_5.0 | all-reduce | flops 6152 | bytes 49216 | tf_op jit(solution)/shard_map/psum | solution.py:59
  398.7 0.6 convolution_multiply_fusion.1
  399.3 0.7 fusion.4
  400.0 1.3 copy.40
  401.3 0.0 all-gather.5.cloned.1.call-update
  401.3 0.0 copy-done.5
  401.3 0.1 reduce_sum.94
  401.5 1.2 fusion.39
  402.6 0.1 fusion.19
  402.8 122.5 %all-gather.5.cloned.1.call-done = f32[2048,1024]{0,1:T(8,128)} async-done(((f32[256,1024]{0,1:T(8,128)}), f32[2048,1024]{0,1:T(8,128)}) %all-gather.5.cloned.1.call-update) | async-done | bytes 8388624 | tf_op jit(solution)/shard_map/all_gather | solution.py:88
  525.3 89.6 %fusion.42 = f32[1024,2816]{1,0:T(8,128)S(1)} fusion(f32[2048,1024]{0,1:T(8,128)} %all-gather.5.cloned.1.call-done, f32[2816,2048]{1,0:T(8,128)} %all-gather.3.cloned.1.call-done), kind=kOutput, calls=%fused_computation.71 | convolution fusion | flops 70866960384 | bytes 42991616 | tf_op jit(solution)/shard_map/dot_general | solution.py:86
  614.9 0.0 copy-start
  614.9 11.2 %fusion = (f32[2,2816]{1,0:T(2,128)S(1)}, f32[2,512]{1,0:T(2,128)S(1)}) fusion(f32[2816,2,512]{0,2,1:T(8,128)S(1)} %bitcast.59, f32[2,512]{1,0:T(2,128)S(1)} %fusion.19, f32[2,512]{1,0:T(2,128)S(1)} %get-tuple-element.19, f32[2,2816,512]{1,2,0:T(8,128)} %copy.31, f32[2,512]{1,0:T(2,128)S(1)} %pmax.7, f32[2,2816]{1,0:T(2,128)S(1)} %get-tuple-element.26), kind=kLoop, calls=%fused_computation.2 | loop fusion | flops 23062016 | bytes 23130112 | tf_op jit(solution)/shard_map/reduce_sum | solution.py:95
  626.0 0.0 copy-done
  626.1 18.8 %all-reduce = (f32[2,512]{1,0:T(2,128)S(1)}, f32[2]{0:T(128)S(1)}, f32[2]{0:T(128)S(1)}) all-reduce(f32[2,512]{1,0:T(2,128)S(1)} %get-tuple-element.13, f32[2]{0:T(128)S(1)} %negate_multiply_fusion.1, f32[2]{0:T(128)S(1)} %get-tuple-element.25), channel_id=1, replica_groups=mesh['cell'=8,'spot'=4] {'cell'}, use_global_device_ids=true, to_apply=%region_10.11 | all-reduce | flops 1028 | bytes 8224 | tf_op jit(solution)/shard_map/psum | solution.py:98
  644.9 0.6 reduce_sum.95
  645.5 0.6 reduce_sum.98
  646.1 14.4 %multiply_multiply_fusion = f32[2,2816,512]{1,2,0:T(8,128)} fusion(f32[2,512]{1,0:T(2,128)S(1)} %get-tuple-element.16, f32[2,512]{1,0:T(2,128)S(1)} %fusion.19, f32[2,2816]{1,0:T(2,128)S(1)} %get-tuple-element.26, f32[1024,2816]{1,0:T(8,128)} %copy-done, f32[2,512]{1,0:T(2,128)S(1)} %get-tuple-element.19, f32[2,2816,512]{1,2,0:T(8,128)} %copy.31, ...), kind=kLoop, calls=%fused_computation.3 | loop fusion | flops 20185088 | bytes 34641920 | tf_op jit(solution)/shard_map/mul | solution.py:100
  660.5 11.9 %copy.41 = f32[2,2816,512]{2,1,0:T(8,128)} copy(f32[2,2816,512]{1,2,0:T(8,128)} %multiply_multiply_fusion) | data formatting | bytes 23068672
  672.4 10.2 %psum.61 = f32[2,2816]{1,0:T(2,128)S(1)} all-reduce(f32[2,2816]{1,0:T(2,128)S(1)} %get-tuple-element.12), channel_id=1, replica_groups=mesh['cell'=8,'spot'=4] {'spot'}, use_global_device_ids=true, to_apply=%region_12.13 | all-reduce | flops 5632 | bytes 45056 | tf_op jit(solution)/shard_map/psum | solution.py:99
  682.7 0.6 subtract_multiply_fusion.2
  (10 shorter events, 0.1 us)
Async XLA Ops:
  7.2 148.3 %all-gather.3.cloned.1.call-start = ((), (), s32[]{:S(2)}) async-start(), calls=%async_computation.1 | async-start | bytes 28835840 | tf_op jit(solution)/shard_map/all_gather | solution.py:31
  7.9 376.2 %reduce-scatter.2.cloned.1.call-start = ((), (), s32[]{:S(2)}) async-start(), calls=%async_computation.2 | async-start | bytes 9437184 | tf_op jit(solution)/shard_map/reduce_scatter | solution.py:33
  20.0 30.4 %copy-start.3 = (f32[2,2816]{1,0:T(2,128)S(1)}, f32[2,2816]{1,0:T(2,128)}, u32[]{:S(2)}) copy-start(f32[2,2816]{1,0:T(2,128)} %param.8) | copy-start | bytes 67588
  155.5 80.6 %copy-start.4 = (s32[4,256]{1,0:T(4,128)S(1)}, s32[4,256]{1,0:T(4,128)}, u32[]{:S(2)}) copy-start(s32[4,256]{1,0:T(4,128)} %param.11) | copy-start | bytes 12292
  155.5 80.7 %copy-start.2 = (s32[512]{0:T(512)S(1)}, s32[512]{0:T(512)}, u32[]{:S(2)}) copy-start(s32[512]{0:T(512)} %param.12) | copy-start | bytes 6148
  155.5 230.2 %copy-start.1 = (f32[2,256,512]{2,1,0:T(8,128)S(1)}, f32[2,256,512]{2,1,0:T(8,128)}, u32[]{:S(2)}) copy-start(f32[2,256,512]{2,1,0:T(8,128)} %param.10) | copy-start | bytes 3145732
  236.1 165.2 %copy-start.5 = (s32[4]{0:T(128)S(1)}, s32[4]{0:T(128)}, u32[]{:S(2)}) copy-start(s32[4]{0:T(128)} %param.13) | copy-start | bytes 52
  236.1 289.2 %all-gather.5.cloned.1.call-start = ((), (), s32[]{:S(2)}) async-start(), calls=%async_computation.3 | async-start | bytes 9437184 | tf_op jit(solution)/shard_map/all_gather | solution.py:88
  614.9 11.2 %copy-start = (f32[1024,2816]{1,0:T(8,128)}, f32[1024,2816]{1,0:T(8,128)S(1)}, u32[]{:S(2)}) copy-start(f32[1024,2816]{1,0:T(8,128)S(1)} %fusion.42) | copy-start | bytes 34603012
Sparse Core Ops, SparseCore 0:
  9.5 145.8 all-gather.2
  236.2 147.8 reduce-scatter.1
  401.4 123.8 all-gather.4
where the time goes:
time: 694 us; the launch traced here: 693 us
  waiting for transfers between devices  341 us (49%)
  matrix products  173 us (25%)
  blocking collectives  80.2 us (12%)
  other arithmetic  54.4 us (8%)
  local copies, waits for them, and re-layouts  26.9 us (4%)
  between operations  16.9 us (2%)
    reduce_scatter x1, waiting for transfers between devices, on_device(): lax.psum_scatter(lax.dot_general(columns, joined, (((0,), (0,)), ((), ())...  148 us
    all_gather x1, waiting for transfers between devices, on_device(): lax.all_gather(grad_rows, 'cell', axis=0, tiled=True)  123 us
    dot_general x1, matrix products, on_device(): jnp.dot(columns, lax.all_gather(grad_rows, 'cell', axis=0, tiled=True), p...  89.6 us
    dot_general x1, matrix products, on_device(): lax.dot_general(columns, joined, (((0,), (0,)), ((), ())), precision=HIGH...  80.5 us
    all_gather x1, waiting for transfers between devices, on_device(): full_expr = lax.all_gather(expression, 'spot', axis=1, tiled=True)  69.8 us
    unnamed x14, local copies, waits for them, and re-layouts  24 us
    pmax x1, blocking collectives, on_device(): column_top = lax.pmax(local_top, 'cell')  22.8 us
    psum x1, blocking collectives, on_device(): column_back = lax.psum(column_local, 'cell')  18.8 us
  transfers between devices with their start and end apart: 3, of which 3 were waited for; matrix products, arithmetic and copies ran while one was open for 6% of the time, Pallas kernels for 0%

commit v1 on v0

v1 whole, which is shorter than its diff:
```python
import functools
import math

import jax
import jax.numpy as jnp
from jax import lax
from jax.experimental import pallas as pl
from jax.experimental.pallas import tpu as pltpu
from jax.sharding import PartitionSpec as P

G = 2048
SLIDES = 4
COUNT_WEIGHT = 0.0625
ENTROPY_WEIGHT = 1.0
EPSILON = 1e-06
HIGHEST = lax.Precision.HIGHEST
SETS = [256, 256]
EARLY = [False]
F32 = jnp.float32
BF16 = jnp.bfloat16
NN = (((1,), (0,)), ((), ()))
NT = (((1,), (1,)), ((), ()))
TN = (((0,), (0,)), ((), ()))


def ring_order(n):
    if n < 8:
        return list(range(n))
    ys = math.isqrt(n // 2)
    zs = n // ys
    walk = [(z, 0) for z in range(zs)]
    for i, z in enumerate(reversed(range(zs))):
        cols = range(1, ys)
        walk += [(z, y) for y in (cols if i % 2 == 0 else reversed(cols))]
    return [z * ys + y for z, y in walk]


def split(v):
    hi = v.astype(BF16)
    return hi, (v - hi.astype(F32)).astype(BF16)


def mm(a, b, dims=NN):
    return lax.dot_general(a, b, dims, preferred_element_type=F32)


def mm_onehot(onehot, v, dims):
    hi, lo = split(v)
    if dims is TN:
        return mm(hi, onehot, dims) + mm(lo, onehot, dims)
    return mm(onehot, hi, dims) + mm(onehot, lo, dims)


def mm_exact(a, b, dims=NN):
    return lax.dot_general(a, b, dims, precision=HIGHEST, preferred_element_type=F32)


def row_tile(rows):
    return rows // 2 if rows % 256 == 0 else rows


def tie(v, *others):
    return lax.optimization_barrier((v, *others))[0]


def prep_kernel(x_ref, kept_ref, hi_ref, lo_ref, sum_ref):
    i = pl.program_id(1)
    e = jnp.exp(x_ref[0])
    rows, cols = e.shape
    kept = jnp.transpose(jnp.broadcast_to(kept_ref[0], (128, rows)))
    u = e * jnp.tile(kept, (1, cols // 128))

    @pl.when(i == 0)
    def _():
        sum_ref[...] = jnp.zeros_like(sum_ref)

    sum_ref[0, 0:1, :] += jnp.sum(e, axis=0, keepdims=True)
    sum_ref[0, 1:2, :] += jnp.sum(u, axis=0, keepdims=True)
    hi, lo = split(jnp.transpose(u))
    hi_ref[...] = hi
    lo_ref[...] = lo


def prep(x, kept):
    layers, rows, cols = x.shape
    tile = row_tile(rows)
    wide = pl.BlockSpec((cols, tile), lambda l, i: (l, i))
    return pl.pallas_call(
        prep_kernel,
        grid=(layers, rows // tile),
        in_specs=[
            pl.BlockSpec((1, tile, cols), lambda l, i: (l, i, 0)),
            pl.BlockSpec((1, 1, tile), lambda l, i: (l, 0, i)),
        ],
        out_specs=[wide, wide, pl.BlockSpec((1, 8, cols), lambda l, i: (l, 0, 0))],
        out_shape=[
            jax.ShapeDtypeStruct((layers * cols, rows), BF16),
            jax.ShapeDtypeStruct((layers * cols, rows), BF16),
            jax.ShapeDtypeStruct((layers, 8, cols), F32),
        ],
        name="prep",
        cost_estimate=pl.CostEstimate(
            flops=10 * layers * rows * cols,
            bytes_accessed=8 * layers * rows * cols,
            transcendentals=layers * rows * cols,
        ),
    )(x, kept.reshape(layers, 1, rows))


def fwd_kernel(n, unit, cols, has_sums, me_ref, hi_hbm, lo_hbm, *refs):
    exprs, refs = refs[: len(cols)], refs[len(cols) :]
    sums_ref, refs = (refs[0], refs[1:]) if has_sums else (None, refs)
    outs, (hi, lo, expr, acc, turn, sems) = refs[:n], refs[n:]
    steps, chunk, genes = expr.shape

    def copies(i):
        at = pl.ds(pl.multiple_of(i * chunk, chunk), chunk)
        todo = [
            pltpu.make_async_copy(hi_hbm.at[:, at], hi.at[i], sems.at[0, i]),
            pltpu.make_async_copy(lo_hbm.at[:, at], lo.at[i], sems.at[1, i]),
        ]
        to = 0
        for j, (e, (col, w)) in enumerate(zip(exprs, cols)):
            todo.append(
                pltpu.make_async_copy(
                    e.at[at, col : col + w], expr.at[i, :, to : to + w], sems.at[2 + j, i]
                )
            )
            to += w
        return todo

    def start(i, carry):
        for c in copies(i):
            c.start()
        return carry

    def multiply(i, carry):
        for c in copies(i):
            c.wait()
        eh, el = split(expr[i])
        part = mm(hi[i], eh) + mm(lo[i], eh) + mm(hi[i], el)
        acc[...] = jnp.where(i == 0, part, acc[...] + part)
        return carry

    lax.fori_loop(0, steps, start, 0)
    lax.fori_loop(0, steps, multiply, 0)
    own = unit // n
    row = 0
    for at in range(0, genes, unit):
        turn[...] = jnp.transpose(acc[:, at : at + unit])
        for d in range(n):
            p = lax.rem(me_ref[0] + d, n)
            outs[d][row : row + own, :] = turn[pl.ds(pl.multiple_of(p * own, own), own), :]
        row += own
    if has_sums:
        layers, _, lanes = sums_ref.shape
        for d in range(n):
            for l in range(layers):
                outs[d][row : row + 8, l * lanes : (l + 1) * lanes] = sums_ref[l]


def forward(n, unit, me, hi, lo, exprs, sums=None):
    wide, rows = hi.shape
    chunk = 256 if rows % 256 == 0 else rows
    steps = rows // chunk
    genes = sum(w for _, _, w in exprs)
    out_rows = genes // n + (8 if sums is not None else 0)
    anywhere = pl.BlockSpec(memory_space=pl.ANY)
    in_specs = [pl.BlockSpec(memory_space=pltpu.SMEM)] + [anywhere] * (2 + len(exprs))
    args = [me, hi, lo] + [e for e, _, _ in exprs]
    if sums is not None:
        in_specs.append(pl.BlockSpec(memory_space=pltpu.VMEM))
        args.append(sums)
    cols = [(c, w) for _, c, w in exprs]
    return pl.pallas_call(
        functools.partial(fwd_kernel, n, unit, cols, sums is not None),
        in_specs=in_specs,
        out_shape=[jax.ShapeDtypeStruct((out_rows, wide), F32)] * n,
        scratch_shapes=[
            pltpu.VMEM((steps, wide, chunk), BF16),
            pltpu.VMEM((steps, wide, chunk), BF16),
            pltpu.VMEM((steps, chunk, genes), F32),
            pltpu.VMEM((wide, genes), F32),
            pltpu.VMEM((unit, wide), F32),
            pltpu.SemaphoreType.DMA((2 + len(exprs), steps)),
        ],
        name="fwd",
        cost_estimate=pl.CostEstimate(
            flops=6 * wide * rows * genes,
            bytes_accessed=4 * wide * rows + 4 * rows * genes + 4 * wide * genes,
            transcendentals=0,
        ),
    )(*args)


def deal_kernel(place, unit, obs_ref, mask_ref, out_ref):
    n = len(place)
    layers, rows, _ = obs_ref.shape
    own, units = unit // n, rows // unit
    cut = layers * units * own
    out_ref[:, cut:, :] = jnp.zeros((n, out_ref.shape[1] - cut, out_ref.shape[2]), F32)
    for j in range(n):
        for u in range(units):
            src = slice(u * unit + place[j] * own, u * unit + (place[j] + 1) * own)
            for l in range(layers):
                to = (l * units + u) * own
                out_ref[j, to : to + own, :] = obs_ref[l, src, :]
            slides = mask_ref.shape[0]
            out_ref[j, cut + 8 * u : cut + 8 * u + slides, 0:own] = mask_ref[:, src].astype(F32)


def deal(ring, unit, me, observed, gene_mask):
    layers, rows, cols = observed.shape
    n, own = ring.n, unit // ring.n
    if rows % unit:
        observed = lax.all_gather(observed, "cell", axis=1, tiled=True)
        gene_mask = lax.all_gather(gene_mask, "cell", axis=1, tiled=True)
        units = observed.shape[1] // unit
        pick = lambda a, at: lax.dynamic_index_in_dim(a, me[0], at, keepdims=False)
        obs = pick(observed.reshape(layers, units, n, own, cols), 2)
        mask = pick(gene_mask.astype(F32).reshape(-1, units, n, own), 2).transpose(1, 0, 2)
        mask = jnp.pad(mask, ((0, 0), (0, 8 - mask.shape[1]), (0, cols - own)))
        slab = jnp.concatenate([obs.reshape(-1, cols), mask.reshape(-1, cols)])
        return slab[None], units
    units = rows // unit
    out = pl.pallas_call(
        functools.partial(deal_kernel, ring.place, unit),
        out_shape=jax.ShapeDtypeStruct((n, layers * units * own + 8 * units, cols), F32),
        name="deal",
    )(observed, gene_mask)
    return lax.all_to_all(out, "cell", 0, 0, tiled=True), units


def slide_rows(ids_ref, cols):
    return lax.broadcasted_iota(jnp.int32, (8, cols), 0) == ids_ref[...]


def held_rows(qs, at, lane, inv):
    return jnp.concatenate([q[r : r + rows, lane] for q, (r, rows) in zip(qs, at)], 0) * inv[:, lane]


class Dealt:
    def __init__(self, units, block_units, first, count, own, layers, blocks):
        self.units, self.block_units = units, block_units
        self.first, self.count, self.own = first, count, own
        self.layers, self.blocks = layers, blocks

    def places(self, me_ref):
        for j in range(self.blocks):
            for u in range(self.first, self.first + self.count):
                unit = me_ref[1 + j] * self.block_units + u
                yield unit // self.units, unit % self.units

    def obs(self, me_ref, slab_ref, l):
        rows = [
            slab_ref[s, pl.ds(pl.multiple_of((l * self.units + u) * self.own, self.own), self.own), :]
            for s, u in self.places(me_ref)
        ]
        return jnp.concatenate(rows, 0)

    def mask(self, me_ref, slab_ref):
        cut = self.layers * self.units * self.own
        cols = [
            slab_ref[s, pl.ds(pl.multiple_of(cut + 8 * u, 8), 8), 0 : self.own]
            for s, u in self.places(me_ref)
        ]
        return jnp.concatenate(cols, 1)


def stats_kernel(dealt, at, first, me_ref, ids_ref, tot_ref, slab_ref, *refs):
    qs, out_ref = refs[:-1], refs[-1]
    cols = ids_ref.shape[1]
    layers = tot_ref.shape[1] // cols
    onehot = slide_rows(ids_ref, cols).astype(F32)
    marks = onehot.astype(BF16)
    inv = 1.0 / tot_ref[-8:-7, :]
    for l in range(layers):
        lane = slice(l * cols, (l + 1) * cols)
        proj = held_rows(qs, at, lane, inv)
        obs = dealt.obs(me_ref, slab_ref, l)
        out_ref[24 * l : 24 * l + 8, :] = mm_onehot(marks, proj * obs, NT)
        out_ref[24 * l + 8 : 24 * l + 16, :] = mm_onehot(marks, proj * proj, NT)
        out_ref[24 * l + 16 : 24 * l + 24, :] = mm_onehot(marks, obs * obs, NT)
        if first:
            mass = onehot * (tot_ref[-7:-6, lane] * inv[:, lane])
            row = 24 * layers + 8 * l
            out_ref[row : row + 8, :] = jnp.broadcast_to(
                jnp.sum(mass, axis=1, keepdims=True), (8, out_ref.shape[1])
            )


SMEM_VMEM = lambda smem, vmem: [pl.BlockSpec(memory_space=pltpu.SMEM)] * smem + [
    pl.BlockSpec(memory_space=pltpu.VMEM)
] * vmem


def stats(dealt, me, ids, totals, slab, qs, at, first):
    layers = totals.shape[1] // ids.shape[1]
    genes = sum(r for _, r in at)
    return pl.pallas_call(
        functools.partial(stats_kernel, dealt, at, first),
        in_specs=SMEM_VMEM(1, 3 + len(qs)),
        out_shape=jax.ShapeDtypeStruct(((32 if first else 24) * layers, genes), F32),
        name="stats",
    )(me, ids, totals, slab, *qs)


def swap_lanes(v, group, shift):
    count, size = group
    run = count * size
    out = []
    for base in range(0, v.shape[1], run):
        for i in range(count):
            j = (i - shift) % count
            out.append(v[:, base + j * size : base + (j + 1) * size])
    return jnp.concatenate(out, 1)


def grad_kernel(shifts, dealt, at, xs, first, me_ref, ent_ref, *refs):
    ids_ref, tot_ref, slab_ref, extra_ref = refs[:4]
    refs = refs[4:]
    st_refs, refs = refs[: len(shifts)], refs[len(shifts) :]
    qs, (out_ref, aux_ref) = refs[:-2], refs[-2:]
    cols = ids_ref.shape[1]
    layers = tot_ref.shape[1] // cols
    genes = st_refs[0].shape[1]
    own = genes // (2 * xs)
    onehot = slide_rows(ids_ref, cols).astype(F32)
    marks = onehot.astype(BF16)
    inv = 1.0 / tot_ref[-8:-7, :]
    st = None
    for (dx, dc), ref in zip(shifts, st_refs):
        v = ref[...]
        if dc:
            v = swap_lanes(v, (2, own), 1)
        if dx:
            v = swap_lanes(v, (xs, 2 * own), dx)
        st = v if st is None else st + v
    mask = dealt.mask(me_ref, slab_ref)
    aux_ref[...] = jnp.zeros_like(aux_ref)
    out_rows = out_ref.shape[0]
    if out_rows > genes:
        out_ref[genes:out_rows, :] = jnp.full((out_rows - genes, layers * cols), ent_ref[0], F32)
    for l in range(layers):
        lane = slice(l * cols, (l + 1) * cols)
        cross = st[24 * l : 24 * l + 8]
        inv_proj = lax.rsqrt(st[24 * l + 8 : 24 * l + 16] + EPSILON)
        inv_obs = lax.rsqrt(st[24 * l + 16 : 24 * l + 24] + EPSILON)
        weight = mask * (-1.0 / G)
        term = jnp.sum(weight * (cross * inv_proj * inv_obs), axis=0, keepdims=True)
        spread_first = mm_onehot(marks, weight * inv_proj * inv_obs, TN)
        spread_second = mm_onehot(
            marks, weight * cross * (inv_proj * inv_proj * inv_proj) * inv_obs, TN
        )
        proj = held_rows(qs, at, lane, inv)
        grad = spread_first * dealt.obs(me_ref, slab_ref, l) - spread_second * proj
        out_ref[0:genes, lane] = grad
        back = jnp.sum(grad * proj, axis=0, keepdims=True)
        term = jnp.concatenate([term, jnp.zeros((1, cols - genes), F32)], 1)
        if first:
            mass = st[24 * layers + 8 * l : 24 * layers + 8 * l + 8]
            counts = extra_ref[:, :genes]
            off = (mass - counts) / counts
            slope = 2.0 * COUNT_WEIGHT * (mass - counts) / (counts * counts)
            aux_ref[1:2, lane] = jnp.sum(onehot * slope[:, 0:1], axis=0, keepdims=True)
            aux_ref[8:16, l * cols : l * cols + genes] = COUNT_WEIGHT * (off * off)
        else:
            back = back + extra_ref[0:1, lane]
            term = term + extra_ref[2:3, lane]
        aux_ref[0:1, lane] = back
        aux_ref[2:3, lane] = term
        if out_rows > genes:
            out_ref[genes : genes + 1, lane] = back
            out_ref[genes + 1 : genes + 2, lane] = term


def grads(shifts, dealt, xs, me, ent, ids, totals, slab, extra, sts, qs, at, first, last):
    genes, wide = sum(r for _, r in at), totals.shape[1]
    return pl.pallas_call(
        functools.partial(grad_kernel, shifts, dealt, at, xs, first),
        in_specs=SMEM_VMEM(2, 4 + len(sts) + len(qs)),
        out_shape=[
            jax.ShapeDtypeStruct((genes + (8 if last else 0), wide), F32),
            jax.ShapeDtypeStruct((16, wide), F32),
        ],
        name="grads",
    )(me, ent, ids, totals, slab, extra, *sts, *qs)


def gather_rows(n, unit, me_ref, offsets, blocks, hi, lo):
    own = unit // n
    for d, block in zip(offsets, blocks):
        p = lax.rem(me_ref[0] + d + n, n)
        for j in range(hi.shape[0] // unit):
            h, lw = split(block[j * own : (j + 1) * own, :])
            at = pl.ds(pl.multiple_of(j * unit + p * own, own), own)
            hi[at, :] = h
            lo[at, :] = lw


def product(exprs, hi, lo, lanes):
    eh, el = split(jnp.concatenate([e[...] for e in exprs], 1))
    gh, gl = hi[:, lanes], lo[:, lanes]
    return mm(eh, gh) + mm(eh, gl) + mm(el, gh)


def bwd_first_kernel(n, unit, offsets, priors, me_ref, *refs):
    out_ref, hi, lo = refs[-3:]
    prior, refs = refs[:priors], refs[priors:]
    blocks = refs[: len(offsets)]
    exprs = refs[len(offsets) : -3]

    @pl.when(pl.program_id(0) == 0)
    def _():
        gather_rows(n, unit, me_ref, offsets, blocks, hi, lo)

    total = product(exprs, hi, lo, slice(None))
    for p in prior:
        total = total + p[...]
    out_ref[...] = total


def bwd_last_kernel(n, unit, offsets, scale, splits, me_ref, *refs):
    x_ref, kept_ref, tot_ref, aux_ref = refs[:4]
    refs = refs[4:]
    priors, refs = refs[: len(splits)], refs[len(splits) :]
    grad_ref, filt_ref, hi, lo, back = refs[-5:]
    blocks = refs[: len(offsets)]
    exprs = refs[len(offsets) : -5]
    layers, rows, cols = x_ref.shape

    @pl.when(pl.program_id(0) == 0)
    def _():
        gather_rows(n, unit, me_ref, offsets, blocks, hi, lo)
        total = blocks[0][-8:, :]
        for b in blocks[1:]:
            total += b[-8:, :]
        back[...] = total
        for l in range(layers):
            lane = slice(l * cols, (l + 1) * cols)
            inv = 1.0 / tot_ref[-8:-7, lane]
            mass = tot_ref[-7:-6, lane] * inv
            back[2:3, lane] = inv
            back[3:4, lane] = total[0:1, lane] + aux_ref[1:2, lane] * mass

    ones = jnp.ones((8, cols), F32)
    for l in range(layers):
        lane = slice(l * cols, (l + 1) * cols)
        gw = product(exprs, hi, lo, lane)
        if splits:
            held = [p[:, lane] for p in priors]
            gw = gw + functools.reduce(
                lambda low, j: jnp.where(pl.program_id(0) < splits[j], low, held[j]),
                range(1, len(held)),
                held[0],
            )
        gw = gw + aux_ref[1:2, lane]
        mapping = jnp.exp(x_ref[l]) * back[2:3, lane]
        kept = jnp.transpose(jnp.broadcast_to(kept_ref[l], (128, rows)))
        kept = jnp.tile(kept, (1, cols // 128))
        grad_ref[l] = scale * (mapping * (kept * gw - back[3:4, lane]))
        filt_ref[l] = mm_exact(ones, mapping * gw, NT)[0:1, :]


def backward_first(n, unit, offsets, me, prior, blocks, exprs, begin, rows):
    tile = rows // 4 if rows % 32 == 0 else rows
    wide = blocks[0].shape[1]
    genes = sum(w for _, _, w in exprs)
    skip = begin // tile
    whole = pl.BlockSpec(blocks[0].shape, lambda i: (0, 0))
    return pl.pallas_call(
        functools.partial(bwd_first_kernel, n, unit, offsets, len(prior)),
        grid=(rows // tile,),
        in_specs=[pl.BlockSpec(memory_space=pltpu.SMEM)]
        + [pl.BlockSpec((tile, wide), lambda i: (i, 0))] * len(prior)
        + [whole] * len(blocks)
        + [pl.BlockSpec((tile, w), lambda i, c=c: (i + skip, c)) for _, c, w in exprs],
        out_specs=pl.BlockSpec((tile, wide), lambda i: (i, 0)),
        out_shape=jax.ShapeDtypeStruct((rows, wide), F32),
        scratch_shapes=[pltpu.VMEM((genes, wide), BF16), pltpu.VMEM((genes, wide), BF16)],
        name="bwd_first",
        cost_estimate=pl.CostEstimate(
            flops=6 * rows * genes * wide,
            bytes_accessed=4 * rows * (genes + wide) + 4 * genes * wide,
            transcendentals=0,
        ),
    )(me, *prior, *blocks, *[e for e, _, _ in exprs])


def backward_last(n, unit, offsets, scale, me, x, kept, totals, aux, prior, blocks, exprs):
    tile = 256
    layers, rows, cols = x.shape
    wide = layers * cols
    genes = sum(w for _, _, w in exprs)
    fixed = lambda a: pl.BlockSpec(a.shape, lambda i: (0,) * a.ndim)
    args = [me, x, kept.reshape(layers, 1, rows), totals, aux]
    in_specs = [
        pl.BlockSpec(memory_space=pltpu.SMEM),
        pl.BlockSpec((layers, tile, cols), lambda i: (0, i, 0)),
        pl.BlockSpec((layers, 1, tile), lambda i: (0, 0, i)),
        fixed(totals),
        fixed(aux),
    ]
    args += prior
    splits = []
    for p in prior:
        begin = splits[-1] + prior[len(splits) - 1].shape[0] // tile if splits else 0
        splits.append(begin)
        steps = p.shape[0] // tile
        in_specs.append(
            pl.BlockSpec(
                (tile, wide), lambda i, b=begin, t=steps: (jnp.clip(i - b, 0, t - 1), 0)
            )
        )
    args += list(blocks) + [e for e, _, _ in exprs]
    in_specs += [fixed(b) for b in blocks]
    in_specs += [pl.BlockSpec((tile, w), lambda i, c=c: (i, c)) for _, c, w in exprs]
    return pl.pallas_call(
        functools.partial(bwd_last_kernel, n, unit, offsets, scale, splits),
        grid=(rows // tile,),
        in_specs=in_specs,
        out_specs=[
            pl.BlockSpec((layers, tile, cols), lambda i: (0, i, 0)),
            pl.BlockSpec((layers, 1, tile), lambda i: (0, 0, i)),
        ],
        out_shape=[
            jax.ShapeDtypeStruct((layers, rows, cols), F32),
            jax.ShapeDtypeStruct((layers, 1, rows), F32),
        ],
        scratch_shapes=[
            pltpu.VMEM((genes, wide), BF16),
            pltpu.VMEM((genes, wide), BF16),
            pltpu.VMEM((8, wide), F32),
        ],
        name="bwd_last",
        cost_estimate=pl.CostEstimate(
            flops=6 * rows * genes * wide,
            bytes_accessed=4 * rows * (genes + 3 * wide) + 4 * genes * wide,
            transcendentals=rows * wide,
        ),
    )(*args)


class Ring:
    def __init__(self, n):
        self.n = n
        order = ring_order(n)
        self.place = [order.index(i) for i in range(n)]
        right = [(order[i], order[(i + 1) % n]) for i in range(n)]
        self.dirs = (right, [(b, a) for a, b in right])
        self.far = n // 2
        self.near = n - 1 - self.far

    def hop(self, v, way):
        return lax.ppermute(v, "cell", self.dirs[way])


class Scatter:
    def __init__(self, ring, v, flip):
        self.ring, self.v, self.flip = ring, v, flip
        self.sign = -1 if flip else 1
        self.step = 0
        self.flying = False
        self.r, self.l = self.at(ring.far), self.at(-ring.near)

    def at(self, d):
        return self.v[(self.sign * d) % self.ring.n]

    def hop(self):
        ring = self.ring
        self.mark = self.r
        self.r = ring.hop(self.r, int(self.flip))
        if self.step < ring.near:
            self.l = ring.hop(self.l, 1 - int(self.flip))
        self.step += 1
        self.flying = True

    def add(self, *after):
        ring, s = self.ring, self.step - 1
        self.flying = False
        if after:
            self.r, self.l = lax.optimization_barrier((self.r, self.l, *after))[:2]
        if s < ring.far - 1:
            self.r = self.r + self.at(ring.far - 1 - s)
        if s < ring.near - 1:
            self.l = self.l + self.at(s + 1 - ring.near)
        if self.step == ring.far:
            self.r = self.r + self.l + self.at(0)

    def advance(self, *after):
        if self.flying:
            self.add(*after)
        if self.step < self.ring.far:
            self.hop()

    def finish(self):
        while self.flying:
            self.advance()
        return self.r


class Gather:
    def __init__(self, ring, v, flip):
        self.ring, self.flip = ring, flip
        self.sign = -1 if flip else 1
        self.blocks, self.offsets = [v], [0]
        self.r = self.l = v
        self.step = 0

    def advance(self, *after):
        ring = self.ring
        if self.step == ring.far:
            return
        if after:
            self.r, self.l = lax.optimization_barrier((self.r, self.l, *after))[:2]
        self.mark = self.r
        self.step += 1
        self.r = ring.hop(self.r, int(self.flip))
        self.blocks.append(self.r)
        self.offsets.append(-self.sign * self.step)
        if self.step <= ring.near:
            self.l = ring.hop(self.l, 1 - int(self.flip))
            self.blocks.append(self.l)
            self.offsets.append(self.sign * self.step)

    def finish(self):
        while self.step < self.ring.far:
            self.advance()
        return self.blocks


def on_device(logits, filter_logits, expression, observed, gene_mask, slide_ids, true_counts):
    layers, cell_rows, spot_cols = logits.shape
    n = lax.axis_size("cell")
    spots = lax.axis_size("spot")
    cells_all = cell_rows * n
    xs = spots // 2
    width = expression.shape[1]
    widths = SETS if sum(SETS) == width and all(w % (16 * n) == 0 for w in SETS) else [width]
    early = EARLY
    starts = [sum(widths[:h]) for h in range(len(widths))]
    owns = [w // n for w in widths]
    unit = math.gcd(*widths)
    sets = len(widths)
    ring = Ring(n)
    spot = lax.axis_index("spot")
    blocks_at = [
        lax.rem(spot // 2 - dx + xs, xs) * 2 + (spot % 2 + dc) % 2
        for dx in range(xs)
        for dc in range(2)
    ]
    me = jnp.stack([jnp.asarray(ring.place, jnp.int32)[lax.axis_index("cell")], *blocks_at])

    def send(v, dx, dc):
        pairs = []
        for s in range(spots):
            x, c = s // 2, s % 2
            pairs.append((s, ((x + dx) % xs) * 2 + (c ^ dc)))
        return lax.ppermute(v, "spot", pairs)

    expr, far = {}, {}
    held = expression
    for h in range(sets):
        piece = held[:, starts[h] : starts[h] + widths[h]]
        held = tie(expression, piece)
        for dx in range(1, xs):
            far[dx, h] = send(piece, dx, 0)
    partner = send(expression, 0, 1)
    for h in range(sets):
        col = starts[h] // widths[h]
        expr[0, 0, h] = (expression, col, widths[h])
        expr[0, 1, h] = (partner, col, widths[h])

    kept = jax.nn.sigmoid(filter_logits)
    entropy = jnp.sum(
        kept * jax.nn.softplus(-filter_logits) + (1.0 - kept) * jax.nn.softplus(filter_logits)
    ).reshape(1)

    hi, lo, sums = prep(logits, kept)

    def project(chosen, dxs, after=(), sums=None):
        parts = [
            (expr[dx, dc, h][0], expr[dx, dc, h][1] * widths[h], widths[h])
            for h in chosen
            for dx in dxs
            for dc in range(2)
        ]
        return forward(n, unit, me, tie(hi, *after) if after else hi, lo, parts, sums)

    def begin_far(h, after):
        for dx in range(1, xs):
            piece = tie(far[dx, h], after)
            expr[dx, 0, h] = (piece, 0, widths[h])
            expr[dx, 1, h] = (send(piece, 0, 1), 0, widths[h])

    away = range(1, xs)
    out = project(range(sets), [0], sums=sums)
    near = Scatter(ring, out, False)
    near.hop()
    slab, units = deal(ring, unit, me, tie(observed, near.mark), gene_mask)
    near.advance()
    begin_far(0, near.mark)
    near.advance()
    out = project([0], away, (near.mark,))
    rings = [Scatter(ring, out, True)]
    near.advance(out[0])
    rings[0].hop()
    near.finish()
    totals = near.r

    ids = slide_ids.reshape(1, spot_cols)
    extra = jnp.broadcast_to(
        jnp.pad(true_counts.astype(F32), (0, 8 - SLIDES), constant_values=1.0)[:, None],
        (8, 2 * xs * owns[0]),
    )
    shifts = [(dx, dc) for dx in range(xs) for dc in range(2)]
    gathers = []
    aux = None

    def begin(h, after):
        begin_far(h, after)
        out = project([h], away, (after,))
        rings.append(Scatter(ring, out, h % 2 == 0))
        return out[0]

    for h in range(sets):
        first, last = h == 0, h == sets - 1
        mine = rings[h]
        while mine.step < ring.far - 1:
            mine.advance()
            for g in gathers:
                g.advance()
        if not last and early[h]:
            out = begin(h + 1, mine.mark)
            mine.advance(out)
            rings[h + 1].hop()
        mine.finish()
        dealt = Dealt(
            units, width // unit, starts[h] // unit, widths[h] // unit, unit // n, layers, 2 * xs
        )
        at = [
            (sum(2 * owns[i] for i in range(h)), 2 * owns[h]),
            (0, 2 * (xs - 1) * owns[h]),
        ]
        qs = [near.r, mine.r]
        st = stats(dealt, me, ids, totals, slab, qs, at, first)
        sts = [st] + [send(st, dx, dc) for dx, dc in shifts[1:]]
        gp, extra = grads(
            shifts, dealt, xs, me, entropy, ids, totals, slab, extra, sts, qs, at, first, last
        )
        if first:
            aux = extra
        gathers.append(Gather(ring, gp, h % 2 == 0))
        gathers[-1].advance()
        if not last and not early[h]:
            begin(h + 1, gp)
            rings[h + 1].hop()
    tail = gathers[-1]
    parts = 2 if cell_rows % 512 == 0 else 1
    prior = [[] for _ in range(parts)]
    mark = tail.mark
    for h in range(sets - 1):
        blocks = gathers[h].finish()
        exprs = [expr[dx, dc, h] for dx in range(xs) for dc in range(2)]
        for j in range(parts):
            share = cell_rows // parts
            prior[j] = [
                backward_first(
                    n,
                    unit,
                    gathers[h].offsets,
                    tie(me, mark),
                    prior[j],
                    blocks,
                    exprs,
                    j * share,
                    share,
                )
            ]
            mark = tail.r
            tail.advance(prior[j][0])
    blocks, offsets = tail.finish(), tail.offsets
    exprs = [expr[dx, dc, sets - 1] for dx in range(xs) for dc in range(2)]
    grad_logits, filt = backward_last(
        n,
        unit,
        offsets,
        float(cells_all * G),
        me,
        logits,
        kept,
        totals,
        aux,
        [p for ps in prior for p in ps],
        blocks,
        exprs,
    )
    tails = sum(b[-8:] for b in blocks)
    count_terms = jnp.stack([aux[8 : 8 + SLIDES, l * spot_cols] for l in range(layers)])
    loss = jnp.sum(tails[1]) + jnp.sum(count_terms) + ENTROPY_WEIGHT * tails[-1, 0] / cells_all
    filt = filt.reshape(layers, cell_rows)
    grad_kept = filt
    for dx, dc in shifts[1:]:
        grad_kept = grad_kept + send(filt, dx, dc)
    slope = kept * (1.0 - kept)
    grad_filter = cells_all * (grad_kept * slope - ENTROPY_WEIGHT * slope * filter_logits / cells_all)
    return (grad_logits, grad_filter, count_terms, loss)


def solution(mesh):
    in_specs = (
        P(None, "cell", "spot"),
        P(None, "cell"),
        P("cell", "spot"),
        P(None, "cell", "spot"),
        P(None, "cell"),
        P("spot"),
        P(),
    )
    out_specs = (P(None, "cell", "spot"), P(None, "cell"), P(), P())
    return jax.shard_map(
        on_device, mesh=mesh, in_specs=in_specs, out_specs=out_specs, check_vma=False
    )
```

time: 694 us -> 393 us (0.57)
  waiting for transfers between devices: 341 us -> 138 us
  matrix products: 173 us -> 0 us
  Pallas kernels: 0 us -> 149 us
  blocking collectives: 80.2 us -> 0 us
  starting transfers between devices: 0.12 us -> 66.7 us
  other arithmetic: 54.4 us -> 18 us
  between operations: 16.9 us -> 4.74 us
  local copies, waits for them, and re-layouts: 26.9 us -> 15 us
    all_gather x2 -> x0, waiting for transfers between devices: 192 us -> none  [the longest x1 123 us: on_device(): lax.all_gather(grad_rows, 'cell', axis=0, tiled=True)]
    dot_general x9 -> x0, matrix products: 173 us -> none  [the longest x1 89.6 us: on_device(): jnp.dot(columns, lax.all_gather(grad_rows, 'cell', axis=0, tiled=True), p...]
    pallas_call x0 -> x11, Pallas kernels: none -> 149 us  [the longest x3 56.7 us: forward(): pl.pallas_call(functools.partial(fwd_kernel, n, unit, cols, sums is not N...]
    reduce_scatter x1 -> x0, waiting for transfers between devices: 148 us -> none  [on_device(): lax.psum_scatter(lax.dot_general(columns, joined, (((0,), (0,)), ((), ())...]
    ppermute x0 -> x49, waiting for transfers between devices: none -> 138 us  [the longest x35 126 us: hop(): return lax.ppermute(v, 'cell', self.dirs[way])]
    ppermute x0 -> x49, starting transfers between devices: none -> 61.8 us  [the longest x35 51.3 us: hop(): return lax.ppermute(v, 'cell', self.dirs[way])]
    psum x4 -> x0, blocking collectives: 57.4 us -> none  [the longest x1 18.8 us: on_device(): column_back = lax.psum(column_local, 'cell')]
    mul x5 -> x1, other arithmetic: 25.8 us -> 1.39 us  [on_device(): cells_all * (grad_kept * slope - ENTROPY_WEIGHT * slope * filter_logits /...]
  transfers between devices with their start and end apart: 3 -> 50, of which waited for: 3 -> 23; matrix products, arithmetic and copies ran while one was open for 6% -> 7% of each run, Pallas kernels for 0% -> 28%
where the time goes in v1:
time: 393 us; the launch traced here: 392 us
  Pallas kernels  149 us (38%)
  waiting for transfers between devices  138 us (35%)
  starting transfers between devices  66.7 us (17%)
  other arithmetic  18 us (5%)
  local copies, waits for them, and re-layouts  15 us (4%)
  between operations  4.74 us (1%)
    ppermute x35, waiting for transfers between devices, hop(): return lax.ppermute(v, 'cell', self.dirs[way])  126 us
    pallas_call x3, Pallas kernels, forward(): pl.pallas_call(functools.partial(fwd_kernel, n, unit, cols, sums is not N...  56.7 us
    ppermute x35, starting transfers between devices, hop(): return lax.ppermute(v, 'cell', self.dirs[way])  51.3 us
    pallas_call x1, Pallas kernels, backward_last(): pl.pallas_call(functools.partial(bwd_last_kernel, n, unit, offsets, scale...  41.5 us
    pallas_call x1, Pallas kernels, backward_first(): pl.pallas_call(functools.partial(bwd_first_kernel, n, unit, offsets, len(...  24 us
    ppermute x14, waiting for transfers between devices, send(): return lax.ppermute(v, 'spot', pairs)  12.1 us
    pallas_call x1, Pallas kernels, prep(): pl.pallas_call(prep_kernel, grid=(layers, rows // tile), in_specs=[pl.Blo...  11.2 us
    ppermute x14, starting transfers between devices, send(): return lax.ppermute(v, 'spot', pairs)  10.5 us
  transfers between devices with their start and end apart: 50, of which 23 were waited for; matrix products, arithmetic and copies ran while one was open for 7% of the time, Pallas kernels for 28%

profile of v1, /device:TPU:0, one launch (start us, length us, event | category | flops | bytes accessed | tf_op | source)
XLA Modules:
  0.0 392.3 jit_solution(9291402918834653257)
XLA Ops:
  1.2 2.0 slice.42
  3.2 2.6 collective-permute-start.7
  7.8 1.3 stack.22.me_ref
  9.0 11.2 %prep.1 = (bf16[1024,2816]{1,0:T(8,128)(2,1)}, bf16[1024,2816]{1,0:T(8,128)(2,1)}, f32[2,8,512]{2,1,0:T(8,128)}) custom-call(f32[2,2816,512]{2,1,0:T(8,128)} %refs_0_.3, f32[2,1,2816]{2,1,0:T(1,128)} %reshape.24.kept_ref.refs_1_), custom_call_target="tpu_custom_call" | custom-call | flops 28835840 | bytes 23068672 | tf_op jit(solution)/shard_map/prep/pallas_call | solution.py:88
  20.3 26.3 %fwd.3 = (f32[136,1024]{1,0:T(8,128)}, f32[136,1024]{1,0:T(8,128)}, f32[136,1024]{1,0:T(8,128)}, f32[136,1024]{1,0:T(8,128)}, f32[136,1024]{1,0:T(8,128)}, /*ind...) custom-call(s32[5]{0:T(128)} %stack.22.me_ref, bf16[1024,2816]{1,0:T(8,128)(2,1)} %get-tuple-element.73.hi_hbm, ...), custom_call_target="tpu_custom_call" | custom-call | flops 17716740096 | bytes 27262976 | tf_op jit(solution)/shard_map/fwd/pallas_call | solution.py:175
  46.5 1.6 collective-permute-start.1
  48.2 13.4 %collective-permute-done.1 = f32[136,1024]{1,0:T(8,128)S(1)} collective-permute-done((f32[136,1024]{1,0:T(8,128)}, f32[136,1024]{1,0:T(8,128)S(1)}, u32[]{:S(2)}, u32[]{:S(2)}) %collective-permute-start.1) | collective-permute-done | bytes 557088 | tf_op jit(solution)/shard_map/ppermute | solution.py:555
  62.7 6.3 %collective-permute-done.7.refs_0_.refs_10_ = f32[2816,256]{1,0:T(8,128)} collective-permute-done((f32[2816,256]{1,0:T(8,128)S(1)}, f32[2816,256]{1,0:T(8,128)}, u32[]{:S(2)}, u32[]{:S(2)}) %collective-permute-start.7) | collective-permute-done | bytes 2883616 | tf_op jit(solution)/shard_map/ppermute | solution.py:659
  69.0 1.8 collective-permute-start.4
  70.8 3.6 slice.43
  74.4 1.5 collective-permute-start.20
  76.4 7.9 %collective-permute-done.4 = f32[136,1024]{1,0:T(8,128)S(1)} collective-permute-done((f32[136,1024]{1,0:T(8,128)}, f32[136,1024]{1,0:T(8,128)S(1)}, u32[]{:S(2)}, u32[]{:S(2)}) %collective-permute-start.4) | collective-permute-done | bytes 557088 | tf_op jit(solution)/shard_map/ppermute | solution.py:555
  85.2 1.7 collective-permute-start.5
  86.9 2.4 deal.1
  89.3 4.9 %all-to-all-start = ((f32[8,72,512]{2,1,0:T(8,128)}), f32[8,72,512]{2,1,0:T(8,128)S(1)}, u32[]{:S(2)}, u32[]{:S(2)}) async-start(f32[8,72,512]{2,1,0:T(8,128)} %deal.1), calls=%async_computation | async-start | bytes 2359296 | tf_op jit(solution)/shard_map/all_to_all | solution.py:231
  94.2 2.1 collective-permute-start.3
  96.3 6.8 %collective-permute-done.5 = f32[136,1024]{1,0:T(8,128)} collective-permute-done((f32[136,1024]{1,0:T(8,128)}, f32[136,1024]{1,0:T(8,128)}, u32[]{:S(2)}, u32[]{:S(2)}) %collective-permute-start.5) | collective-permute-done | bytes 557088 | tf_op jit(solution)/shard_map/ppermute | solution.py:555
  103.1 1.9 add.175
  105.0 3.2 collective-permute-start.6
  108.3 15.2 %fwd.4 = (f32[64,1024]{1,0:T(8,128)}, f32[64,1024]{1,0:T(8,128)}, f32[64,1024]{1,0:T(8,128)}, f32[64,1024]{1,0:T(8,128)}, f32[64,1024]{1,0:T(8,128)}, /*index=5*...) custom-call(s32[5]{0:T(128)} %stack.22.me_ref, bf16[1024,2816]{1,0:T(8,128)(2,1)} %get-tuple-element.73.hi_hbm, ...), custom_call_target="tpu_custom_call" | custom-call | flops 8858370048 | bytes 19398656 | tf_op jit(solution)/shard_map/fwd/pallas_call | solution.py:175
  123.5 3.0 collective-permute-start.10
  126.5 5.3 %collective-permute-done.6 = f32[136,1024]{1,0:T(8,128)S(1)} collective-permute-done((f32[136,1024]{1,0:T(8,128)}, f32[136,1024]{1,0:T(8,128)S(1)}, u32[]{:S(2)}, u32[]{:S(2)}) %collective-permute-start.6) | collective-permute-done | bytes 557088 | tf_op jit(solution)/shard_map/ppermute | solution.py:555
  131.9 8.2 %collective-permute-start.9 = (f32[136,1024]{1,0:T(8,128)S(1)}, f32[136,1024]{1,0:T(8,128)S(1)}, u32[]{:S(2)}, u32[]{:S(2)}) collective-permute-start(f32[136,1024]{1,0:T(8,128)S(1)} %add.176), channel_id=1, source_target_pairs={{0,8},{8,16},{16,24},{24,28},{28,20},{20,12},{12,4},{4,0},{1,9},{9... | collective-permute-start | bytes 1671176 | tf_op jit(solution)/shard_map/ppermute | solution.py:555
  141.1 2.0 collective-permute-start.11
  143.1 12.5 %collective-permute-done.14 = f32[64,1024]{1,0:T(8,128)S(1)} collective-permute-done((f32[64,1024]{1,0:T(8,128)}, f32[64,1024]{1,0:T(8,128)S(1)}, u32[]{:S(2)}, u32[]{:S(2)}) %collective-permute-start.14) | collective-permute-done | bytes 262176 | tf_op jit(solution)/shard_map/ppermute | solution.py:555
  156.6 2.4 collective-permute-start.15
  159.1 5.3 %collective-permute-done.15 = f32[64,1024]{1,0:T(8,128)S(1)} collective-permute-done((f32[64,1024]{1,0:T(8,128)S(1)}, f32[64,1024]{1,0:T(8,128)S(1)}, u32[]{:S(2)}, u32[]{:S(2)}) %collective-permute-start.15) | collective-permute-done | bytes 262176 | tf_op jit(solution)/shard_map/ppermute | solution.py:555
  164.5 2.5 collective-permute-start.16
  168.1 2.8 collective-permute-done.16
  170.9 2.6 collective-permute-done.13
  175.3 2.9 stats.2.refs_4_
  178.2 1.5 collective-permute-start.18
  180.1 2.2 collective-permute-done.18.refs_6_
  183.9 4.0 %grads.2 = (f32[128,1024]{1,0:T(8,128)}, f32[16,1024]{1,0:T(8,128)}) custom-call(s32[5]{0:T(128)} %stack.22.me_ref, f32[1]{0:T(128)} %bitcast.4.ent_ref, s32[1,512]{1,0:T(1,128)} %bitcast.15, f32[136,1024]{1,0:T(8,128)} %add_add_fusion.tot_ref.refs_0_.refs_1_.refs_8_.refs_2_, f32[8,72,512]{2,1,0:T(8,128)} %copy-done, f32[8,128]{1,0:T(8,128)} %broadcast_in_dim.2.refs_3_, ...), custom_call_target="tpu_custom_call" | custom-call | tf_op jit(solution)/shard_map/grads/pallas_call | solution.py:379
  188.1 2.0 collective-permute-start.33
  190.1 12.3 %collective-permute-done.32.refs_1_ = f32[128,1024]{1,0:T(8,128)S(1)} collective-permute-done((f32[128,1024]{1,0:T(8,128)}, f32[128,1024]{1,0:T(8,128)S(1)}, u32[]{:S(2)}, u32[]{:S(2)}) %collective-permute-start.32) | collective-permute-done | bytes 524320 | tf_op jit(solution)/shard_map/ppermute | solution.py:555
  202.7 1.6 copy-done.25
  204.3 15.2 %fwd.5 = (f32[64,1024]{1,0:T(8,128)}, f32[64,1024]{1,0:T(8,128)}, f32[64,1024]{1,0:T(8,128)}, f32[64,1024]{1,0:T(8,128)}, f32[64,1024]{1,0:T(8,128)}, /*index=5*...) custom-call(s32[5]{0:T(128)} %stack.22.me_ref, bf16[1024,2816]{1,0:T(8,128)(2,1)} %get-tuple-element.73.hi_hbm, ...), custom_call_target="tpu_custom_call" | custom-call | flops 8858370048 | bytes 19398656 | tf_op jit(solution)/shard_map/fwd/pallas_call | solution.py:175
  219.6 1.8 collective-permute-start.22
  221.7 5.9 %collective-permute-done.22 = f32[64,1024]{1,0:T(8,128)S(1)} collective-permute-done((f32[64,1024]{1,0:T(8,128)}, f32[64,1024]{1,0:T(8,128)S(1)}, u32[]{:S(2)}, u32[]{:S(2)}) %collective-permute-start.22) | collective-permute-done | bytes 262176 | tf_op jit(solution)/shard_map/ppermute | solution.py:555
  228.6 1.5 collective-permute-start.23
  230.4 1.7 collective-permute-start.36
  233.7 4.1 %collective-permute-done.23 = f32[64,1024]{1,0:T(8,128)S(1)} collective-permute-done((f32[64,1024]{1,0:T(8,128)S(1)}, f32[64,1024]{1,0:T(8,128)S(1)}, u32[]{:S(2)}, u32[]{:S(2)}) %collective-permute-start.23) | collective-permute-done | bytes 262176 | tf_op jit(solution)/shard_map/ppermute | solution.py:555
  238.8 1.5 collective-permute-start.24
  240.3 8.0 %collective-permute-done.27 = f32[64,1024]{1,0:T(8,128)S(1)} collective-permute-done((f32[64,1024]{1,0:T(8,128)S(1)}, f32[64,1024]{1,0:T(8,128)S(1)}, u32[]{:S(2)}, u32[]{:S(2)}) %collective-permute-start.27) | collective-permute-done | bytes 262176 | tf_op jit(solution)/shard_map/ppermute | solution.py:555
  249.3 1.4 collective-permute-start.28
  250.7 1.7 collective-permute-done.24
  252.4 1.2 collective-permute-start.25
  254.0 1.7 collective-permute-start.38
  255.7 1.3 collective-permute-done.28
  257.0 4.7 %collective-permute-done.25 = f32[64,1024]{1,0:T(8,128)S(1)} collective-permute-done((f32[64,1024]{1,0:T(8,128)S(1)}, f32[64,1024]{1,0:T(8,128)S(1)}, u32[]{:S(2)}, u32[]{:S(2)}) %collective-permute-start.25) | collective-permute-done | bytes 262176 | tf_op jit(solution)/shard_map/ppermute | solution.py:555
  262.4 2.8 stats.3.refs_4_
  267.1 2.2 collective-permute-done.30.refs_6_
  270.3 4.0 %grads.3 = (f32[136,1024]{1,0:T(8,128)}, f32[16,1024]{1,0:T(8,128)}) custom-call(s32[5]{0:T(128)} %stack.22.me_ref, f32[1]{0:T(128)} %bitcast.4.ent_ref, s32[1,512]{1,0:T(1,128)} %bitcast.17, f32[136,1024]{1,0:T(8,128)} %add_add_fusion.tot_ref.refs_0_.refs_1_.refs_8_.refs_2_, f32[8,72,512]{2,1,0:T(8,128)} %copy-done, f32[16,1024]{1,0:T(8,128)} %get-tuple-element.71.refs_3_, ...), custom_call_target="tpu_custom_call" | custom-call | tf_op jit(solution)/shard_map/grads/pallas_call | solution.py:379
  274.3 1.2 collective-permute-start.39
  278.0 24.0 %bwd_first.1.refs_4_ = f32[2816,1024]{1,0:T(8,128)} custom-call(s32[5]{0:T(128)} %stack.22.me_ref, f32[128,1024]{1,0:T(8,128)} %get-tuple-element.72.refs_0_, f32[128,1024]{1,0:T(8,128)} %copy-done.26, f32[128,1024]{1,0:T(8,128)} %collective-permute-done.33.refs_2_, f32[128,1024]{1,0:T(8,128)} %collective-permute-done.34.refs_3_, f32[128,1024]{1,0:T(8,128)} %copy-done.27, ...), custom_call_target="tpu_custom_call" | custom-call | flops 17716740096 | bytes 27262976 | tf_op jit(solution)/shard_map/bwd_first/pallas_call | solution.py:471
  302.0 1.2 collective-permute-start.41
  304.1 12.2 %collective-permute-done.41.refs_8_ = f32[136,1024]{1,0:T(8,128)S(1)} collective-permute-done((f32[136,1024]{1,0:T(8,128)S(1)}, f32[136,1024]{1,0:T(8,128)S(1)}, u32[]{:S(2)}, u32[]{:S(2)}) %collective-permute-start.41) | collective-permute-done | bytes 557088 | tf_op jit(solution)/shard_map/ppermute | solution.py:555
  318.3 11.3 %collective-permute-done.43.refs_10_ = f32[136,1024]{1,0:T(8,128)S(1)} collective-permute-done((f32[136,1024]{1,0:T(8,128)S(1)}, f32[136,1024]{1,0:T(8,128)S(1)}, u32[]{:S(2)}, u32[]{:S(2)}) %collective-permute-start.43) | collective-permute-done | bytes 557088 | tf_op jit(solution)/shard_map/ppermute | solution.py:555
  329.6 1.2 collective-permute-start.45
  330.8 1.3 slice_reduce_fusion.1
  334.0 8.2 %collective-permute-done.45.refs_12_ = f32[136,1024]{1,0:T(8,128)} collective-permute-done((f32[136,1024]{1,0:T(8,128)S(1)}, f32[136,1024]{1,0:T(8,128)}, u32[]{:S(2)}, u32[]{:S(2)}) %collective-permute-start.45) | collective-permute-done | bytes 557088 | tf_op jit(solution)/shard_map/ppermute | solution.py:555
  342.2 41.5 %bwd_last.1 = (f32[2,2816,512]{2,1,0:T(8,128)}, f32[2,1,2816]{2,1,0:T(1,128)}) custom-call(s32[5]{0:T(128)} %stack.22.me_ref, f32[2,2816,512]{2,1,0:T(8,128)} %refs_0_.3, f32[2,1,2816]{2,1,0:T(1,128)} %reshape.24.kept_ref.refs_1_, f32[136,1024]{1,0:T(8,128)} %add_add_fusion.tot_ref.refs_0_.refs_1_.refs_8_.refs_2_, f32[16,1024]{1,0:T(8,128)} %get-tuple-element.71.refs_3_, ...), custom_call_target="tpu_custom_call" | custom-call | flops 17716740096 | bytes 50331648 | tf_op jit(solution)/shard_map/bwd_last/pallas_call | solution.py:518
  389.8 1.4 subtract_multiply_fusion.2
  (147 shorter events, 32.6 us)
Async XLA Ops:
  0.7 19.6 %collective-permute-start = (f32[2816,512]{1,0:T(8,128)}, f32[2816,512]{1,0:T(8,128)}, u32[]{:S(2)}, u32[]{:S(2)}) collective-permute-start(f32[2816,512]{1,0:T(8,128)} %refs_13_.1), channel_id=1, source_target_pairs={{0,1},{1,0},{2,3},{3,2},{4,5},{5,4},{6,7},{7,6},{8,9},{9,8},{10,11... | collective-permute-start | bytes 17301512 | tf_op jit(solution)/shard_map/ppermute | solution.py:659
  3.2 65.8 %collective-permute-start.7 = (f32[2816,256]{1,0:T(8,128)S(1)}, f32[2816,256]{1,0:T(8,128)}, u32[]{:S(2)}, u32[]{:S(2)}) collective-permute-start(f32[2816,256]{1,0:T(8,128)S(1)} %slice.42), channel_id=1, source_target_pairs={{0,2},{1,3},{2,0},{3,1},{4,6},{5,7},{6,4},{7,5},{8,10},{9,11},{10,... | collective-permute-start | bytes 8650760 | tf_op jit(solution)/shard_map/ppermute | solution.py:659
  46.5 15.0 %collective-permute-start.1 = (f32[136,1024]{1,0:T(8,128)}, f32[136,1024]{1,0:T(8,128)S(1)}, u32[]{:S(2)}, u32[]{:S(2)}) collective-permute-start(f32[136,1024]{1,0:T(8,128)} %get-tuple-element.50), channel_id=1, source_target_pairs={{0,8},{8,16},{16,24},{24,28},{28,20},{20,12},{12,4},{4,0},{1,9},{9... | collective-permute-start | bytes 1671176 | tf_op jit(solution)/shard_map/ppermute | solution.py:555
  69.0 39.2 %collective-permute-start.8 = (f32[2816,256]{1,0:T(8,128)}, f32[2816,256]{1,0:T(8,128)}, u32[]{:S(2)}, u32[]{:S(2)}) collective-permute-start(f32[2816,256]{1,0:T(8,128)} %collective-permute-done.7.refs_0_.refs_10_), channel_id=1, source_target_pairs={{0,1},{1,0},{2,3},{3,2},{4,5},{5,4},{6,7},{7,6},{8,9},{9,8},{10,11... | collective-permute-start | bytes 8650760 | tf_op jit(solution)/shard_map/ppermute | solution.py:659
  69.0 15.3 %collective-permute-start.4 = (f32[136,1024]{1,0:T(8,128)}, f32[136,1024]{1,0:T(8,128)S(1)}, u32[]{:S(2)}, u32[]{:S(2)}) collective-permute-start(f32[136,1024]{1,0:T(8,128)} %get-tuple-element.53), channel_id=1, source_target_pairs={{8,0},{16,8},{24,16},{28,24},{20,28},{12,20},{4,12},{0,4},{9,1},{1... | collective-permute-start | bytes 1671176 | tf_op jit(solution)/shard_map/ppermute | solution.py:555
  74.4 113.4 %collective-permute-start.20 = (f32[2816,256]{1,0:T(8,128)}, f32[2816,256]{1,0:T(8,128)}, u32[]{:S(2)}, u32[]{:S(2)}) collective-permute-start(f32[2816,256]{1,0:T(8,128)} %slice.43), channel_id=1, source_target_pairs={{0,2},{1,3},{2,0},{3,1},{4,6},{5,7},{6,4},{7,5},{8,10},{9,11},{10,... | collective-permute-start | bytes 8650760 | tf_op jit(solution)/shard_map/ppermute | solution.py:659
  75.9 18.2 %collective-permute-start.2 = (f32[136,1024]{1,0:T(8,128)S(1)}, f32[136,1024]{1,0:T(8,128)S(1)}, u32[]{:S(2)}, u32[]{:S(2)}) collective-permute-start(f32[136,1024]{1,0:T(8,128)S(1)} %add.172), channel_id=1, source_target_pairs={{0,8},{8,16},{16,24},{24,28},{28,20},{20,12},{12,4},{4,0},{1,9},{9... | collective-permute-start | bytes 1671176 | tf_op jit(solution)/shard_map/ppermute | solution.py:555
  85.2 17.9 %collective-permute-start.5 = (f32[136,1024]{1,0:T(8,128)}, f32[136,1024]{1,0:T(8,128)}, u32[]{:S(2)}, u32[]{:S(2)}) collective-permute-start(f32[136,1024]{1,0:T(8,128)} %add.174), channel_id=1, source_target_pairs={{8,0},{16,8},{24,16},{28,24},{20,28},{12,20},{4,12},{0,4},{9,1},{1... | collective-permute-start | bytes 1671176 | tf_op jit(solution)/shard_map/ppermute | solution.py:555
  89.3 85.0 %all-to-all-start = ((f32[8,72,512]{2,1,0:T(8,128)}), f32[8,72,512]{2,1,0:T(8,128)S(1)}, u32[]{:S(2)}, u32[]{:S(2)}) async-start(f32[8,72,512]{2,1,0:T(8,128)} %deal.1), calls=%async_computation | async-start | bytes 2359296 | tf_op jit(solution)/shard_map/all_to_all | solution.py:231
  94.2 32.3 %collective-permute-start.3 = (f32[136,1024]{1,0:T(8,128)S(1)}, f32[136,1024]{1,0:T(8,128)S(1)}, u32[]{:S(2)}, u32[]{:S(2)}) collective-permute-start(f32[136,1024]{1,0:T(8,128)S(1)} %add.173), channel_id=1, source_target_pairs={{0,8},{8,16},{16,24},{24,28},{28,20},{20,12},{12,4},{4,0},{1,9},{9... | collective-permute-start | bytes 1671176 | tf_op jit(solution)/shard_map/ppermute | solution.py:555
  105.0 26.8 %copy-start.2 = (f32[136,1024]{1,0:T(8,128)S(1)}, f32[136,1024]{1,0:T(8,128)}, u32[]{:S(2)}) copy-start(f32[136,1024]{1,0:T(8,128)} %get-tuple-element.60) | copy-start | bytes 1671172
  105.0 26.8 %collective-permute-start.6 = (f32[136,1024]{1,0:T(8,128)}, f32[136,1024]{1,0:T(8,128)S(1)}, u32[]{:S(2)}, u32[]{:S(2)}) collective-permute-start(f32[136,1024]{1,0:T(8,128)} %add.175), channel_id=1, source_target_pairs={{8,0},{16,8},{24,16},{28,24},{20,28},{12,20},{4,12},{0,4},{9,1},{1... | collective-permute-start | bytes 1671176 | tf_op jit(solution)/shard_map/ppermute | solution.py:555
  123.5 35.5 %copy-start.9 = (f32[64,1024]{1,0:T(8,128)S(1)}, f32[64,1024]{1,0:T(8,128)}, u32[]{:S(2)}) copy-start(f32[64,1024]{1,0:T(8,128)} %get-tuple-element.66) | copy-start | bytes 786436
  123.5 41.0 %copy-start.8 = (f32[64,1024]{1,0:T(8,128)S(1)}, f32[64,1024]{1,0:T(8,128)}, u32[]{:S(2)}) copy-start(f32[64,1024]{1,0:T(8,128)} %get-tuple-element.70) | copy-start | bytes 786436
  123.5 43.5 %copy-start.7 = (f32[64,1024]{1,0:T(8,128)S(1)}, f32[64,1024]{1,0:T(8,128)}, u32[]{:S(2)}) copy-start(f32[64,1024]{1,0:T(8,128)} %get-tuple-element.67) | copy-start | bytes 786436
  123.5 43.6 %copy-start.1 = (f32[136,1024]{1,0:T(8,128)S(1)}, f32[136,1024]{1,0:T(8,128)}, u32[]{:S(2)}) copy-start(f32[136,1024]{1,0:T(8,128)} %get-tuple-element.62) | copy-start | bytes 1671172
  123.5 16.6 %collective-permute-start.10 = (f32[64,1024]{1,0:T(8,128)}, f32[64,1024]{1,0:T(8,128)S(1)}, u32[]{:S(2)}, u32[]{:S(2)}) collective-permute-start(f32[64,1024]{1,0:T(8,128)} %get-tuple-element.64), channel_id=1, source_target_pairs={{8,0},{16,8},{24,16},{28,24},{20,28},{12,20},{4,12},{0,4},{9,1},{1... | collective-permute-start | bytes 786440 | tf_op jit(solution)/shard_map/ppermute | solution.py:555
  131.9 35.2 %collective-permute-start.9 = (f32[136,1024]{1,0:T(8,128)S(1)}, f32[136,1024]{1,0:T(8,128)S(1)}, u32[]{:S(2)}, u32[]{:S(2)}) collective-permute-start(f32[136,1024]{1,0:T(8,128)S(1)} %add.176), channel_id=1, source_target_pairs={{0,8},{8,16},{16,24},{24,28},{28,20},{20,12},{12,4},{4,0},{1,9},{9... | collective-permute-start | bytes 1671176 | tf_op jit(solution)/shard_map/ppermute | solution.py:555
  140.1 15.6 %collective-permute-start.14 = (f32[64,1024]{1,0:T(8,128)}, f32[64,1024]{1,0:T(8,128)S(1)}, u32[]{:S(2)}, u32[]{:S(2)}) collective-permute-start(f32[64,1024]{1,0:T(8,128)} %get-tuple-element.68), channel_id=1, source_target_pairs={{0,8},{8,16},{16,24},{24,28},{28,20},{20,12},{12,4},{4,0},{1,9},{9... | collective-permute-start | bytes 786440 | tf_op jit(solution)/shard_map/ppermute | solution.py:555
  141.1 32.4 %copy-start.11 = (f32[64,1024]{1,0:T(8,128)S(1)}, f32[64,1024]{1,0:T(8,128)}, u32[]{:S(2)}) copy-start(f32[64,1024]{1,0:T(8,128)} %get-tuple-element.58) | copy-start | bytes 786436
  141.1 17.9 %collective-permute-start.11 = (f32[64,1024]{1,0:T(8,128)S(1)}, f32[64,1024]{1,0:T(8,128)S(1)}, u32[]{:S(2)}, u32[]{:S(2)}) collective-permute-start(f32[64,1024]{1,0:T(8,128)S(1)} %add.182), channel_id=1, source_target_pairs={{8,0},{16,8},{24,16},{28,24},{20,28},{12,20},{4,12},{0,4},{9,1},{1... | collective-permute-start | bytes 786440 | tf_op jit(solution)/shard_map/ppermute | solution.py:555
  156.6 7.8 %collective-permute-start.15 = (f32[64,1024]{1,0:T(8,128)S(1)}, f32[64,1024]{1,0:T(8,128)S(1)}, u32[]{:S(2)}, u32[]{:S(2)}) collective-permute-start(f32[64,1024]{1,0:T(8,128)S(1)} %add.185), channel_id=1, source_target_pairs={{0,8},{8,16},{16,24},{24,28},{28,20},{20,12},{12,4},{4,0},{1,9},{9... | collective-permute-start | bytes 786440 | tf_op jit(solution)/shard_map/ppermute | solution.py:555
  159.1 7.9 %collective-permute-start.12 = (f32[64,1024]{1,0:T(8,128)S(1)}, f32[64,1024]{1,0:T(8,128)S(1)}, u32[]{:S(2)}, u32[]{:S(2)}) collective-permute-start(f32[64,1024]{1,0:T(8,128)S(1)} %add.183), channel_id=1, source_target_pairs={{8,0},{16,8},{24,16},{28,24},{20,28},{12,20},{4,12},{0,4},{9,1},{1... | collective-permute-start | bytes 786440 | tf_op jit(solution)/shard_map/ppermute | solution.py:555
  164.5 6.4 %collective-permute-start.16 = (f32[64,1024]{1,0:T(8,128)S(1)}, f32[64,1024]{1,0:T(8,128)S(1)}, u32[]{:S(2)}, u32[]{:S(2)}) collective-permute-start(f32[64,1024]{1,0:T(8,128)S(1)} %add.186), channel_id=1, source_target_pairs={{0,8},{8,16},{16,24},{24,28},{28,20},{20,12},{12,4},{4,0},{1,9},{9... | collective-permute-start | bytes 786440 | tf_op jit(solution)/shard_map/ppermute | solution.py:555
  167.1 6.4 %collective-permute-start.13 = (f32[64,1024]{1,0:T(8,128)S(1)}, f32[64,1024]{1,0:T(8,128)S(1)}, u32[]{:S(2)}, u32[]{:S(2)}) collective-permute-start(f32[64,1024]{1,0:T(8,128)S(1)} %add.184), channel_id=1, source_target_pairs={{8,0},{16,8},{24,16},{28,24},{20,28},{12,20},{4,12},{0,4},{9,1},{1... | collective-permute-start | bytes 786440 | tf_op jit(solution)/shard_map/ppermute | solution.py:555
  178.2 1.9 collective-permute-start.17
  178.2 4.1 %collective-permute-start.18 = (f32[64,128]{1,0:T(8,128)}, f32[64,128]{1,0:T(8,128)S(1)}, u32[]{:S(2)}, u32[]{:S(2)}) collective-permute-start(f32[64,128]{1,0:T(8,128)} %stats.2.refs_4_), channel_id=1, source_target_pairs={{0,2},{1,3},{2,0},{3,1},{4,6},{5,7},{6,4},{7,5},{8,10},{9,11},{10,... | collective-permute-start | bytes 98312 | tf_op jit(solution)/shard_map/ppermute | solution.py:659
  179.6 3.6 collective-permute-start.19
  187.8 14.9 %collective-permute-start.21 = (f32[2816,256]{1,0:T(8,128)}, f32[2816,256]{1,0:T(8,128)S(1)}, u32[]{:S(2)}, u32[]{:S(2)}) collective-permute-start(f32[2816,256]{1,0:T(8,128)} %collective-permute-done.20.refs_0_.refs_15_), channel_id=1, source_target_pairs={{0,1},{1,0},{2,3},{3,2},{4,5},{5,4},{6,7},{7,6},{8,9},{9,8},{10,11... | collective-permute-start | bytes 8650760 | tf_op jit(solution)/shard_map/ppermute | solution.py:659
  188.1 14.3 %collective-permute-start.32 = (f32[128,1024]{1,0:T(8,128)}, f32[128,1024]{1,0:T(8,128)S(1)}, u32[]{:S(2)}, u32[]{:S(2)}) collective-permute-start(f32[128,1024]{1,0:T(8,128)} %get-tuple-element.72.refs_0_), channel_id=1, source_target_pairs={{8,0},{16,8},{24,16},{28,24},{20,28},{12,20},{4,12},{0,4},{9,1},{1... | collective-permute-start | bytes 1572872 | tf_op jit(solution)/shard_map/ppermute | solution.py:555
  188.1 42.0 %collective-permute-start.33 = (f32[128,1024]{1,0:T(8,128)}, f32[128,1024]{1,0:T(8,128)}, u32[]{:S(2)}, u32[]{:S(2)}) collective-permute-start(f32[128,1024]{1,0:T(8,128)} %get-tuple-element.72.refs_0_), channel_id=1, source_target_pairs={{0,8},{8,16},{16,24},{24,28},{28,20},{20,12},{12,4},{4,0},{1,9},{9... | collective-permute-start | bytes 1572872 | tf_op jit(solution)/shard_map/ppermute | solution.py:555
  202.4 28.0 %collective-permute-start.34 = (f32[128,1024]{1,0:T(8,128)S(1)}, f32[128,1024]{1,0:T(8,128)}, u32[]{:S(2)}, u32[]{:S(2)}) collective-permute-start(f32[128,1024]{1,0:T(8,128)S(1)} %collective-permute-done.32.refs_1_), channel_id=1, source_target_pairs={{8,0},{16,8},{24,16},{28,24},{20,28},{12,20},{4,12},{0,4},{9,1},{1... | collective-permute-start | bytes 1572872 | tf_op jit(solution)/shard_map/ppermute | solution.py:555
  219.6 32.8 %copy-start.6 = (f32[64,1024]{1,0:T(8,128)S(1)}, f32[64,1024]{1,0:T(8,128)}, u32[]{:S(2)}) copy-start(f32[64,1024]{1,0:T(8,128)} %get-tuple-element.79) | copy-start | bytes 786436
  219.6 42.0 %copy-start.10 = (f32[64,1024]{1,0:T(8,128)S(1)}, f32[64,1024]{1,0:T(8,128)}, u32[]{:S(2)}) copy-start(f32[64,1024]{1,0:T(8,128)} %get-tuple-element.83) | copy-start | bytes 786436
  219.6 8.0 %collective-permute-start.22 = (f32[64,1024]{1,0:T(8,128)}, f32[64,1024]{1,0:T(8,128)S(1)}, u32[]{:S(2)}, u32[]{:S(2)}) collective-permute-start(f32[64,1024]{1,0:T(8,128)} %get-tuple-element.76), channel_id=1, source_target_pairs={{0,8},{8,16},{16,24},{24,28},{28,20},{20,12},{12,4},{4,0},{1,9},{9... | collective-permute-start | bytes 786440 | tf_op jit(solution)/shard_map/ppermute | solution.py:555
  221.4 10.7 %collective-permute-start.26 = (f32[64,1024]{1,0:T(8,128)}, f32[64,1024]{1,0:T(8,128)S(1)}, u32[]{:S(2)}, u32[]{:S(2)}) collective-permute-start(f32[64,1024]{1,0:T(8,128)} %get-tuple-element.80), channel_id=1, source_target_pairs={{8,0},{16,8},{24,16},{28,24},{20,28},{12,20},{4,12},{0,4},{9,1},{1... | collective-permute-start | bytes 786440 | tf_op jit(solution)/shard_map/ppermute | solution.py:555
  228.6 9.2 %collective-permute-start.23 = (f32[64,1024]{1,0:T(8,128)S(1)}, f32[64,1024]{1,0:T(8,128)S(1)}, u32[]{:S(2)}, u32[]{:S(2)}) collective-permute-start(f32[64,1024]{1,0:T(8,128)S(1)} %add.189), channel_id=1, source_target_pairs={{0,8},{8,16},{16,24},{24,28},{28,20},{20,12},{12,4},{4,0},{1,9},{9... | collective-permute-start | bytes 786440 | tf_op jit(solution)/shard_map/ppermute | solution.py:555
  230.1 23.5 %collective-permute-start.35 = (f32[128,1024]{1,0:T(8,128)}, f32[128,1024]{1,0:T(8,128)S(1)}, u32[]{:S(2)}, u32[]{:S(2)}) collective-permute-start(f32[128,1024]{1,0:T(8,128)} %collective-permute-done.33.refs_2_), channel_id=1, source_target_pairs={{0,8},{8,16},{16,24},{24,28},{28,20},{20,12},{12,4},{4,0},{1,9},{9... | collective-permute-start | bytes 1572872 | tf_op jit(solution)/shard_map/ppermute | solution.py:555
  230.4 23.6 %collective-permute-start.36 = (f32[128,1024]{1,0:T(8,128)}, f32[128,1024]{1,0:T(8,128)S(1)}, u32[]{:S(2)}, u32[]{:S(2)}) collective-permute-start(f32[128,1024]{1,0:T(8,128)} %collective-permute-done.34.refs_3_), channel_id=1, source_target_pairs={{8,0},{16,8},{24,16},{28,24},{20,28},{12,20},{4,12},{0,4},{9,1},{1... | collective-permute-start | bytes 1572872 | tf_op jit(solution)/shard_map/ppermute | solution.py:555
  233.1 15.2 %collective-permute-start.27 = (f32[64,1024]{1,0:T(8,128)S(1)}, f32[64,1024]{1,0:T(8,128)S(1)}, u32[]{:S(2)}, u32[]{:S(2)}) collective-permute-start(f32[64,1024]{1,0:T(8,128)S(1)} %add.192), channel_id=1, source_target_pairs={{8,0},{16,8},{24,16},{28,24},{20,28},{12,20},{4,12},{0,4},{9,1},{1... | collective-permute-start | bytes 786440 | tf_op jit(solution)/shard_map/ppermute | solution.py:555
  238.8 13.6 %collective-permute-start.24 = (f32[64,1024]{1,0:T(8,128)S(1)}, f32[64,1024]{1,0:T(8,128)S(1)}, u32[]{:S(2)}, u32[]{:S(2)}) collective-permute-start(f32[64,1024]{1,0:T(8,128)S(1)} %add.190), channel_id=1, source_target_pairs={{0,8},{8,16},{16,24},{24,28},{28,20},{20,12},{12,4},{4,0},{1,9},{9... | collective-permute-start | bytes 786440 | tf_op jit(solution)/shard_map/ppermute | solution.py:555
  249.3 7.6 %collective-permute-start.28 = (f32[64,1024]{1,0:T(8,128)S(1)}, f32[64,1024]{1,0:T(8,128)S(1)}, u32[]{:S(2)}, u32[]{:S(2)}) collective-permute-start(f32[64,1024]{1,0:T(8,128)S(1)} %add.193), channel_id=1, source_target_pairs={{8,0},{16,8},{24,16},{28,24},{20,28},{12,20},{4,12},{0,4},{9,1},{1... | collective-permute-start | bytes 786440 | tf_op jit(solution)/shard_map/ppermute | solution.py:555
  252.4 9.2 %collective-permute-start.25 = (f32[64,1024]{1,0:T(8,128)S(1)}, f32[64,1024]{1,0:T(8,128)S(1)}, u32[]{:S(2)}, u32[]{:S(2)}) collective-permute-start(f32[64,1024]{1,0:T(8,128)S(1)} %add.191), channel_id=1, source_target_pairs={{0,8},{8,16},{16,24},{24,28},{28,20},{20,12},{12,4},{4,0},{1,9},{9... | collective-permute-start | bytes 786440 | tf_op jit(solution)/shard_map/ppermute | solution.py:555
  253.7 20.6 %copy-start.27 = (f32[128,1024]{1,0:T(8,128)}, f32[128,1024]{1,0:T(8,128)S(1)}, u32[]{:S(2)}) copy-start(f32[128,1024]{1,0:T(8,128)S(1)} %collective-permute-done.35.refs_4_) | copy-start | bytes 1572868
  253.7 22.7 %collective-permute-start.37 = (f32[128,1024]{1,0:T(8,128)S(1)}, f32[128,1024]{1,0:T(8,128)S(1)}, u32[]{:S(2)}, u32[]{:S(2)}) collective-permute-start(f32[128,1024]{1,0:T(8,128)S(1)} %collective-permute-done.35.refs_4_), channel_id=1, source_target_pairs={{0,8},{8,16},{16,24},{24,28},{28,20},{20,12},{12,4},{4,0},{1,9},{9... | collective-permute-start | bytes 1572872 | tf_op jit(solution)/shard_map/ppermute | solution.py:555
  254.0 20.3 %copy-start.28 = (f32[128,1024]{1,0:T(8,128)}, f32[128,1024]{1,0:T(8,128)S(1)}, u32[]{:S(2)}) copy-start(f32[128,1024]{1,0:T(8,128)S(1)} %collective-permute-done.36.refs_5_) | copy-start | bytes 1572868
  254.0 22.4 %collective-permute-start.38 = (f32[128,1024]{1,0:T(8,128)S(1)}, f32[128,1024]{1,0:T(8,128)S(1)}, u32[]{:S(2)}, u32[]{:S(2)}) collective-permute-start(f32[128,1024]{1,0:T(8,128)S(1)} %collective-permute-done.36.refs_5_), channel_id=1, source_target_pairs={{8,0},{16,8},{24,16},{28,24},{20,28},{12,20},{4,12},{0,4},{9,1},{1... | collective-permute-start | bytes 1572872 | tf_op jit(solution)/shard_map/ppermute | solution.py:555
  265.2 1.9 collective-permute-start.29
  265.2 4.0 %collective-permute-start.30 = (f32[48,128]{1,0:T(8,128)}, f32[48,128]{1,0:T(8,128)S(1)}, u32[]{:S(2)}, u32[]{:S(2)}) collective-permute-start(f32[48,128]{1,0:T(8,128)} %stats.3.refs_4_), channel_id=1, source_target_pairs={{0,2},{1,3},{2,0},{3,1},{4,6},{5,7},{6,4},{7,5},{8,10},{9,11},{10,... | collective-permute-start | bytes 73736 | tf_op jit(solution)/shard_map/ppermute | solution.py:659
  266.2 3.5 collective-permute-start.31
  274.3 27.7 %collective-permute-start.39 = (f32[136,1024]{1,0:T(8,128)}, f32[136,1024]{1,0:T(8,128)S(1)}, u32[]{:S(2)}, u32[]{:S(2)}) collective-permute-start(f32[136,1024]{1,0:T(8,128)} %get-tuple-element.84.refs_5_), channel_id=1, source_target_pairs={{0,8},{8,16},{16,24},{24,28},{28,20},{20,12},{12,4},{4,0},{1,9},{9... | collective-permute-start | bytes 1671176 | tf_op jit(solution)/shard_map/ppermute | solution.py:555
  275.5 26.5 %collective-permute-start.40 = (f32[136,1024]{1,0:T(8,128)}, f32[136,1024]{1,0:T(8,128)S(1)}, u32[]{:S(2)}, u32[]{:S(2)}) collective-permute-start(f32[136,1024]{1,0:T(8,128)} %get-tuple-element.84.refs_5_), channel_id=1, source_target_pairs={{8,0},{16,8},{24,16},{28,24},{20,28},{12,20},{4,12},{0,4},{9,1},{1... | collective-permute-start | bytes 1671176 | tf_op jit(solution)/shard_map/ppermute | solution.py:555
  302.0 40.2 %copy-start.19 = (f32[136,1024]{1,0:T(8,128)}, f32[136,1024]{1,0:T(8,128)S(1)}, u32[]{:S(2)}) copy-start(f32[136,1024]{1,0:T(8,128)S(1)} %collective-permute-done.39.refs_6_) | copy-start | bytes 1671172
  302.0 40.2 %copy-start.20 = (f32[136,1024]{1,0:T(8,128)}, f32[136,1024]{1,0:T(8,128)S(1)}, u32[]{:S(2)}) copy-start(f32[136,1024]{1,0:T(8,128)S(1)} %collective-permute-done.40.refs_7_) | copy-start | bytes 1671172
  302.0 14.2 %collective-permute-start.41 = (f32[136,1024]{1,0:T(8,128)S(1)}, f32[136,1024]{1,0:T(8,128)S(1)}, u32[]{:S(2)}, u32[]{:S(2)}) collective-permute-start(f32[136,1024]{1,0:T(8,128)S(1)} %collective-permute-done.39.refs_6_), channel_id=1, source_target_pairs={{0,8},{8,16},{16,24},{24,28},{28,20},{20,12},{12,4},{4,0},{1,9},{9... | collective-permute-start | bytes 1671176 | tf_op jit(solution)/shard_map/ppermute | solution.py:555
  303.3 14.2 %collective-permute-start.42 = (f32[136,1024]{1,0:T(8,128)S(1)}, f32[136,1024]{1,0:T(8,128)S(1)}, u32[]{:S(2)}, u32[]{:S(2)}) collective-permute-start(f32[136,1024]{1,0:T(8,128)S(1)} %collective-permute-done.40.refs_7_), channel_id=1, source_target_pairs={{8,0},{16,8},{24,16},{28,24},{20,28},{12,20},{4,12},{0,4},{9,1},{1... | collective-permute-start | bytes 1671176 | tf_op jit(solution)/shard_map/ppermute | solution.py:555
  316.3 25.9 %copy-start.21 = (f32[136,1024]{1,0:T(8,128)}, f32[136,1024]{1,0:T(8,128)S(1)}, u32[]{:S(2)}) copy-start(f32[136,1024]{1,0:T(8,128)S(1)} %collective-permute-done.41.refs_8_) | copy-start | bytes 1671172
  316.3 13.3 %collective-permute-start.43 = (f32[136,1024]{1,0:T(8,128)S(1)}, f32[136,1024]{1,0:T(8,128)S(1)}, u32[]{:S(2)}, u32[]{:S(2)}) collective-permute-start(f32[136,1024]{1,0:T(8,128)S(1)} %collective-permute-done.41.refs_8_), channel_id=1, source_target_pairs={{0,8},{8,16},{16,24},{24,28},{28,20},{20,12},{12,4},{4,0},{1,9},{9... | collective-permute-start | bytes 1671176 | tf_op jit(solution)/shard_map/ppermute | solution.py:555
  317.5 24.7 %copy-start.22 = (f32[136,1024]{1,0:T(8,128)}, f32[136,1024]{1,0:T(8,128)S(1)}, u32[]{:S(2)}) copy-start(f32[136,1024]{1,0:T(8,128)S(1)} %collective-permute-done.42.refs_9_) | copy-start | bytes 1671172
  317.5 16.5 %collective-permute-start.44 = (f32[136,1024]{1,0:T(8,128)S(1)}, f32[136,1024]{1,0:T(8,128)S(1)}, u32[]{:S(2)}, u32[]{:S(2)}) collective-permute-start(f32[136,1024]{1,0:T(8,128)S(1)} %collective-permute-done.42.refs_9_), channel_id=1, source_target_pairs={{8,0},{16,8},{24,16},{28,24},{20,28},{12,20},{4,12},{0,4},{9,1},{1... | collective-permute-start | bytes 1671176 | tf_op jit(solution)/shard_map/ppermute | solution.py:555
  329.6 12.6 %collective-permute-start.45 = (f32[136,1024]{1,0:T(8,128)S(1)}, f32[136,1024]{1,0:T(8,128)}, u32[]{:S(2)}, u32[]{:S(2)}) collective-permute-start(f32[136,1024]{1,0:T(8,128)S(1)} %collective-permute-done.43.refs_10_), channel_id=1, source_target_pairs={{0,8},{8,16},{16,24},{24,28},{28,20},{20,12},{12,4},{4,0},{1,9},{9... | collective-permute-start | bytes 1671176 | tf_op jit(solution)/shard_map/ppermute | solution.py:555
  384.5 5.2 %collective-permute-start.48 = (f32[2,2816]{1,0:T(2,128)S(1)}, f32[2,2816]{1,0:T(2,128)S(1)}, u32[]{:S(2)}, u32[]{:S(2)}) collective-permute-start(f32[2,2816]{1,0:T(2,128)S(1)} %bitcast.18), channel_id=1, source_target_pairs={{0,3},{1,2},{2,1},{3,0},{4,7},{5,6},{6,5},{7,4},{8,11},{9,10},{10,... | collective-permute-start | bytes 67592 | tf_op jit(solution)/shard_map/ppermute | solution.py:659
  384.6 5.2 %collective-permute-start.47 = (f32[2,2816]{1,0:T(2,128)S(1)}, f32[2,2816]{1,0:T(2,128)S(1)}, u32[]{:S(2)}, u32[]{:S(2)}) collective-permute-start(f32[2,2816]{1,0:T(2,128)S(1)} %bitcast.19), channel_id=1, source_target_pairs={{0,2},{1,3},{2,0},{3,1},{4,6},{5,7},{6,4},{7,5},{8,10},{9,11},{10,... | collective-permute-start | bytes 67592 | tf_op jit(solution)/shard_map/ppermute | solution.py:659
  385.7 4.1 %collective-permute-start.46 = (f32[2,2816]{1,0:T(2,128)S(1)}, f32[2,2816]{1,0:T(2,128)S(1)}, u32[]{:S(2)}, u32[]{:S(2)}) collective-permute-start(f32[2,2816]{1,0:T(2,128)S(1)} %bitcast.20), channel_id=1, source_target_pairs={{0,1},{1,0},{2,3},{3,2},{4,5},{5,4},{6,7},{7,6},{8,9},{9,8},{10,11... | collective-permute-start | bytes 67592 | tf_op jit(solution)/shard_map/ppermute | solution.py:659
  (19 other events, 119.8 us)

commit v2 on v1

--- a/solution.py
+++ b/solution.py
@@ -13,9 +13,8 @@
 COUNT_WEIGHT = 0.0625
 ENTROPY_WEIGHT = 1.0
 EPSILON = 1e-06
-HIGHEST = lax.Precision.HIGHEST
+COST = pl.CostEstimate(flops=1, bytes_accessed=1, transcendentals=0)
 SETS = [256, 256]
-EARLY = [False]
 F32 = jnp.float32
 BF16 = jnp.bfloat16
 NN = (((1,), (0,)), ((), ()))
@@ -51,16 +50,17 @@
     return mm(onehot, hi, dims) + mm(onehot, lo, dims)
 
 
-def mm_exact(a, b, dims=NN):
-    return lax.dot_general(a, b, dims, precision=HIGHEST, preferred_element_type=F32)
-
-
 def row_tile(rows):
     return rows // 2 if rows % 256 == 0 else rows
 
 
-def tie(v, *others):
-    return lax.optimization_barrier((v, *others))[0]
+class Clock:
+    def __init__(self, token):
+        self.token = token
+
+    def after(self, *vs):
+        *vs, self.token = lax.optimization_barrier((*vs, self.token))
+        return vs
 
 
 def prep_kernel(x_ref, kept_ref, hi_ref, lo_ref, sum_ref):
@@ -99,11 +99,7 @@
             jax.ShapeDtypeStruct((layers, 8, cols), F32),
         ],
         name="prep",
-        cost_estimate=pl.CostEstimate(
-            flops=10 * layers * rows * cols,
-            bytes_accessed=8 * layers * rows * cols,
-            transcendentals=layers * rows * cols,
-        ),
+        cost_estimate=COST,
     )(x, kept.reshape(layers, 1, rows))
 
 
@@ -185,11 +181,7 @@
             pltpu.SemaphoreType.DMA((2 + len(exprs), steps)),
         ],
         name="fwd",
-        cost_estimate=pl.CostEstimate(
-            flops=6 * wide * rows * genes,
-            bytes_accessed=4 * wide * rows + 4 * rows * genes + 4 * wide * genes,
-            transcendentals=0,
-        ),
+        cost_estimate=COST,
     )(*args)
 
 
@@ -209,25 +201,27 @@
             out_ref[j, cut + 8 * u : cut + 8 * u + slides, 0:own] = mask_ref[:, src].astype(F32)
 
 
-def deal(ring, unit, me, observed, gene_mask):
+def deal(ring, unit, clock, observed, gene_mask):
     layers, rows, cols = observed.shape
     n, own = ring.n, unit // ring.n
     if rows % unit:
         observed = lax.all_gather(observed, "cell", axis=1, tiled=True)
         gene_mask = lax.all_gather(gene_mask, "cell", axis=1, tiled=True)
         units = observed.shape[1] // unit
-        pick = lambda a, at: lax.dynamic_index_in_dim(a, me[0], at, keepdims=False)
+        pick = lambda a, at: lax.dynamic_index_in_dim(a, clock.token[0], at, keepdims=False)
         obs = pick(observed.reshape(layers, units, n, own, cols), 2)
         mask = pick(gene_mask.astype(F32).reshape(-1, units, n, own), 2).transpose(1, 0, 2)
         mask = jnp.pad(mask, ((0, 0), (0, 8 - mask.shape[1]), (0, cols - own)))
         slab = jnp.concatenate([obs.reshape(-1, cols), mask.reshape(-1, cols)])
         return slab[None], units
     units = rows // unit
+    (gene_mask,) = clock.after(gene_mask)
     out = pl.pallas_call(
         functools.partial(deal_kernel, ring.place, unit),
         out_shape=jax.ShapeDtypeStruct((n, layers * units * own + 8 * units, cols), F32),
         name="deal",
     )(observed, gene_mask)
+    (out,) = clock.after(out)
     return lax.all_to_all(out, "cell", 0, 0, tiled=True), units
 
 
@@ -443,7 +437,6 @@
             back[2:3, lane] = inv
             back[3:4, lane] = total[0:1, lane] + aux_ref[1:2, lane] * mass
 
-    ones = jnp.ones((8, cols), F32)
     for l in range(layers):
         lane = slice(l * cols, (l + 1) * cols)
         gw = product(exprs, hi, lo, lane)
@@ -459,11 +452,15 @@
         kept = jnp.transpose(jnp.broadcast_to(kept_ref[l], (128, rows)))
         kept = jnp.tile(kept, (1, cols // 128))
         grad_ref[l] = scale * (mapping * (kept * gw - back[3:4, lane]))
-        filt_ref[l] = mm_exact(ones, mapping * gw, NT)[0:1, :]
+        share = mapping * gw
+        lanes = share[:, 0:128]
+        for c in range(128, cols, 128):
+            lanes = lanes + share[:, c : c + 128]
+        filt_ref[l] = jnp.sum(jnp.transpose(lanes), axis=0, keepdims=True)
 
 
 def backward_first(n, unit, offsets, me, prior, blocks, exprs, begin, rows):
-    tile = rows // 4 if rows % 32 == 0 else rows
+    tile = 256 if rows % 256 == 0 else rows
     wide = blocks[0].shape[1]
     genes = sum(w for _, _, w in exprs)
     skip = begin // tile
@@ -479,11 +476,7 @@
         out_shape=jax.ShapeDtypeStruct((rows, wide), F32),
         scratch_shapes=[pltpu.VMEM((genes, wide), BF16), pltpu.VMEM((genes, wide), BF16)],
         name="bwd_first",
-        cost_estimate=pl.CostEstimate(
-            flops=6 * rows * genes * wide,
-            bytes_accessed=4 * rows * (genes + wide) + 4 * genes * wide,
-            transcendentals=0,
-        ),
+        cost_estimate=COST,
     )(me, *prior, *blocks, *[e for e, _, _ in exprs])
 
 
@@ -533,11 +526,7 @@
             pltpu.VMEM((8, wide), F32),
         ],
         name="bwd_last",
-        cost_estimate=pl.CostEstimate(
-            flops=6 * rows * genes * wide,
-            bytes_accessed=4 * rows * (genes + 3 * wide) + 4 * genes * wide,
-            transcendentals=rows * wide,
-        ),
+        cost_estimate=COST,
     )(*args)
 
 
@@ -556,77 +545,86 @@
 
 
 class Scatter:
-    def __init__(self, ring, v, flip):
-        self.ring, self.v, self.flip = ring, v, flip
+    def __init__(self, ring, clock, v, flip):
+        self.ring, self.clock, self.v, self.flip = ring, clock, v, flip
         self.sign = -1 if flip else 1
         self.step = 0
-        self.flying = False
         self.r, self.l = self.at(ring.far), self.at(-ring.near)
+        self.hop()
 
     def at(self, d):
         return self.v[(self.sign * d) % self.ring.n]
 
     def hop(self):
-        ring = self.ring
-        self.mark = self.r
-        self.r = ring.hop(self.r, int(self.flip))
-        if self.step < ring.near:
-            self.l = ring.hop(self.l, 1 - int(self.flip))
+        self.r = self.ring.hop(self.r, int(self.flip))
+        if self.step < self.ring.near:
+            self.l = self.ring.hop(self.l, 1 - int(self.flip))
         self.step += 1
-        self.flying = True
-
-    def add(self, *after):
+
+    def wait(self):
+        self.r, self.l = self.clock.after(self.r, self.l)
+
+    def advance(self):
         ring, s = self.ring, self.step - 1
-        self.flying = False
-        if after:
-            self.r, self.l = lax.optimization_barrier((self.r, self.l, *after))[:2]
         if s < ring.far - 1:
             self.r = self.r + self.at(ring.far - 1 - s)
         if s < ring.near - 1:
             self.l = self.l + self.at(s + 1 - ring.near)
         if self.step == ring.far:
             self.r = self.r + self.l + self.at(0)
-
-    def advance(self, *after):
-        if self.flying:
-            self.add(*after)
-        if self.step < self.ring.far:
+        if self.step < ring.near:
+            self.r, self.l = self.clock.after(self.r, self.l)
+        else:
+            (self.r,) = self.clock.after(self.r)
+        if self.step < ring.far:
             self.hop()
-
-    def finish(self):
-        while self.flying:
-            self.advance()
-        return self.r
+            return True
+        return False
 
 
 class Gather:
-    def __init__(self, ring, v, flip):
-        self.ring, self.flip = ring, flip
+    def __init__(self, ring, clock, v, flip):
+        self.ring, self.clock, self.flip = ring, clock, flip
         self.sign = -1 if flip else 1
         self.blocks, self.offsets = [v], [0]
         self.r = self.l = v
         self.step = 0
-
-    def advance(self, *after):
+        self.hop()
+
+    def hop(self):
+        self.step += 1
+        self.r = self.ring.hop(self.r, int(self.flip))
+        if self.step <= self.ring.near:
+            self.l = self.ring.hop(self.l, 1 - int(self.flip))
+
+    def wait(self):
+        if self.step <= self.ring.near:
+            self.r, self.l = self.clock.after(self.r, self.l)
+        else:
+            (self.r,) = self.clock.after(self.r)
+
+    def advance(self):
         ring = self.ring
-        if self.step == ring.far:
-            return
-        if after:
-            self.r, self.l = lax.optimization_barrier((self.r, self.l, *after))[:2]
-        self.mark = self.r
-        self.step += 1
-        self.r = ring.hop(self.r, int(self.flip))
         self.blocks.append(self.r)
         self.offsets.append(-self.sign * self.step)
         if self.step <= ring.near:
-            self.l = ring.hop(self.l, 1 - int(self.flip))
             self.blocks.append(self.l)
             self.offsets.append(self.sign * self.step)
-
-    def finish(self):
-        while self.step < self.ring.far:
-            self.advance()
-        return self.blocks
+        if self.step < ring.far:
+            self.hop()
+            return True
+        return False
+
+
+def slot(*chains):
+    for c in chains:
+        c.wait()
+    return any([c.advance() for c in chains])
+
+
+def finish(chain):
+    while slot(chain):
+        pass
 
 
 def on_device(logits, filter_logits, expression, observed, gene_mask, slide_ids, true_counts):
@@ -637,19 +635,19 @@
     xs = spots // 2
     width = expression.shape[1]
     widths = SETS if sum(SETS) == width and all(w % (16 * n) == 0 for w in SETS) else [width]
-    early = EARLY
     starts = [sum(widths[:h]) for h in range(len(widths))]
     owns = [w // n for w in widths]
     unit = math.gcd(*widths)
     sets = len(widths)
     ring = Ring(n)
-    spot = lax.axis_index("spot")
-    blocks_at = [
-        lax.rem(spot // 2 - dx + xs, xs) * 2 + (spot % 2 + dc) % 2
-        for dx in range(xs)
-        for dc in range(2)
+    table = [
+        [place] + [(q // 2 - dx) % xs * 2 + (q + dc) % 2 for dx in range(xs) for dc in range(2)]
+        for place in ring.place
+        for q in range(spots)
     ]
-    me = jnp.stack([jnp.asarray(ring.place, jnp.int32)[lax.axis_index("cell")], *blocks_at])
+    me = lax.dynamic_index_in_dim(
+        jnp.asarray(table, jnp.int32), lax.axis_index(("cell", "spot")), keepdims=False
+    )
 
     def send(v, dx, dc):
         pairs = []
@@ -659,134 +657,167 @@
         return lax.ppermute(v, "spot", pairs)
 
     expr, far = {}, {}
-    held = expression
-    for h in range(sets):
-        piece = held[:, starts[h] : starts[h] + widths[h]]
-        held = tie(expression, piece)
+    clock = Clock(me)
+
+    def begin_x(h):
+        (held,) = clock.after(expression)
+        (piece,) = clock.after(held[:, starts[h] : starts[h] + widths[h]])
         for dx in range(1, xs):
             far[dx, h] = send(piece, dx, 0)
-    partner = send(expression, 0, 1)
+
+    begin_x(0)
+    partner = send(clock.after(expression)[0], 0, 1)
     for h in range(sets):
         col = starts[h] // widths[h]
         expr[0, 0, h] = (expression, col, widths[h])
         expr[0, 1, h] = (partner, col, widths[h])
 
     kept = jax.nn.sigmoid(filter_logits)
-    entropy = jnp.sum(
-        kept * jax.nn.softplus(-filter_logits) + (1.0 - kept) * jax.nn.softplus(filter_logits)
-    ).reshape(1)
-
+    slab, units = deal(ring, unit, clock, observed, gene_mask)
+    (kept,) = clock.after(kept)
     hi, lo, sums = prep(logits, kept)
-
-    def project(chosen, dxs, after=(), sums=None):
+    hi, lo, sums = clock.after(hi, lo, sums)
+    away = range(1, xs)
+
+    def project(chosen, dxs, flip, sums=None):
         parts = [
             (expr[dx, dc, h][0], expr[dx, dc, h][1] * widths[h], widths[h])
             for h in chosen
             for dx in dxs
             for dc in range(2)
         ]
-        return forward(n, unit, me, tie(hi, *after) if after else hi, lo, parts, sums)
-
-    def begin_far(h, after):
+        out = forward(n, unit, clock.token, hi, lo, parts, sums)
+        out = clock.after(*out)
+        return Scatter(ring, clock, out, flip)
+
+    def begin_far(h):
         for dx in range(1, xs):
-            piece = tie(far[dx, h], after)
+            (piece,) = clock.after(far[dx, h])
             expr[dx, 0, h] = (piece, 0, widths[h])
             expr[dx, 1, h] = (send(piece, 0, 1), 0, widths[h])
 
-    away = range(1, xs)
-    out = project(range(sets), [0], sums=sums)
-    near = Scatter(ring, out, False)
-    near.hop()
-    slab, units = deal(ring, unit, me, tie(observed, near.mark), gene_mask)
-    near.advance()
-    begin_far(0, near.mark)
-    near.advance()
-    out = project([0], away, (near.mark,))
-    rings = [Scatter(ring, out, True)]
-    near.advance(out[0])
-    rings[0].hop()
-    near.finish()
-    totals = near.r
-
     ids = slide_ids.reshape(1, spot_cols)
-    extra = jnp.broadcast_to(
-        jnp.pad(true_counts.astype(F32), (0, 8 - SLIDES), constant_values=1.0)[:, None],
-        (8, 2 * xs * owns[0]),
-    )
     shifts = [(dx, dc) for dx in range(xs) for dc in range(2)]
-    gathers = []
-    aux = None
-
-    def begin(h, after):
-        begin_far(h, after)
-        out = project([h], away, (after,))
-        rings.append(Scatter(ring, out, h % 2 == 0))
-        return out[0]
-
-    for h in range(sets):
-        first, last = h == 0, h == sets - 1
-        mine = rings[h]
-        while mine.step < ring.far - 1:
-            mine.advance()
-            for g in gathers:
-                g.advance()
-        if not last and early[h]:
-            out = begin(h + 1, mine.mark)
-            mine.advance(out)
-            rings[h + 1].hop()
-        mine.finish()
-        dealt = Dealt(
+    held = {
+        "extra": jnp.broadcast_to(
+            jnp.pad(true_counts.astype(F32), (0, 8 - SLIDES), constant_values=1.0)[:, None],
+            (8, 2 * xs * owns[0]),
+        )
+    }
+
+    def rows_of(h):
+        at = Dealt(
             units, width // unit, starts[h] // unit, widths[h] // unit, unit // n, layers, 2 * xs
         )
-        at = [
-            (sum(2 * owns[i] for i in range(h)), 2 * owns[h]),
-            (0, 2 * (xs - 1) * owns[h]),
+        return at, [near[h].r, rings[h].r], [(0, 2 * owns[h]), (0, 2 * (xs - 1) * owns[h])]
+
+    def take_stats(h):
+        dealt, qs, at = rows_of(h)
+        st = stats(dealt, clock.token, ids, near[0].r, slab, qs, at, h == 0)
+        (st,) = clock.after(st)
+        return [st] + [send(st, dx, dc) for dx, dc in shifts[1:]]
+
+    def take_grads(h, sts):
+        dealt, qs, at = rows_of(h)
+        gp, more = grads(
+            shifts,
+            dealt,
+            xs,
+            clock.token,
+            entropy,
+            ids,
+            near[0].r,
+            slab,
+            held["extra"],
+            sts,
+            qs,
+            at,
+            h == 0,
+            h == sets - 1,
+        )
+        held["extra"] = more
+        if h == 0:
+            held["aux"] = more
+        (gp,) = clock.after(gp)
+        return Gather(ring, clock, gp, h % 2 == 0)
+
+    if cell_rows % 256 == 0 and cell_rows > 256:
+        cut = cell_rows // 512 * 256
+        shares = [(0, cut), (cut, cell_rows - cut)]
+    else:
+        shares = [(0, cell_rows)]
+    parts = len(shares)
+    prior = [[] for _ in range(parts)]
+
+    def multiply_back(h, j):
+        prior[j] = [
+            backward_first(
+                n,
+                unit,
+                gathers[h].offsets,
+                clock.token,
+                prior[j],
+                gathers[h].blocks,
+                [expr[dx, dc, h] for dx in range(xs) for dc in range(2)],
+                *shares[j],
+            )
         ]
-        qs = [near.r, mine.r]
-        st = stats(dealt, me, ids, totals, slab, qs, at, first)
-        sts = [st] + [send(st, dx, dc) for dx, dc in shifts[1:]]
-        gp, extra = grads(
-            shifts, dealt, xs, me, entropy, ids, totals, slab, extra, sts, qs, at, first, last
-        )
-        if first:
-            aux = extra
-        gathers.append(Gather(ring, gp, h % 2 == 0))
-        gathers[-1].advance()
-        if not last and not early[h]:
-            begin(h + 1, gp)
-            rings[h + 1].hop()
-    tail = gathers[-1]
-    parts = 2 if cell_rows % 512 == 0 else 1
-    prior = [[] for _ in range(parts)]
-    mark = tail.mark
-    for h in range(sets - 1):
-        blocks = gathers[h].finish()
-        exprs = [expr[dx, dc, h] for dx in range(xs) for dc in range(2)]
+        prior[j] = clock.after(prior[j][0])
+
+    rings, gathers = [], []
+    near = [project([0], [0], False, sums)]
+    (slab,) = clock.after(slab)
+    scores, gates = clock.after(filter_logits, kept)
+    entropy = jnp.sum(
+        gates * jax.nn.softplus(-scores) + (1.0 - gates) * jax.nn.softplus(scores)
+    ).reshape(1)
+    for h in range(1, sets):
+        near.append(project([h], [0], h % 2 == 1))
+        begin_x(h)
+    if sets == 2:
+        slot(near[0])
+        begin_far(0)
+        rings.append(project([0], away, True))
+        slot(near[0], near[1])
+        slot(near[0], near[1], rings[0])
+        slot(near[0], near[1], rings[0])
+        begin_far(1)
+        rings.append(project([1], away, False))
+        slot(near[1], rings[0])
+        slot(rings[0], rings[1])
+        sts = take_stats(0)
+        slot(rings[1])
+        gathers.append(take_grads(0, sts))
+        slot(rings[1], gathers[0])
+        slot(rings[1], gathers[0])
+        gathers.append(take_grads(1, take_stats(1)))
+        slot(gathers[0])
+        slot(gathers[0], gathers[1])
         for j in range(parts):
-            share = cell_rows // parts
-            prior[j] = [
-                backward_first(
-                    n,
-                    unit,
-                    gathers[h].offsets,
-                    tie(me, mark),
-                    prior[j],
-                    blocks,
-                    exprs,
-                    j * share,
-                    share,
-                )
-            ]
-            mark = tail.r
-            tail.advance(prior[j][0])
-    blocks, offsets = tail.finish(), tail.offsets
+            multiply_back(0, j)
+            slot(gathers[1])
+        finish(gathers[1])
+    else:
+        for q in near:
+            finish(q)
+        for h in range(sets):
+            begin_far(h)
+            rings.append(project([h], away, True))
+            finish(rings[h])
+            gathers.append(take_grads(h, take_stats(h)))
+            finish(gathers[h])
+        for h in range(sets - 1):
+            for j in range(parts):
+                multiply_back(h, j)
+    totals, aux = near[0].r, held["aux"]
+    blocks, offsets = gathers[-1].blocks, gathers[-1].offsets
     exprs = [expr[dx, dc, sets - 1] for dx in range(xs) for dc in range(2)]
     grad_logits, filt = backward_last(
         n,
         unit,
         offsets,
         float(cells_all * G),
-        me,
+        clock.token,
         logits,
         kept,
         totals,

time: 393 us -> 366 us (0.931)
  waiting for transfers between devices: 138 us -> 111 us
  other arithmetic: 18 us -> 23.3 us
    ppermute x35 -> x42, waiting for transfers between devices: 126 us -> 99.9 us  [hop(): return lax.ppermute(v, 'cell', self.dirs[way])]
    pallas_call x1, Pallas kernels: 41.5 us -> 30.1 us  [backward_last(): pl.pallas_call(functools.partial(bwd_last_kernel, n, unit, offsets, scale...]
    pallas_call x3 -> x4, Pallas kernels: 56.7 us -> 62.2 us  [forward(): pl.pallas_call(functools.partial(fwd_kernel, n, unit, cols, sums is not N...]
    add x18 -> x24, other arithmetic: 12.5 us -> 17.8 us  [the longest x12 7.62 us: advance(): self.r = self.r + self.at(ring.far - 1 - s)]
    pallas_call x1 -> x2, Pallas kernels: 24 us -> 28.4 us  [backward_first(): pl.pallas_call(functools.partial(bwd_first_kernel, n, unit, offsets, len(...]
    ppermute x35 -> x42, starting transfers between devices: 51.3 us -> 46.9 us  [hop(): return lax.ppermute(v, 'cell', self.dirs[way])]
  transfers between devices with their start and end apart: 50 -> 57, of which waited for: 23 -> 24; matrix products, arithmetic and copies ran while one was open for 7% -> 5% of each run, Pallas kernels for 28% -> 31%
where the time goes in v2:
time: 366 us; the launch traced here: 365 us
  Pallas kernels  147 us (40%)
  waiting for transfers between devices  111 us (30%)
  starting transfers between devices  63.2 us (17%)
  other arithmetic  23.3 us (6%)
  local copies, waits for them, and re-layouts  15 us (4%)
  between operations  4.93 us (1%)
    ppermute x42, waiting for transfers between devices, hop(): return lax.ppermute(v, 'cell', self.dirs[way])  99.9 us
    pallas_call x4, Pallas kernels, forward(): pl.pallas_call(functools.partial(fwd_kernel, n, unit, cols, sums is not N...  62.2 us
    ppermute x42, starting transfers between devices, hop(): return lax.ppermute(v, 'cell', self.dirs[way])  46.9 us
    pallas_call x1, Pallas kernels, backward_last(): pl.pallas_call(functools.partial(bwd_last_kernel, n, unit, offsets, scale...  30.1 us
    pallas_call x2, Pallas kernels, backward_first(): pl.pallas_call(functools.partial(bwd_first_kernel, n, unit, offsets, len(...  28.4 us
    pallas_call x1, Pallas kernels, prep(): pl.pallas_call(prep_kernel, grid=(layers, rows // tile), in_specs=[pl.Blo...  11.2 us
    ppermute x14, waiting for transfers between devices, send(): return lax.ppermute(v, 'spot', pairs)  11.2 us
    ppermute x14, starting transfers between devices, send(): return lax.ppermute(v, 'spot', pairs)  10.4 us
  transfers between devices with their start and end apart: 57, of which 24 were waited for; matrix products, arithmetic and copies ran while one was open for 5% of the time, Pallas kernels for 31%

profile of v2, /device:TPU:0, one launch (start us, length us, event | category | flops | bytes accessed | tf_op | source)
XLA Modules:
  0.0 364.9 jit_solution(10389372960153866872)
XLA Ops:
  1.9 3.6 slice.42
  6.0 2.5 collective-permute-start.2
  8.4 2.3 deal.1
  10.7 5.8 %all-to-all-start = ((f32[8,72,512]{2,1,0:T(8,128)}), f32[8,72,512]{2,1,0:T(8,128)S(1)}, u32[]{:S(2)}, u32[]{:S(2)}) async-start(f32[8,72,512]{2,1,0:T(8,128)} %deal.1), calls=%async_computation | async-start | bytes 2359296 | tf_op jit(solution)/shard_map/all_to_all | solution.py:225
  17.3 11.2 %prep.1 = (bf16[1024,2816]{1,0:T(8,128)(2,1)}, bf16[1024,2816]{1,0:T(8,128)(2,1)}, f32[2,8,512]{2,1,0:T(8,128)}) custom-call(f32[2,2816,512]{2,1,0:T(8,128)} %refs_0_.5, f32[2,1,2816]{2,1,0:T(1,128)} %reshape.24.kept_ref.refs_1_), custom_call_target="tpu_custom_call" | custom-call | flops 1 | bytes 1 | tf_op jit(solution)/shard_map/prep/pallas_call | solution.py:88
  28.5 15.7 %fwd.4 = (f32[72,1024]{1,0:T(8,128)}, f32[72,1024]{1,0:T(8,128)}, f32[72,1024]{1,0:T(8,128)}, f32[72,1024]{1,0:T(8,128)}, f32[72,1024]{1,0:T(8,128)}, /*index=5*...) custom-call(s32[5]{0:T(128)} %dynamic-slice_bitcast_fusion.me_ref, ...), custom_call_target="tpu_custom_call" | custom-call | flops 1 | bytes 1 | tf_op jit(solution)/shard_map/fwd/pallas_call | solution.py:171
  44.2 2.1 collective-permute-start.3
  46.3 15.5 %fwd.5 = (f32[64,1024]{1,0:T(8,128)}, f32[64,1024]{1,0:T(8,128)}, f32[64,1024]{1,0:T(8,128)}, f32[64,1024]{1,0:T(8,128)}, f32[64,1024]{1,0:T(8,128)}, /*index=5*...) custom-call(s32[5]{0:T(128)} %dynamic-slice_bitcast_fusion.me_ref, ...), custom_call_target="tpu_custom_call" | custom-call | flops 1 | bytes 1 | tf_op jit(solution)/shard_map/fwd/pallas_call | solution.py:171
  61.9 3.6 slice.43
  67.1 4.8 %collective-permute-done.2.refs_0_.refs_10_ = f32[2816,256]{1,0:T(8,128)} collective-permute-done((f32[2816,256]{1,0:T(8,128)}, f32[2816,256]{1,0:T(8,128)}, u32[]{:S(2)}, u32[]{:S(2)}) %collective-permute-start.2) | collective-permute-done | bytes 2883616 | tf_op jit(solution)/shard_map/ppermute | solution.py:657
  71.9 1.7 collective-permute-start.1
  73.6 1.6 collective-permute-start.10
  75.7 1.5 collective-permute-start.8
  77.4 1.8 collective-permute-start.9
  79.2 15.5 %fwd.6 = (f32[64,1024]{1,0:T(8,128)}, f32[64,1024]{1,0:T(8,128)}, f32[64,1024]{1,0:T(8,128)}, f32[64,1024]{1,0:T(8,128)}, f32[64,1024]{1,0:T(8,128)}, /*index=5*...) custom-call(s32[5]{0:T(128)} %dynamic-slice_bitcast_fusion.me_ref, ...), custom_call_target="tpu_custom_call" | custom-call | flops 1 | bytes 1 | tf_op jit(solution)/shard_map/fwd/pallas_call | solution.py:171
  97.0 1.7 collective-permute-start.14
  101.2 1.6 collective-permute-start.12
  103.3 3.7 %collective-permute-done.14 = f32[72,1024]{1,0:T(8,128)S(1)} collective-permute-done((f32[72,1024]{1,0:T(8,128)S(1)}, f32[72,1024]{1,0:T(8,128)S(1)}, u32[]{:S(2)}, u32[]{:S(2)}) %collective-permute-start.14) | collective-permute-done | bytes 294944 | tf_op jit(solution)/shard_map/ppermute | solution.py:544
  106.9 1.6 collective-permute-start.6
  108.6 1.6 collective-permute-start.7
  110.1 4.0 %collective-permute-done.12 = f32[64,1024]{1,0:T(8,128)S(1)} collective-permute-done((f32[64,1024]{1,0:T(8,128)S(1)}, f32[64,1024]{1,0:T(8,128)S(1)}, u32[]{:S(2)}, u32[]{:S(2)}) %collective-permute-start.12) | collective-permute-done | bytes 262176 | tf_op jit(solution)/shard_map/ppermute | solution.py:544
  114.2 4.5 %collective-permute-done.6 = f32[64,1024]{1,0:T(8,128)S(1)} collective-permute-done((f32[64,1024]{1,0:T(8,128)}, f32[64,1024]{1,0:T(8,128)S(1)}, u32[]{:S(2)}, u32[]{:S(2)}) %collective-permute-start.6) | collective-permute-done | bytes 262176 | tf_op jit(solution)/shard_map/ppermute | solution.py:544
  118.7 1.6 collective-permute-start.20
  122.9 1.6 collective-permute-start.19
  125.0 3.7 %collective-permute-done.20 = f32[72,1024]{1,0:T(8,128)S(1)} collective-permute-done((f32[72,1024]{1,0:T(8,128)S(1)}, f32[72,1024]{1,0:T(8,128)S(1)}, u32[]{:S(2)}, u32[]{:S(2)}) %collective-permute-start.20) | collective-permute-done | bytes 294944 | tf_op jit(solution)/shard_map/ppermute | solution.py:544
  128.7 1.6 collective-permute-start.17
  130.2 1.4 collective-permute-done.18
  131.7 2.6 collective-permute-done.19
  135.1 2.9 collective-permute-done.17
  141.0 1.6 collective-permute-start.24
  143.0 2.9 collective-permute-done.21.refs_1_.refs_17_
  145.9 1.7 copy-done.2
  147.6 15.5 %fwd.7 = (f32[64,1024]{1,0:T(8,128)}, f32[64,1024]{1,0:T(8,128)}, f32[64,1024]{1,0:T(8,128)}, f32[64,1024]{1,0:T(8,128)}, f32[64,1024]{1,0:T(8,128)}, /*index=5*...) custom-call(s32[5]{0:T(128)} %dynamic-slice_bitcast_fusion.me_ref, ...), custom_call_target="tpu_custom_call" | custom-call | flops 1 | bytes 1 | tf_op jit(solution)/shard_map/fwd/pallas_call | solution.py:171
  163.2 1.9 add_add_fusion.3.refs_0_.refs_8_
  166.7 1.5 collective-permute-start.22
  168.7 6.7 %collective-permute-done.27 = f32[64,1024]{1,0:T(8,128)S(1)} collective-permute-done((f32[64,1024]{1,0:T(8,128)S(1)}, f32[64,1024]{1,0:T(8,128)S(1)}, u32[]{:S(2)}, u32[]{:S(2)}) %collective-permute-start.27) | collective-permute-done | bytes 262176 | tf_op jit(solution)/shard_map/ppermute | solution.py:544
  175.4 4.8 %collective-permute-done.23 = f32[64,1024]{1,0:T(8,128)S(1)} collective-permute-done((f32[64,1024]{1,0:T(8,128)}, f32[64,1024]{1,0:T(8,128)S(1)}, u32[]{:S(2)}, u32[]{:S(2)}) %collective-permute-start.23) | collective-permute-done | bytes 262176 | tf_op jit(solution)/shard_map/ppermute | solution.py:544
  180.2 1.8 add_add_fusion.2.refs_1_.refs_9_
  184.0 1.6 collective-permute-start.28
  186.1 2.7 stats.2.refs_4_
  188.8 1.5 collective-permute-start.33
  194.5 3.8 %grads.2 = (f32[128,1024]{1,0:T(8,128)}, f32[16,1024]{1,0:T(8,128)}) custom-call(s32[5]{0:T(128)} %dynamic-slice_bitcast_fusion.me_ref, f32[1]{0:T(128)} %bitcast.2.ent_ref, s32[1,512]{1,0:T(1,128)} %bitcast.13, f32[72,1024]{1,0:T(8,128)} %add_add_fusion.tot_ref.refs_0_.refs_1_.refs_8_.refs_2_, f32[8,72,512]{2,1,0:T(8,128)} %copy-done, ...), custom_call_target="tpu_custom_call" | custom-call | tf_op jit(solution)/shard_map/grads/pallas_call | solution.py:373
  198.8 1.5 collective-permute-start.36
  200.3 1.6 collective-permute-start.30
  202.4 16.0 %collective-permute-done.30 = f32[64,1024]{1,0:T(8,128)S(1)} collective-permute-done((f32[64,1024]{1,0:T(8,128)S(1)}, f32[64,1024]{1,0:T(8,128)S(1)}, u32[]{:S(2)}, u32[]{:S(2)}) %collective-permute-start.30) | collective-permute-done | bytes 262176 | tf_op jit(solution)/shard_map/ppermute | solution.py:544
  218.4 1.6 collective-permute-start.38
  220.6 1.6 collective-permute-start.37
  222.1 16.2 %collective-permute-done.37 = f32[64,1024]{1,0:T(8,128)S(1)} collective-permute-done((f32[64,1024]{1,0:T(8,128)S(1)}, f32[64,1024]{1,0:T(8,128)S(1)}, u32[]{:S(2)}, u32[]{:S(2)}) %collective-permute-start.37) | collective-permute-done | bytes 262176 | tf_op jit(solution)/shard_map/ppermute | solution.py:544
  238.3 1.6 collective-permute-start.45
  241.2 2.7 stats.3.refs_4_
  245.7 2.2 collective-permute-done.41.refs_6_
  248.8 3.8 %grads.3 = (f32[136,1024]{1,0:T(8,128)}, f32[16,1024]{1,0:T(8,128)}) custom-call(s32[5]{0:T(128)} %dynamic-slice_bitcast_fusion.me_ref, f32[1]{0:T(128)} %bitcast.2.ent_ref, s32[1,512]{1,0:T(1,128)} %bitcast.15, f32[72,1024]{1,0:T(8,128)} %add_add_fusion.tot_ref.refs_0_.refs_1_.refs_8_.refs_2_, f32[8,72,512]{2,1,0:T(8,128)} %copy-done, ...), custom_call_target="tpu_custom_call" | custom-call | tf_op jit(solution)/shard_map/grads/pallas_call | solution.py:373
  253.1 1.5 collective-permute-start.44
  254.7 1.6 collective-permute-start.47
  256.3 23.0 %collective-permute-done.47.refs_7_ = f32[128,1024]{1,0:T(8,128)S(1)} collective-permute-done((f32[128,1024]{1,0:T(8,128)S(1)}, f32[128,1024]{1,0:T(8,128)S(1)}, u32[]{:S(2)}, u32[]{:S(2)}) %collective-permute-start.47) | collective-permute-done | bytes 524320 | tf_op jit(solution)/shard_map/ppermute | solution.py:544
  280.1 1.6 collective-permute-start.48
  282.1 13.3 %bwd_first.2.refs_4_ = f32[1280,1024]{1,0:T(8,128)} custom-call(s32[5]{0:T(128)} %dynamic-slice_bitcast_fusion.me_ref, f32[128,1024]{1,0:T(8,128)} %get-tuple-element.412.refs_0_, f32[128,1024]{1,0:T(8,128)} %copy-done.3, f32[128,1024]{1,0:T(8,128)} %copy-done.4, f32[128,1024]{1,0:T(8,128)} %copy-done.5, f32[128,1024]{1,0:T(8,128)} %copy-done.6, ...), custom_call_target="tpu_custom_call" | custom-call | flops 1 | bytes 1 | tf_op jit(solution)/shard_map/bwd_first/pallas_call | solution.py:468
  295.6 1.6 collective-permute-start.50
  297.6 15.1 %bwd_first.3.refs_5_ = f32[1536,1024]{1,0:T(8,128)} custom-call(s32[5]{0:T(128)} %dynamic-slice_bitcast_fusion.me_ref, f32[128,1024]{1,0:T(8,128)} %get-tuple-element.412.refs_0_, f32[128,1024]{1,0:T(8,128)} %copy-done.3, f32[128,1024]{1,0:T(8,128)} %copy-done.4, f32[128,1024]{1,0:T(8,128)} %copy-done.5, f32[128,1024]{1,0:T(8,128)} %copy-done.6, ...), custom_call_target="tpu_custom_call" | custom-call | flops 1 | bytes 1 | tf_op jit(solution)/shard_map/bwd_first/pallas_call | solution.py:468
  312.7 1.6 collective-permute-start.52
  317.5 7.9 %collective-permute-done.52.refs_13_ = f32[136,1024]{1,0:T(8,128)S(1)} collective-permute-done((f32[136,1024]{1,0:T(8,128)S(1)}, f32[136,1024]{1,0:T(8,128)S(1)}, u32[]{:S(2)}, u32[]{:S(2)}) %collective-permute-start.52) | collective-permute-done | bytes 557088 | tf_op jit(solution)/shard_map/ppermute | solution.py:544
  326.3 30.1 %bwd_last.1 = (f32[2,2816,512]{2,1,0:T(8,128)}, f32[2,1,2816]{2,1,0:T(1,128)}) custom-call(s32[5]{0:T(128)} %dynamic-slice_bitcast_fusion.me_ref, f32[2,2816,512]{2,1,0:T(8,128)} %refs_0_.5, f32[2,1,2816]{2,1,0:T(1,128)} %reshape.24.kept_ref.refs_1_, f32[72,1024]{1,0:T(8,128)} %add_add_fusion.tot_ref.refs_0_.refs_1_.refs_8_.refs_2_, ...), custom_call_target="tpu_custom_call" | custom-call | flops 1 | bytes 1 | tf_op jit(solution)/shard_map/bwd_last/pallas_call | solution.py:511
  357.2 1.4 collective-permute-start.54
  362.4 1.4 subtract_multiply_fusion.1
  (177 shorter events, 39.6 us)
Async XLA Ops:
  5.5 23.0 %collective-permute-start = (f32[2816,512]{1,0:T(8,128)}, f32[2816,512]{1,0:T(8,128)}, u32[]{:S(2)}, u32[]{:S(2)}) collective-permute-start(f32[2816,512]{1,0:T(8,128)} %refs_14_.1), channel_id=1, source_target_pairs={{0,1},{1,0},{2,3},{3,2},{4,5},{5,4},{6,7},{7,6},{8,9},{9,8},{10,11... | collective-permute-start | bytes 17301512 | tf_op jit(solution)/shard_map/ppermute | solution.py:657
  6.0 65.9 %collective-permute-start.2 = (f32[2816,256]{1,0:T(8,128)}, f32[2816,256]{1,0:T(8,128)}, u32[]{:S(2)}, u32[]{:S(2)}) collective-permute-start(f32[2816,256]{1,0:T(8,128)} %slice.42), channel_id=1, source_target_pairs={{0,2},{1,3},{2,0},{3,1},{4,6},{5,7},{6,4},{7,5},{8,10},{9,11},{10,... | collective-permute-start | bytes 8650760 | tf_op jit(solution)/shard_map/ppermute | solution.py:657
  10.7 35.6 %all-to-all-start = ((f32[8,72,512]{2,1,0:T(8,128)}), f32[8,72,512]{2,1,0:T(8,128)S(1)}, u32[]{:S(2)}, u32[]{:S(2)}) async-start(f32[8,72,512]{2,1,0:T(8,128)} %deal.1), calls=%async_computation | async-start | bytes 2359296 | tf_op jit(solution)/shard_map/all_to_all | solution.py:225
  44.2 21.3 %collective-permute-start.3 = (f32[72,1024]{1,0:T(8,128)}, f32[72,1024]{1,0:T(8,128)S(1)}, u32[]{:S(2)}, u32[]{:S(2)}) collective-permute-start(f32[72,1024]{1,0:T(8,128)} %get-tuple-element.273), channel_id=1, source_target_pairs={{0,8},{8,16},{16,24},{24,28},{28,20},{20,12},{12,4},{4,0},{1,9},{9... | collective-permute-start | bytes 884744 | tf_op jit(solution)/shard_map/ppermute | solution.py:544
  46.3 19.3 %collective-permute-start.4 = (f32[72,1024]{1,0:T(8,128)}, f32[72,1024]{1,0:T(8,128)S(1)}, u32[]{:S(2)}, u32[]{:S(2)}) collective-permute-start(f32[72,1024]{1,0:T(8,128)} %get-tuple-element.274), channel_id=1, source_target_pairs={{8,0},{16,8},{24,16},{28,24},{20,28},{12,20},{4,12},{0,4},{9,1},{1... | collective-permute-start | bytes 884744 | tf_op jit(solution)/shard_map/ppermute | solution.py:544
  67.1 51.6 %copy-start.13 = (f32[72,1024]{1,0:T(8,128)S(1)}, f32[72,1024]{1,0:T(8,128)}, u32[]{:S(2)}) copy-start(f32[72,1024]{1,0:T(8,128)} %get-tuple-element.326) | copy-start | bytes 884740
  71.9 5.5 %collective-permute-start.5 = (f32[2816,256]{1,0:T(8,128)}, f32[2816,256]{1,0:T(8,128)S(1)}, u32[]{:S(2)}, u32[]{:S(2)}) collective-permute-start(f32[2816,256]{1,0:T(8,128)} %collective-permute-done.2.refs_0_.refs_10_), channel_id=1, source_target_pairs={{0,1},{1,0},{2,3},{3,2},{4,5},{5,4},{6,7},{7,6},{8,9},{9,8},{10,11... | collective-permute-start | bytes 8650760 | tf_op jit(solution)/shard_map/ppermute | solution.py:657
  71.9 68.4 %collective-permute-start.1 = (f32[2816,256]{1,0:T(8,128)}, f32[2816,256]{1,0:T(8,128)}, u32[]{:S(2)}, u32[]{:S(2)}) collective-permute-start(f32[2816,256]{1,0:T(8,128)} %slice.43), channel_id=1, source_target_pairs={{0,2},{1,3},{2,0},{3,1},{4,6},{5,7},{6,4},{7,5},{8,10},{9,11},{10,... | collective-permute-start | bytes 8650760 | tf_op jit(solution)/shard_map/ppermute | solution.py:657
  73.6 21.1 %collective-permute-start.10 = (f32[72,1024]{1,0:T(8,128)}, f32[72,1024]{1,0:T(8,128)}, u32[]{:S(2)}, u32[]{:S(2)}) collective-permute-start(f32[72,1024]{1,0:T(8,128)} %add.145), channel_id=1, source_target_pairs={{0,8},{8,16},{16,24},{24,28},{28,20},{20,12},{12,4},{4,0},{1,9},{9... | collective-permute-start | bytes 884744 | tf_op jit(solution)/shard_map/ppermute | solution.py:544
  75.2 19.5 %collective-permute-start.11 = (f32[72,1024]{1,0:T(8,128)}, f32[72,1024]{1,0:T(8,128)}, u32[]{:S(2)}, u32[]{:S(2)}) collective-permute-start(f32[72,1024]{1,0:T(8,128)} %add.146), channel_id=1, source_target_pairs={{8,0},{16,8},{24,16},{28,24},{20,28},{12,20},{4,12},{0,4},{9,1},{1... | collective-permute-start | bytes 884744 | tf_op jit(solution)/shard_map/ppermute | solution.py:544
  75.7 19.1 %collective-permute-start.8 = (f32[64,1024]{1,0:T(8,128)}, f32[64,1024]{1,0:T(8,128)}, u32[]{:S(2)}, u32[]{:S(2)}) collective-permute-start(f32[64,1024]{1,0:T(8,128)} %get-tuple-element.294), channel_id=1, source_target_pairs={{8,0},{16,8},{24,16},{28,24},{20,28},{12,20},{4,12},{0,4},{9,1},{1... | collective-permute-start | bytes 786440 | tf_op jit(solution)/shard_map/ppermute | solution.py:544
  77.4 17.4 %collective-permute-start.9 = (f32[64,1024]{1,0:T(8,128)}, f32[64,1024]{1,0:T(8,128)}, u32[]{:S(2)}, u32[]{:S(2)}) collective-permute-start(f32[64,1024]{1,0:T(8,128)} %get-tuple-element.295), channel_id=1, source_target_pairs={{0,8},{8,16},{16,24},{24,28},{28,20},{20,12},{12,4},{4,0},{1,9},{9... | collective-permute-start | bytes 786440 | tf_op jit(solution)/shard_map/ppermute | solution.py:544
  94.7 45.5 %copy-start.21 = (f32[64,1024]{1,0:T(8,128)S(1)}, f32[64,1024]{1,0:T(8,128)}, u32[]{:S(2)}) copy-start(f32[64,1024]{1,0:T(8,128)} %get-tuple-element.342) | copy-start | bytes 786436
  97.0 9.9 %collective-permute-start.14 = (f32[72,1024]{1,0:T(8,128)S(1)}, f32[72,1024]{1,0:T(8,128)S(1)}, u32[]{:S(2)}, u32[]{:S(2)}) collective-permute-start(f32[72,1024]{1,0:T(8,128)S(1)} %add.149), channel_id=1, source_target_pairs={{0,8},{8,16},{16,24},{24,28},{28,20},{20,12},{12,4},{4,0},{1,9},{9... | collective-permute-start | bytes 884744 | tf_op jit(solution)/shard_map/ppermute | solution.py:544
  98.7 9.9 %collective-permute-start.15 = (f32[72,1024]{1,0:T(8,128)S(1)}, f32[72,1024]{1,0:T(8,128)S(1)}, u32[]{:S(2)}, u32[]{:S(2)}) collective-permute-start(f32[72,1024]{1,0:T(8,128)S(1)} %add.150), channel_id=1, source_target_pairs={{8,0},{16,8},{24,16},{28,24},{20,28},{12,20},{4,12},{0,4},{9,1},{1... | collective-permute-start | bytes 884744 | tf_op jit(solution)/shard_map/ppermute | solution.py:544
  101.2 13.0 %collective-permute-start.12 = (f32[64,1024]{1,0:T(8,128)S(1)}, f32[64,1024]{1,0:T(8,128)S(1)}, u32[]{:S(2)}, u32[]{:S(2)}) collective-permute-start(f32[64,1024]{1,0:T(8,128)S(1)} %add.147), channel_id=1, source_target_pairs={{8,0},{16,8},{24,16},{28,24},{20,28},{12,20},{4,12},{0,4},{9,1},{1... | collective-permute-start | bytes 786440 | tf_op jit(solution)/shard_map/ppermute | solution.py:544
  102.8 11.4 %collective-permute-start.13 = (f32[64,1024]{1,0:T(8,128)S(1)}, f32[64,1024]{1,0:T(8,128)S(1)}, u32[]{:S(2)}, u32[]{:S(2)}) collective-permute-start(f32[64,1024]{1,0:T(8,128)S(1)} %add.148), channel_id=1, source_target_pairs={{0,8},{8,16},{16,24},{24,28},{28,20},{20,12},{12,4},{4,0},{1,9},{9... | collective-permute-start | bytes 786440 | tf_op jit(solution)/shard_map/ppermute | solution.py:544
  106.9 11.7 %collective-permute-start.6 = (f32[64,1024]{1,0:T(8,128)}, f32[64,1024]{1,0:T(8,128)S(1)}, u32[]{:S(2)}, u32[]{:S(2)}) collective-permute-start(f32[64,1024]{1,0:T(8,128)} %get-tuple-element.292), channel_id=1, source_target_pairs={{8,0},{16,8},{24,16},{28,24},{20,28},{12,20},{4,12},{0,4},{9,1},{1... | collective-permute-start | bytes 786440 | tf_op jit(solution)/shard_map/ppermute | solution.py:544
  108.6 10.1 %collective-permute-start.7 = (f32[64,1024]{1,0:T(8,128)}, f32[64,1024]{1,0:T(8,128)S(1)}, u32[]{:S(2)}, u32[]{:S(2)}) collective-permute-start(f32[64,1024]{1,0:T(8,128)} %get-tuple-element.293), channel_id=1, source_target_pairs={{0,8},{8,16},{16,24},{24,28},{28,20},{20,12},{12,4},{4,0},{1,9},{9... | collective-permute-start | bytes 786440 | tf_op jit(solution)/shard_map/ppermute | solution.py:544
  118.7 9.9 %collective-permute-start.20 = (f32[72,1024]{1,0:T(8,128)S(1)}, f32[72,1024]{1,0:T(8,128)S(1)}, u32[]{:S(2)}, u32[]{:S(2)}) collective-permute-start(f32[72,1024]{1,0:T(8,128)S(1)} %add.155), channel_id=1, source_target_pairs={{0,8},{8,16},{16,24},{24,28},{28,20},{20,12},{12,4},{4,0},{1,9},{9... | collective-permute-start | bytes 884744 | tf_op jit(solution)/shard_map/ppermute | solution.py:544
  122.4 9.2 %collective-permute-start.18 = (f32[64,1024]{1,0:T(8,128)S(1)}, f32[64,1024]{1,0:T(8,128)S(1)}, u32[]{:S(2)}, u32[]{:S(2)}) collective-permute-start(f32[64,1024]{1,0:T(8,128)S(1)} %add.153), channel_id=1, source_target_pairs={{8,0},{16,8},{24,16},{28,24},{20,28},{12,20},{4,12},{0,4},{9,1},{1... | collective-permute-start | bytes 786440 | tf_op jit(solution)/shard_map/ppermute | solution.py:544
  122.9 11.4 %collective-permute-start.19 = (f32[64,1024]{1,0:T(8,128)S(1)}, f32[64,1024]{1,0:T(8,128)S(1)}, u32[]{:S(2)}, u32[]{:S(2)}) collective-permute-start(f32[64,1024]{1,0:T(8,128)S(1)} %add.154), channel_id=1, source_target_pairs={{0,8},{8,16},{16,24},{24,28},{28,20},{20,12},{12,4},{4,0},{1,9},{9... | collective-permute-start | bytes 786440 | tf_op jit(solution)/shard_map/ppermute | solution.py:544
  124.5 10.6 %collective-permute-start.16 = (f32[64,1024]{1,0:T(8,128)S(1)}, f32[64,1024]{1,0:T(8,128)S(1)}, u32[]{:S(2)}, u32[]{:S(2)}) collective-permute-start(f32[64,1024]{1,0:T(8,128)S(1)} %add.151), channel_id=1, source_target_pairs={{8,0},{16,8},{24,16},{28,24},{20,28},{12,20},{4,12},{0,4},{9,1},{1... | collective-permute-start | bytes 786440 | tf_op jit(solution)/shard_map/ppermute | solution.py:544
  128.7 9.4 %collective-permute-start.17 = (f32[64,1024]{1,0:T(8,128)S(1)}, f32[64,1024]{1,0:T(8,128)S(1)}, u32[]{:S(2)}, u32[]{:S(2)}) collective-permute-start(f32[64,1024]{1,0:T(8,128)S(1)} %add.152), channel_id=1, source_target_pairs={{0,8},{8,16},{16,24},{24,28},{28,20},{20,12},{12,4},{4,0},{1,9},{9... | collective-permute-start | bytes 786440 | tf_op jit(solution)/shard_map/ppermute | solution.py:544
  140.3 45.8 %copy-start.36 = (s32[4]{0:T(128)S(1)}, s32[4]{0:T(128)}, u32[]{:S(2)}) copy-start(s32[4]{0:T(128)} %param.14) | copy-start | bytes 52
  140.3 5.6 %collective-permute-start.21 = (f32[2816,256]{1,0:T(8,128)}, f32[2816,256]{1,0:T(8,128)S(1)}, u32[]{:S(2)}, u32[]{:S(2)}) collective-permute-start(f32[2816,256]{1,0:T(8,128)} %collective-permute-done.1.refs_0_.refs_16_), channel_id=1, source_target_pairs={{0,1},{1,0},{2,3},{3,2},{4,5},{5,4},{6,7},{7,6},{8,9},{9,8},{10,11... | collective-permute-start | bytes 8650760 | tf_op jit(solution)/shard_map/ppermute | solution.py:657
  140.4 22.7 %collective-permute-start.26 = (f32[64,1024]{1,0:T(8,128)}, f32[64,1024]{1,0:T(8,128)}, u32[]{:S(2)}, u32[]{:S(2)}) collective-permute-start(f32[64,1024]{1,0:T(8,128)} %add.158), channel_id=1, source_target_pairs={{8,0},{16,8},{24,16},{28,24},{20,28},{12,20},{4,12},{0,4},{9,1},{1... | collective-permute-start | bytes 786440 | tf_op jit(solution)/shard_map/ppermute | solution.py:544
  141.0 22.2 %collective-permute-start.24 = (f32[64,1024]{1,0:T(8,128)}, f32[64,1024]{1,0:T(8,128)}, u32[]{:S(2)}, u32[]{:S(2)}) collective-permute-start(f32[64,1024]{1,0:T(8,128)} %add.156), channel_id=1, source_target_pairs={{8,0},{16,8},{24,16},{28,24},{20,28},{12,20},{4,12},{0,4},{9,1},{1... | collective-permute-start | bytes 786440 | tf_op jit(solution)/shard_map/ppermute | solution.py:544
  142.6 20.6 %collective-permute-start.25 = (f32[64,1024]{1,0:T(8,128)S(1)}, f32[64,1024]{1,0:T(8,128)}, u32[]{:S(2)}, u32[]{:S(2)}) collective-permute-start(f32[64,1024]{1,0:T(8,128)S(1)} %add.157), channel_id=1, source_target_pairs={{0,8},{8,16},{16,24},{24,28},{28,20},{20,12},{12,4},{4,0},{1,9},{9... | collective-permute-start | bytes 786440 | tf_op jit(solution)/shard_map/ppermute | solution.py:544
  163.1 57.4 %copy-start.20 = (f32[64,1024]{1,0:T(8,128)S(1)}, f32[64,1024]{1,0:T(8,128)}, u32[]{:S(2)}) copy-start(f32[64,1024]{1,0:T(8,128)} %get-tuple-element.411) | copy-start | bytes 786436
  165.1 75.3 %copy-start.27 = (f32[64,1024]{1,0:T(8,128)S(1)}, f32[64,1024]{1,0:T(8,128)}, u32[]{:S(2)}) copy-start(f32[64,1024]{1,0:T(8,128)} %get-tuple-element.420) | copy-start | bytes 786436
  166.2 9.2 %collective-permute-start.27 = (f32[64,1024]{1,0:T(8,128)S(1)}, f32[64,1024]{1,0:T(8,128)S(1)}, u32[]{:S(2)}, u32[]{:S(2)}) collective-permute-start(f32[64,1024]{1,0:T(8,128)S(1)} %add.161), channel_id=1, source_target_pairs={{8,0},{16,8},{24,16},{28,24},{20,28},{12,20},{4,12},{0,4},{9,1},{1... | collective-permute-start | bytes 786440 | tf_op jit(solution)/shard_map/ppermute | solution.py:544
  166.7 8.7 %collective-permute-start.22 = (f32[64,1024]{1,0:T(8,128)}, f32[64,1024]{1,0:T(8,128)S(1)}, u32[]{:S(2)}, u32[]{:S(2)}) collective-permute-start(f32[64,1024]{1,0:T(8,128)} %get-tuple-element.362), channel_id=1, source_target_pairs={{0,8},{8,16},{16,24},{24,28},{28,20},{20,12},{12,4},{4,0},{1,9},{9... | collective-permute-start | bytes 786440 | tf_op jit(solution)/shard_map/ppermute | solution.py:544
  168.2 11.9 %collective-permute-start.23 = (f32[64,1024]{1,0:T(8,128)}, f32[64,1024]{1,0:T(8,128)S(1)}, u32[]{:S(2)}, u32[]{:S(2)}) collective-permute-start(f32[64,1024]{1,0:T(8,128)} %get-tuple-element.363), channel_id=1, source_target_pairs={{8,0},{16,8},{24,16},{28,24},{20,28},{12,20},{4,12},{0,4},{9,1},{1... | collective-permute-start | bytes 786440 | tf_op jit(solution)/shard_map/ppermute | solution.py:544
  184.0 7.5 %collective-permute-start.28 = (f32[64,1024]{1,0:T(8,128)S(1)}, f32[64,1024]{1,0:T(8,128)S(1)}, u32[]{:S(2)}, u32[]{:S(2)}) collective-permute-start(f32[64,1024]{1,0:T(8,128)S(1)} %add.164), channel_id=1, source_target_pairs={{0,8},{8,16},{16,24},{24,28},{28,20},{20,12},{12,4},{4,0},{1,9},{9... | collective-permute-start | bytes 786440 | tf_op jit(solution)/shard_map/ppermute | solution.py:544
  185.6 7.2 %collective-permute-start.29 = (f32[64,1024]{1,0:T(8,128)S(1)}, f32[64,1024]{1,0:T(8,128)S(1)}, u32[]{:S(2)}, u32[]{:S(2)}) collective-permute-start(f32[64,1024]{1,0:T(8,128)S(1)} %add.165), channel_id=1, source_target_pairs={{8,0},{16,8},{24,16},{28,24},{20,28},{12,20},{4,12},{0,4},{9,1},{1... | collective-permute-start | bytes 786440 | tf_op jit(solution)/shard_map/ppermute | solution.py:544
  188.8 4.1 %collective-permute-start.32 = (f32[64,128]{1,0:T(8,128)}, f32[64,128]{1,0:T(8,128)S(1)}, u32[]{:S(2)}, u32[]{:S(2)}) collective-permute-start(f32[64,128]{1,0:T(8,128)} %stats.2.refs_4_), channel_id=1, source_target_pairs={{0,1},{1,0},{2,3},{3,2},{4,5},{5,4},{6,7},{7,6},{8,9},{9,8},{10,11... | collective-permute-start | bytes 98312 | tf_op jit(solution)/shard_map/ppermute | solution.py:657
  188.8 4.2 %collective-permute-start.33 = (f32[64,128]{1,0:T(8,128)}, f32[64,128]{1,0:T(8,128)S(1)}, u32[]{:S(2)}, u32[]{:S(2)}) collective-permute-start(f32[64,128]{1,0:T(8,128)} %stats.2.refs_4_), channel_id=1, source_target_pairs={{0,2},{1,3},{2,0},{3,1},{4,6},{5,7},{6,4},{7,5},{8,10},{9,11},{10,... | collective-permute-start | bytes 98312 | tf_op jit(solution)/shard_map/ppermute | solution.py:657
  190.3 3.6 collective-permute-start.34
  198.3 20.1 %collective-permute-start.35 = (f32[128,1024]{1,0:T(8,128)}, f32[128,1024]{1,0:T(8,128)S(1)}, u32[]{:S(2)}, u32[]{:S(2)}) collective-permute-start(f32[128,1024]{1,0:T(8,128)} %get-tuple-element.412.refs_0_), channel_id=1, source_target_pairs={{8,0},{16,8},{24,16},{28,24},{20,28},{12,20},{4,12},{0,4},{9,1},{1... | collective-permute-start | bytes 1572872 | tf_op jit(solution)/shard_map/ppermute | solution.py:544
  198.8 19.6 %collective-permute-start.36 = (f32[128,1024]{1,0:T(8,128)}, f32[128,1024]{1,0:T(8,128)S(1)}, u32[]{:S(2)}, u32[]{:S(2)}) collective-permute-start(f32[128,1024]{1,0:T(8,128)} %get-tuple-element.412.refs_0_), channel_id=1, source_target_pairs={{0,8},{8,16},{16,24},{24,28},{28,20},{20,12},{12,4},{4,0},{1,9},{9... | collective-permute-start | bytes 1572872 | tf_op jit(solution)/shard_map/ppermute | solution.py:544
  200.3 18.1 %collective-permute-start.30 = (f32[64,1024]{1,0:T(8,128)S(1)}, f32[64,1024]{1,0:T(8,128)S(1)}, u32[]{:S(2)}, u32[]{:S(2)}) collective-permute-start(f32[64,1024]{1,0:T(8,128)S(1)} %add.168), channel_id=1, source_target_pairs={{0,8},{8,16},{16,24},{24,28},{28,20},{20,12},{12,4},{4,0},{1,9},{9... | collective-permute-start | bytes 786440 | tf_op jit(solution)/shard_map/ppermute | solution.py:544
  201.9 16.5 %collective-permute-start.31 = (f32[64,1024]{1,0:T(8,128)S(1)}, f32[64,1024]{1,0:T(8,128)S(1)}, u32[]{:S(2)}, u32[]{:S(2)}) collective-permute-start(f32[64,1024]{1,0:T(8,128)S(1)} %add.169), channel_id=1, source_target_pairs={{8,0},{16,8},{24,16},{28,24},{20,28},{12,20},{4,12},{0,4},{9,1},{1... | collective-permute-start | bytes 786440 | tf_op jit(solution)/shard_map/ppermute | solution.py:544
  218.4 63.7 %copy-start.3 = (f32[128,1024]{1,0:T(8,128)}, f32[128,1024]{1,0:T(8,128)S(1)}, u32[]{:S(2)}) copy-start(f32[128,1024]{1,0:T(8,128)S(1)} %collective-permute-done.35.refs_1_) | copy-start | bytes 1572868
  218.4 63.7 %copy-start.4 = (f32[128,1024]{1,0:T(8,128)}, f32[128,1024]{1,0:T(8,128)S(1)}, u32[]{:S(2)}) copy-start(f32[128,1024]{1,0:T(8,128)S(1)} %collective-permute-done.36.refs_2_) | copy-start | bytes 1572868
  218.4 19.9 %collective-permute-start.38 = (f32[128,1024]{1,0:T(8,128)S(1)}, f32[128,1024]{1,0:T(8,128)S(1)}, u32[]{:S(2)}, u32[]{:S(2)}) collective-permute-start(f32[128,1024]{1,0:T(8,128)S(1)} %collective-permute-done.35.refs_1_), channel_id=1, source_target_pairs={{8,0},{16,8},{24,16},{28,24},{20,28},{12,20},{4,12},{0,4},{9,1},{1... | collective-permute-start | bytes 1572872 | tf_op jit(solution)/shard_map/ppermute | solution.py:544
  220.1 18.3 %collective-permute-start.39 = (f32[128,1024]{1,0:T(8,128)S(1)}, f32[128,1024]{1,0:T(8,128)S(1)}, u32[]{:S(2)}, u32[]{:S(2)}) collective-permute-start(f32[128,1024]{1,0:T(8,128)S(1)} %collective-permute-done.36.refs_2_), channel_id=1, source_target_pairs={{0,8},{8,16},{16,24},{24,28},{28,20},{20,12},{12,4},{4,0},{1,9},{9... | collective-permute-start | bytes 1572872 | tf_op jit(solution)/shard_map/ppermute | solution.py:544
  220.6 17.8 %collective-permute-start.37 = (f32[64,1024]{1,0:T(8,128)S(1)}, f32[64,1024]{1,0:T(8,128)S(1)}, u32[]{:S(2)}, u32[]{:S(2)}) collective-permute-start(f32[64,1024]{1,0:T(8,128)S(1)} %add.173), channel_id=1, source_target_pairs={{0,8},{8,16},{16,24},{24,28},{28,20},{20,12},{12,4},{4,0},{1,9},{9... | collective-permute-start | bytes 786440 | tf_op jit(solution)/shard_map/ppermute | solution.py:544
  238.3 16.3 %collective-permute-start.45 = (f32[128,1024]{1,0:T(8,128)S(1)}, f32[128,1024]{1,0:T(8,128)S(1)}, u32[]{:S(2)}, u32[]{:S(2)}) collective-permute-start(f32[128,1024]{1,0:T(8,128)S(1)} %collective-permute-done.38.refs_3_), channel_id=1, source_target_pairs={{8,0},{16,8},{24,16},{28,24},{20,28},{12,20},{4,12},{0,4},{9,1},{1... | collective-permute-start | bytes 1572872 | tf_op jit(solution)/shard_map/ppermute | solution.py:544
  240.0 14.7 %collective-permute-start.46 = (f32[128,1024]{1,0:T(8,128)S(1)}, f32[128,1024]{1,0:T(8,128)S(1)}, u32[]{:S(2)}, u32[]{:S(2)}) collective-permute-start(f32[128,1024]{1,0:T(8,128)S(1)} %collective-permute-done.39.refs_4_), channel_id=1, source_target_pairs={{0,8},{8,16},{16,24},{24,28},{28,20},{20,12},{12,4},{4,0},{1,9},{9... | collective-permute-start | bytes 1572872 | tf_op jit(solution)/shard_map/ppermute | solution.py:544
  243.9 1.9 collective-permute-start.40
  243.9 4.1 %collective-permute-start.41 = (f32[48,128]{1,0:T(8,128)}, f32[48,128]{1,0:T(8,128)S(1)}, u32[]{:S(2)}, u32[]{:S(2)}) collective-permute-start(f32[48,128]{1,0:T(8,128)} %stats.3.refs_4_), channel_id=1, source_target_pairs={{0,2},{1,3},{2,0},{3,1},{4,6},{5,7},{6,4},{7,5},{8,10},{9,11},{10,... | collective-permute-start | bytes 73736 | tf_op jit(solution)/shard_map/ppermute | solution.py:657
  244.7 3.5 collective-permute-start.42
  252.6 27.5 %collective-permute-start.43 = (f32[136,1024]{1,0:T(8,128)}, f32[136,1024]{1,0:T(8,128)}, u32[]{:S(2)}, u32[]{:S(2)}) collective-permute-start(f32[136,1024]{1,0:T(8,128)} %get-tuple-element.432.refs_6_), channel_id=1, source_target_pairs={{0,8},{8,16},{16,24},{24,28},{28,20},{20,12},{12,4},{4,0},{1,9},{9... | collective-permute-start | bytes 1671176 | tf_op jit(solution)/shard_map/ppermute | solution.py:544
  253.1 27.0 %collective-permute-start.44 = (f32[136,1024]{1,0:T(8,128)}, f32[136,1024]{1,0:T(8,128)}, u32[]{:S(2)}, u32[]{:S(2)}) collective-permute-start(f32[136,1024]{1,0:T(8,128)} %get-tuple-element.432.refs_6_), channel_id=1, source_target_pairs={{8,0},{16,8},{24,16},{28,24},{20,28},{12,20},{4,12},{0,4},{9,1},{1... | collective-permute-start | bytes 1671176 | tf_op jit(solution)/shard_map/ppermute | solution.py:544
  254.7 24.6 %collective-permute-start.47 = (f32[128,1024]{1,0:T(8,128)S(1)}, f32[128,1024]{1,0:T(8,128)S(1)}, u32[]{:S(2)}, u32[]{:S(2)}) collective-permute-start(f32[128,1024]{1,0:T(8,128)S(1)} %collective-permute-done.45.refs_5_), channel_id=1, source_target_pairs={{8,0},{16,8},{24,16},{28,24},{20,28},{12,20},{4,12},{0,4},{9,1},{1... | collective-permute-start | bytes 1572872 | tf_op jit(solution)/shard_map/ppermute | solution.py:544
  280.1 15.3 %collective-permute-start.48 = (f32[136,1024]{1,0:T(8,128)}, f32[136,1024]{1,0:T(8,128)}, u32[]{:S(2)}, u32[]{:S(2)}) collective-permute-start(f32[136,1024]{1,0:T(8,128)} %collective-permute-done.43.refs_7_), channel_id=1, source_target_pairs={{0,8},{8,16},{16,24},{24,28},{28,20},{20,12},{12,4},{4,0},{1,9},{9... | collective-permute-start | bytes 1671176 | tf_op jit(solution)/shard_map/ppermute | solution.py:544
  281.7 13.9 %collective-permute-start.49 = (f32[136,1024]{1,0:T(8,128)}, f32[136,1024]{1,0:T(8,128)}, u32[]{:S(2)}, u32[]{:S(2)}) collective-permute-start(f32[136,1024]{1,0:T(8,128)} %collective-permute-done.44.refs_8_), channel_id=1, source_target_pairs={{8,0},{16,8},{24,16},{28,24},{20,28},{12,20},{4,12},{0,4},{9,1},{1... | collective-permute-start | bytes 1671176 | tf_op jit(solution)/shard_map/ppermute | solution.py:544
  295.6 17.1 %collective-permute-start.50 = (f32[136,1024]{1,0:T(8,128)}, f32[136,1024]{1,0:T(8,128)S(1)}, u32[]{:S(2)}, u32[]{:S(2)}) collective-permute-start(f32[136,1024]{1,0:T(8,128)} %collective-permute-done.48.refs_9_), channel_id=1, source_target_pairs={{0,8},{8,16},{16,24},{24,28},{28,20},{20,12},{12,4},{4,0},{1,9},{9... | collective-permute-start | bytes 1671176 | tf_op jit(solution)/shard_map/ppermute | solution.py:544
  297.1 15.6 %collective-permute-start.51 = (f32[136,1024]{1,0:T(8,128)}, f32[136,1024]{1,0:T(8,128)S(1)}, u32[]{:S(2)}, u32[]{:S(2)}) collective-permute-start(f32[136,1024]{1,0:T(8,128)} %collective-permute-done.49.refs_10_), channel_id=1, source_target_pairs={{8,0},{16,8},{24,16},{28,24},{20,28},{12,20},{4,12},{0,4},{9,1},{1... | collective-permute-start | bytes 1671176 | tf_op jit(solution)/shard_map/ppermute | solution.py:544
  312.7 12.7 %collective-permute-start.52 = (f32[136,1024]{1,0:T(8,128)S(1)}, f32[136,1024]{1,0:T(8,128)S(1)}, u32[]{:S(2)}, u32[]{:S(2)}) collective-permute-start(f32[136,1024]{1,0:T(8,128)S(1)} %collective-permute-done.50.refs_11_), channel_id=1, source_target_pairs={{0,8},{8,16},{16,24},{24,28},{28,20},{20,12},{12,4},{4,0},{1,9},{9... | collective-permute-start | bytes 1671176 | tf_op jit(solution)/shard_map/ppermute | solution.py:544
  357.1 5.2 %collective-permute-start.55 = (f32[2,2816]{1,0:T(2,128)S(1)}, f32[2,2816]{1,0:T(2,128)S(1)}, u32[]{:S(2)}, u32[]{:S(2)}) collective-permute-start(f32[2,2816]{1,0:T(2,128)S(1)} %bitcast.16), channel_id=1, source_target_pairs={{0,3},{1,2},{2,1},{3,0},{4,7},{5,6},{6,5},{7,4},{8,11},{9,10},{10,... | collective-permute-start | bytes 67592 | tf_op jit(solution)/shard_map/ppermute | solution.py:657
  357.2 5.2 %collective-permute-start.54 = (f32[2,2816]{1,0:T(2,128)S(1)}, f32[2,2816]{1,0:T(2,128)S(1)}, u32[]{:S(2)}, u32[]{:S(2)}) collective-permute-start(f32[2,2816]{1,0:T(2,128)S(1)} %bitcast.17), channel_id=1, source_target_pairs={{0,2},{1,3},{2,0},{3,1},{4,6},{5,7},{6,4},{7,5},{8,10},{9,11},{10,... | collective-permute-start | bytes 67592 | tf_op jit(solution)/shard_map/ppermute | solution.py:657
  358.6 3.8 %collective-permute-start.53 = (f32[2,2816]{1,0:T(2,128)S(1)}, f32[2,2816]{1,0:T(2,128)S(1)}, u32[]{:S(2)}, u32[]{:S(2)}) collective-permute-start(f32[2,2816]{1,0:T(2,128)S(1)} %bitcast.18), channel_id=1, source_target_pairs={{0,1},{1,0},{2,3},{3,2},{4,5},{5,4},{6,7},{7,6},{8,9},{9,8},{10,11... | collective-permute-start | bytes 67592 | tf_op jit(solution)/shard_map/ppermute | solution.py:657
  (30 other events, 521.8 us)

commit v3 on v2

--- a/solution.py
+++ b/solution.py
@@ -741,11 +741,11 @@
         (gp,) = clock.after(gp)
         return Gather(ring, clock, gp, h % 2 == 0)
 
-    if cell_rows % 256 == 0 and cell_rows > 256:
-        cut = cell_rows // 512 * 256
-        shares = [(0, cut), (cut, cell_rows - cut)]
+    if cell_rows % 256 == 0 and cell_rows >= 768:
+        cuts = [256 * -(-i * (cell_rows // 256) // 3) for i in range(4)]
     else:
-        shares = [(0, cell_rows)]
+        cuts = [0, cell_rows]
+    shares = [(begin, end - begin) for begin, end in zip(cuts, cuts[1:])]
     parts = len(shares)
     prior = [[] for _ in range(parts)]
 
@@ -790,9 +790,9 @@
         gathers.append(take_grads(0, sts))
         slot(rings[1], gathers[0])
         slot(rings[1], gathers[0])
-        gathers.append(take_grads(1, take_stats(1)))
-        slot(gathers[0])
-        slot(gathers[0], gathers[1])
+        sts = take_stats(1)
+        finish(gathers[0])
+        gathers.append(take_grads(1, sts))
         for j in range(parts):
             multiply_back(0, j)
             slot(gathers[1])

time: 366 us -> 355 us (0.970)
  waiting for transfers between devices: 111 us -> 97.6 us
  Pallas kernels: 147 us -> 152 us
    ppermute x42, waiting for transfers between devices: 99.9 us -> 89 us  [hop(): return lax.ppermute(v, 'cell', self.dirs[way])]
    pallas_call x2 -> x3, Pallas kernels: 28.4 us -> 32.4 us  [backward_first(): pl.pallas_call(functools.partial(bwd_first_kernel, n, unit, offsets, len(...]
  transfers between devices with their start and end apart: 57 -> 57, of which waited for: 24 -> 20; matrix products, arithmetic and copies ran while one was open for 5% -> 5% of each run, Pallas kernels for 31% -> 32%
where the time goes in v3:
time: 355 us; the launch traced here: 354 us
  Pallas kernels  152 us (43%)
  waiting for transfers between devices  97.6 us (27%)
  starting transfers between devices  61.4 us (17%)
  other arithmetic  21.4 us (6%)
  local copies, waits for them, and re-layouts  17.3 us (5%)
  between operations  5.04 us (1%)
    ppermute x42, waiting for transfers between devices, hop(): return lax.ppermute(v, 'cell', self.dirs[way])  89 us
    pallas_call x4, Pallas kernels, forward(): pl.pallas_call(functools.partial(fwd_kernel, n, unit, cols, sums is not N...  62.1 us
    ppermute x42, starting transfers between devices, hop(): return lax.ppermute(v, 'cell', self.dirs[way])  45.1 us
    pallas_call x3, Pallas kernels, backward_first(): pl.pallas_call(functools.partial(bwd_first_kernel, n, unit, offsets, len(...  32.4 us
    pallas_call x1, Pallas kernels, backward_last(): pl.pallas_call(functools.partial(bwd_last_kernel, n, unit, offsets, scale...  30.5 us
    pallas_call x1, Pallas kernels, prep(): pl.pallas_call(prep_kernel, grid=(layers, rows // tile), in_specs=[pl.Blo...  11.2 us
    ppermute x14, starting transfers between devices, send(): return lax.ppermute(v, 'spot', pairs)  10.4 us
    ppermute x14, waiting for transfers between devices, send(): return lax.ppermute(v, 'spot', pairs)  8.65 us
  transfers between devices with their start and end apart: 57, of which 20 were waited for; matrix products, arithmetic and copies ran while one was open for 5% of the time, Pallas kernels for 32%

profile of v3, /device:TPU:0, one launch (start us, length us, event | category | flops | bytes accessed | tf_op | source)
XLA Modules:
  0.0 354.3 jit_solution(11756179093347621894)
XLA Ops:
  1.8 3.6 %slice.42 = f32[2816,256]{1,0:T(8,128)} slice(f32[2816,512]{1,0:T(8,128)} %refs_15_.1), slice={[0:2816], [0:256]} | slice | bytes 5767168 | tf_op jit(solution)/shard_map/slice | solution.py:664
  5.9 2.5 collective-permute-start.2
  8.4 2.4 deal.1
  10.7 5.8 %all-to-all-start = ((f32[8,72,512]{2,1,0:T(8,128)}), f32[8,72,512]{2,1,0:T(8,128)}, u32[]{:S(2)}, u32[]{:S(2)}) async-start(f32[8,72,512]{2,1,0:T(8,128)} %deal.1), calls=%async_computation | async-start | bytes 2359296 | tf_op jit(solution)/shard_map/all_to_all | solution.py:225
  17.3 11.2 %prep.1 = (bf16[1024,2816]{1,0:T(8,128)(2,1)}, bf16[1024,2816]{1,0:T(8,128)(2,1)}, f32[2,8,512]{2,1,0:T(8,128)}) custom-call(f32[2,2816,512]{2,1,0:T(8,128)} %refs_0_.5, f32[2,1,2816]{2,1,0:T(1,128)} %reshape.24.kept_ref.refs_1_), custom_call_target="tpu_custom_call" | custom-call | flops 1 | bytes 1 | tf_op jit(solution)/shard_map/prep/pallas_call | solution.py:88
  28.5 15.7 %fwd.4 = (f32[72,1024]{1,0:T(8,128)}, f32[72,1024]{1,0:T(8,128)}, f32[72,1024]{1,0:T(8,128)}, f32[72,1024]{1,0:T(8,128)}, f32[72,1024]{1,0:T(8,128)}, /*index=5*...) custom-call(s32[5]{0:T(128)} %dynamic-slice_bitcast_fusion.me_ref, ...), custom_call_target="tpu_custom_call" | custom-call | flops 1 | bytes 1 | tf_op jit(solution)/shard_map/fwd/pallas_call | solution.py:171
  44.1 2.1 collective-permute-start.3
  46.3 15.5 %fwd.5 = (f32[64,1024]{1,0:T(8,128)}, f32[64,1024]{1,0:T(8,128)}, f32[64,1024]{1,0:T(8,128)}, f32[64,1024]{1,0:T(8,128)}, f32[64,1024]{1,0:T(8,128)}, /*index=5*...) custom-call(s32[5]{0:T(128)} %dynamic-slice_bitcast_fusion.me_ref, ...), custom_call_target="tpu_custom_call" | custom-call | flops 1 | bytes 1 | tf_op jit(solution)/shard_map/fwd/pallas_call | solution.py:171
  61.8 3.6 %slice.43 = f32[2816,256]{1,0:T(8,128)} slice(f32[2816,512]{1,0:T(8,128)} %refs_15_.1), slice={[0:2816], [256:512]} | slice | bytes 5767168 | tf_op jit(solution)/shard_map/slice | solution.py:664
  66.9 4.8 %collective-permute-done.2.refs_0_.refs_10_ = f32[2816,256]{1,0:T(8,128)S(1)} collective-permute-done((f32[2816,256]{1,0:T(8,128)}, f32[2816,256]{1,0:T(8,128)S(1)}, u32[]{:S(2)}, u32[]{:S(2)}) %collective-permute-start.2) | collective-permute-done | bytes 2883616 | tf_op jit(solution)/shard_map/ppermute | solution.py:657
  71.8 1.7 collective-permute-start.1
  73.5 1.6 collective-permute-start.10
  75.5 1.5 collective-permute-start.8
  77.1 1.6 copy-done.1
  78.7 1.8 collective-permute-start.9
  80.5 15.5 %fwd.6 = (f32[64,1024]{1,0:T(8,128)}, f32[64,1024]{1,0:T(8,128)}, f32[64,1024]{1,0:T(8,128)}, f32[64,1024]{1,0:T(8,128)}, f32[64,1024]{1,0:T(8,128)}, /*index=5*...) custom-call(s32[5]{0:T(128)} %dynamic-slice_bitcast_fusion.me_ref, ...), custom_call_target="tpu_custom_call" | custom-call | flops 1 | bytes 1 | tf_op jit(solution)/shard_map/fwd/pallas_call | solution.py:171
  98.3 1.6 collective-permute-start.14
  102.8 1.8 collective-permute-start.13
  104.6 3.6 %collective-permute-done.14 = f32[72,1024]{1,0:T(8,128)S(1)} collective-permute-done((f32[72,1024]{1,0:T(8,128)S(1)}, f32[72,1024]{1,0:T(8,128)S(1)}, u32[]{:S(2)}, u32[]{:S(2)}) %collective-permute-start.14) | collective-permute-done | bytes 294944 | tf_op jit(solution)/shard_map/ppermute | solution.py:544
  108.4 1.4 collective-permute-done.15
  109.8 1.6 collective-permute-start.7
  111.4 4.0 %collective-permute-done.12 = f32[64,1024]{1,0:T(8,128)S(1)} collective-permute-done((f32[64,1024]{1,0:T(8,128)S(1)}, f32[64,1024]{1,0:T(8,128)S(1)}, u32[]{:S(2)}, u32[]{:S(2)}) %collective-permute-start.12) | collective-permute-done | bytes 262176 | tf_op jit(solution)/shard_map/ppermute | solution.py:544
  115.4 4.2 %collective-permute-done.6 = f32[64,1024]{1,0:T(8,128)S(1)} collective-permute-done((f32[64,1024]{1,0:T(8,128)S(1)}, f32[64,1024]{1,0:T(8,128)S(1)}, u32[]{:S(2)}, u32[]{:S(2)}) %collective-permute-start.6) | collective-permute-done | bytes 262176 | tf_op jit(solution)/shard_map/ppermute | solution.py:544
  119.7 1.6 collective-permute-start.20
  122.0 1.6 collective-permute-start.19
  124.1 5.6 %collective-permute-done.20 = f32[72,1024]{1,0:T(8,128)S(1)} collective-permute-done((f32[72,1024]{1,0:T(8,128)S(1)}, f32[72,1024]{1,0:T(8,128)S(1)}, u32[]{:S(2)}, u32[]{:S(2)}) %collective-permute-start.20) | collective-permute-done | bytes 294944 | tf_op jit(solution)/shard_map/ppermute | solution.py:544
  129.6 1.6 collective-permute-start.17
  131.2 4.0 %collective-permute-done.19 = f32[64,1024]{1,0:T(8,128)S(1)} collective-permute-done((f32[64,1024]{1,0:T(8,128)S(1)}, f32[64,1024]{1,0:T(8,128)S(1)}, u32[]{:S(2)}, u32[]{:S(2)}) %collective-permute-start.19) | collective-permute-done | bytes 262176 | tf_op jit(solution)/shard_map/ppermute | solution.py:544
  136.0 2.8 collective-permute-done.17
  142.1 1.5 collective-permute-start.25
  143.6 2.9 collective-permute-done.21.refs_1_.refs_18_
  146.6 1.7 copy-done.2
  148.3 15.5 %fwd.7 = (f32[64,1024]{1,0:T(8,128)}, f32[64,1024]{1,0:T(8,128)}, f32[64,1024]{1,0:T(8,128)}, f32[64,1024]{1,0:T(8,128)}, f32[64,1024]{1,0:T(8,128)}, /*index=5*...) custom-call(s32[5]{0:T(128)} %dynamic-slice_bitcast_fusion.me_ref, ...), custom_call_target="tpu_custom_call" | custom-call | flops 1 | bytes 1 | tf_op jit(solution)/shard_map/fwd/pallas_call | solution.py:171
  163.8 1.9 add_add_fusion.3.refs_0_.refs_8_
  167.3 1.6 collective-permute-start.22
  169.3 6.7 %collective-permute-done.27 = f32[64,1024]{1,0:T(8,128)S(1)} collective-permute-done((f32[64,1024]{1,0:T(8,128)S(1)}, f32[64,1024]{1,0:T(8,128)S(1)}, u32[]{:S(2)}, u32[]{:S(2)}) %collective-permute-start.27) | collective-permute-done | bytes 262176 | tf_op jit(solution)/shard_map/ppermute | solution.py:544
  176.0 4.8 %collective-permute-done.23 = f32[64,1024]{1,0:T(8,128)S(1)} collective-permute-done((f32[64,1024]{1,0:T(8,128)}, f32[64,1024]{1,0:T(8,128)S(1)}, u32[]{:S(2)}, u32[]{:S(2)}) %collective-permute-start.23) | collective-permute-done | bytes 262176 | tf_op jit(solution)/shard_map/ppermute | solution.py:544
  180.8 1.8 add_add_fusion.2.refs_1_.refs_9_
  183.7 1.6 collective-permute-start.28
  185.8 2.7 stats.2.refs_4_
  188.4 1.5 collective-permute-start.31
  191.2 1.3 collective-permute-done.29
  194.2 3.8 %grads.2 = (f32[128,1024]{1,0:T(8,128)}, f32[16,1024]{1,0:T(8,128)}) custom-call(s32[5]{0:T(128)} %dynamic-slice_bitcast_fusion.me_ref, f32[1]{0:T(128)} %bitcast.2.ent_ref, s32[1,512]{1,0:T(1,128)} %bitcast.13, f32[72,1024]{1,0:T(8,128)} %add_add_fusion.tot_ref.refs_0_.refs_1_.refs_8_.refs_2_, f32[8,72,512]{2,1,0:T(8,128)} %all-to-all-done.slab_ref.refs_2_, ...), custom_call_target="tpu_custom_call" | custom-call | tf_op jit(solution)/shard_map/grads/pallas_call | solution.py:373
  198.4 1.6 collective-permute-start.34
  200.0 1.6 collective-permute-start.35
  202.0 16.0 %collective-permute-done.35 = f32[64,1024]{1,0:T(8,128)S(1)} collective-permute-done((f32[64,1024]{1,0:T(8,128)S(1)}, f32[64,1024]{1,0:T(8,128)S(1)}, u32[]{:S(2)}, u32[]{:S(2)}) %collective-permute-start.35) | collective-permute-done | bytes 262176 | tf_op jit(solution)/shard_map/ppermute | solution.py:544
  218.6 1.5 collective-permute-start.38
  220.2 1.6 collective-permute-start.39
  221.8 15.1 %collective-permute-done.39 = f32[64,1024]{1,0:T(8,128)S(1)} collective-permute-done((f32[64,1024]{1,0:T(8,128)S(1)}, f32[64,1024]{1,0:T(8,128)S(1)}, u32[]{:S(2)}, u32[]{:S(2)}) %collective-permute-start.39) | collective-permute-done | bytes 262176 | tf_op jit(solution)/shard_map/ppermute | solution.py:544
  236.9 1.6 collective-permute-start.40
  239.0 1.7 add_add_fusion.1.refs_1_.refs_9_
  240.7 2.7 stats.3.refs_4_
  243.4 5.4 %collective-permute-done.40.refs_5_ = f32[128,1024]{1,0:T(8,128)S(1)} collective-permute-done((f32[128,1024]{1,0:T(8,128)S(1)}, f32[128,1024]{1,0:T(8,128)S(1)}, u32[]{:S(2)}, u32[]{:S(2)}) %collective-permute-start.40) | collective-permute-done | bytes 524320 | tf_op jit(solution)/shard_map/ppermute | solution.py:544
  250.0 1.6 collective-permute-start.42
  253.5 7.2 %collective-permute-done.42.refs_7_ = f32[128,1024]{1,0:T(8,128)S(1)} collective-permute-done((f32[128,1024]{1,0:T(8,128)S(1)}, f32[128,1024]{1,0:T(8,128)S(1)}, u32[]{:S(2)}, u32[]{:S(2)}) %collective-permute-start.42) | collective-permute-done | bytes 524320 | tf_op jit(solution)/shard_map/ppermute | solution.py:544
  262.1 3.8 %grads.3 = (f32[136,1024]{1,0:T(8,128)}, f32[16,1024]{1,0:T(8,128)}) custom-call(s32[5]{0:T(128)} %dynamic-slice_bitcast_fusion.me_ref, f32[1]{0:T(128)} %bitcast.2.ent_ref, s32[1,512]{1,0:T(1,128)} %bitcast.15, f32[72,1024]{1,0:T(8,128)} %add_add_fusion.tot_ref.refs_0_.refs_1_.refs_8_.refs_2_, f32[8,72,512]{2,1,0:T(8,128)} %all-to-all-done.slab_ref.refs_2_, ...), custom_call_target="tpu_custom_call" | custom-call | tf_op jit(solution)/shard_map/grads/pallas_call | solution.py:373
  268.0 11.4 %bwd_first.3.refs_4_ = f32[1024,1024]{1,0:T(8,128)} custom-call(s32[5]{0:T(128)} %dynamic-slice_bitcast_fusion.me_ref, f32[128,1024]{1,0:T(8,128)} %get-tuple-element.409.refs_0_, f32[128,1024]{1,0:T(8,128)} %copy-done.3, f32[128,1024]{1,0:T(8,128)} %copy-done.4, f32[128,1024]{1,0:T(8,128)} %copy-done.5, f32[128,1024]{1,0:T(8,128)} %copy-done.6, ...), custom_call_target="tpu_custom_call" | custom-call | flops 1 | bytes 1 | tf_op jit(solution)/shard_map/bwd_first/pallas_call | solution.py:468
  281.5 11.4 %bwd_first.4.refs_5_ = f32[1024,1024]{1,0:T(8,128)} custom-call(s32[5]{0:T(128)} %dynamic-slice_bitcast_fusion.me_ref, f32[128,1024]{1,0:T(8,128)} %get-tuple-element.409.refs_0_, f32[128,1024]{1,0:T(8,128)} %copy-done.3, f32[128,1024]{1,0:T(8,128)} %copy-done.4, f32[128,1024]{1,0:T(8,128)} %copy-done.5, f32[128,1024]{1,0:T(8,128)} %copy-done.6, ...), custom_call_target="tpu_custom_call" | custom-call | flops 1 | bytes 1 | tf_op jit(solution)/shard_map/bwd_first/pallas_call | solution.py:468
  295.0 9.6 %bwd_first.5.refs_6_ = f32[768,1024]{1,0:T(8,128)} custom-call(s32[5]{0:T(128)} %dynamic-slice_bitcast_fusion.me_ref, f32[128,1024]{1,0:T(8,128)} %get-tuple-element.409.refs_0_, f32[128,1024]{1,0:T(8,128)} %copy-done.3, f32[128,1024]{1,0:T(8,128)} %copy-done.4, f32[128,1024]{1,0:T(8,128)} %copy-done.5, f32[128,1024]{1,0:T(8,128)} %copy-done.6, ...), custom_call_target="tpu_custom_call" | custom-call | flops 1 | bytes 1 | tf_op jit(solution)/shard_map/bwd_first/pallas_call | solution.py:468
  304.7 1.2 collective-permute-start.52
  305.9 1.3 slice_reduce_fusion.1
  309.1 5.4 %collective-permute-done.52.refs_14_ = f32[136,1024]{1,0:T(8,128)S(1)} collective-permute-done((f32[136,1024]{1,0:T(8,128)S(1)}, f32[136,1024]{1,0:T(8,128)S(1)}, u32[]{:S(2)}, u32[]{:S(2)}) %collective-permute-start.52) | collective-permute-done | bytes 557088 | tf_op jit(solution)/shard_map/ppermute | solution.py:544
  315.3 30.5 %bwd_last.1 = (f32[2,2816,512]{2,1,0:T(8,128)}, f32[2,1,2816]{2,1,0:T(1,128)}) custom-call(s32[5]{0:T(128)} %dynamic-slice_bitcast_fusion.me_ref, f32[2,2816,512]{2,1,0:T(8,128)} %refs_0_.5, f32[2,1,2816]{2,1,0:T(1,128)} %reshape.24.kept_ref.refs_1_, f32[72,1024]{1,0:T(8,128)} %add_add_fusion.tot_ref.refs_0_.refs_1_.refs_8_.refs_2_, ...), custom_call_target="tpu_custom_call" | custom-call | flops 1 | bytes 1 | tf_op jit(solution)/shard_map/bwd_last/pallas_call | solution.py:511
  351.8 1.4 subtract_multiply_fusion.1
  (192 shorter events, 40.1 us)
Async XLA Ops:
  5.4 23.1 %collective-permute-start = (f32[2816,512]{1,0:T(8,128)}, f32[2816,512]{1,0:T(8,128)}, u32[]{:S(2)}, u32[]{:S(2)}) collective-permute-start(f32[2816,512]{1,0:T(8,128)} %refs_15_.1), channel_id=1, source_target_pairs={{0,1},{1,0},{2,3},{3,2},{4,5},{5,4},{6,7},{7,6},{8,9},{9,8},{10,11... | collective-permute-start | bytes 17301512 | tf_op jit(solution)/shard_map/ppermute | solution.py:657
  5.9 65.8 %collective-permute-start.2 = (f32[2816,256]{1,0:T(8,128)}, f32[2816,256]{1,0:T(8,128)S(1)}, u32[]{:S(2)}, u32[]{:S(2)}) collective-permute-start(f32[2816,256]{1,0:T(8,128)} %slice.42), channel_id=1, source_target_pairs={{0,2},{1,3},{2,0},{3,1},{4,6},{5,7},{6,4},{7,5},{8,10},{9,11},{10,... | collective-permute-start | bytes 8650760 | tf_op jit(solution)/shard_map/ppermute | solution.py:657
  10.7 35.5 %all-to-all-start = ((f32[8,72,512]{2,1,0:T(8,128)}), f32[8,72,512]{2,1,0:T(8,128)}, u32[]{:S(2)}, u32[]{:S(2)}) async-start(f32[8,72,512]{2,1,0:T(8,128)} %deal.1), calls=%async_computation | async-start | bytes 2359296 | tf_op jit(solution)/shard_map/all_to_all | solution.py:225
  44.1 21.3 %collective-permute-start.3 = (f32[72,1024]{1,0:T(8,128)}, f32[72,1024]{1,0:T(8,128)S(1)}, u32[]{:S(2)}, u32[]{:S(2)}) collective-permute-start(f32[72,1024]{1,0:T(8,128)} %get-tuple-element.275), channel_id=1, source_target_pairs={{0,8},{8,16},{16,24},{24,28},{28,20},{20,12},{12,4},{4,0},{1,9},{9... | collective-permute-start | bytes 884744 | tf_op jit(solution)/shard_map/ppermute | solution.py:544
  46.2 19.2 %collective-permute-start.4 = (f32[72,1024]{1,0:T(8,128)}, f32[72,1024]{1,0:T(8,128)S(1)}, u32[]{:S(2)}, u32[]{:S(2)}) collective-permute-start(f32[72,1024]{1,0:T(8,128)} %get-tuple-element.276), channel_id=1, source_target_pairs={{8,0},{16,8},{24,16},{28,24},{20,28},{12,20},{4,12},{0,4},{9,1},{1... | collective-permute-start | bytes 884744 | tf_op jit(solution)/shard_map/ppermute | solution.py:544
  71.8 5.3 %collective-permute-start.5 = (f32[2816,256]{1,0:T(8,128)S(1)}, f32[2816,256]{1,0:T(8,128)S(1)}, u32[]{:S(2)}, u32[]{:S(2)}) collective-permute-start(f32[2816,256]{1,0:T(8,128)S(1)} %collective-permute-done.2.refs_0_.refs_10_), channel_id=1, source_target_pairs={{0,1},{1,0},{2,3},{3,2},{4,5},{5,4},{6,7},{7,6},{8,9},{9,8},{10,11... | collective-permute-start | bytes 8650760 | tf_op jit(solution)/shard_map/ppermute | solution.py:657
  71.8 69.3 %collective-permute-start.1 = (f32[2816,256]{1,0:T(8,128)}, f32[2816,256]{1,0:T(8,128)}, u32[]{:S(2)}, u32[]{:S(2)}) collective-permute-start(f32[2816,256]{1,0:T(8,128)} %slice.43), channel_id=1, source_target_pairs={{0,2},{1,3},{2,0},{3,1},{4,6},{5,7},{6,4},{7,5},{8,10},{9,11},{10,... | collective-permute-start | bytes 8650760 | tf_op jit(solution)/shard_map/ppermute | solution.py:657
  73.5 22.5 %collective-permute-start.10 = (f32[72,1024]{1,0:T(8,128)}, f32[72,1024]{1,0:T(8,128)}, u32[]{:S(2)}, u32[]{:S(2)}) collective-permute-start(f32[72,1024]{1,0:T(8,128)} %add.145), channel_id=1, source_target_pairs={{0,8},{8,16},{16,24},{24,28},{28,20},{20,12},{12,4},{4,0},{1,9},{9... | collective-permute-start | bytes 884744 | tf_op jit(solution)/shard_map/ppermute | solution.py:544
  75.1 21.0 %collective-permute-start.11 = (f32[72,1024]{1,0:T(8,128)}, f32[72,1024]{1,0:T(8,128)}, u32[]{:S(2)}, u32[]{:S(2)}) collective-permute-start(f32[72,1024]{1,0:T(8,128)} %add.146), channel_id=1, source_target_pairs={{8,0},{16,8},{24,16},{28,24},{20,28},{12,20},{4,12},{0,4},{9,1},{1... | collective-permute-start | bytes 884744 | tf_op jit(solution)/shard_map/ppermute | solution.py:544
  75.5 20.5 %collective-permute-start.8 = (f32[64,1024]{1,0:T(8,128)}, f32[64,1024]{1,0:T(8,128)}, u32[]{:S(2)}, u32[]{:S(2)}) collective-permute-start(f32[64,1024]{1,0:T(8,128)} %get-tuple-element.296), channel_id=1, source_target_pairs={{8,0},{16,8},{24,16},{28,24},{20,28},{12,20},{4,12},{0,4},{9,1},{1... | collective-permute-start | bytes 786440 | tf_op jit(solution)/shard_map/ppermute | solution.py:544
  78.7 17.4 %collective-permute-start.9 = (f32[64,1024]{1,0:T(8,128)}, f32[64,1024]{1,0:T(8,128)}, u32[]{:S(2)}, u32[]{:S(2)}) collective-permute-start(f32[64,1024]{1,0:T(8,128)} %get-tuple-element.297), channel_id=1, source_target_pairs={{0,8},{8,16},{16,24},{24,28},{28,20},{20,12},{12,4},{4,0},{1,9},{9... | collective-permute-start | bytes 786440 | tf_op jit(solution)/shard_map/ppermute | solution.py:544
  97.2 41.5 %copy-start.20 = (f32[72,1024]{1,0:T(8,128)S(1)}, f32[72,1024]{1,0:T(8,128)}, u32[]{:S(2)}) copy-start(f32[72,1024]{1,0:T(8,128)} %get-tuple-element.349) | copy-start | bytes 884740
  98.3 9.9 %collective-permute-start.14 = (f32[72,1024]{1,0:T(8,128)S(1)}, f32[72,1024]{1,0:T(8,128)S(1)}, u32[]{:S(2)}, u32[]{:S(2)}) collective-permute-start(f32[72,1024]{1,0:T(8,128)S(1)} %add.149), channel_id=1, source_target_pairs={{0,8},{8,16},{16,24},{24,28},{28,20},{20,12},{12,4},{4,0},{1,9},{9... | collective-permute-start | bytes 884744 | tf_op jit(solution)/shard_map/ppermute | solution.py:544
  99.9 9.9 %collective-permute-start.15 = (f32[72,1024]{1,0:T(8,128)S(1)}, f32[72,1024]{1,0:T(8,128)S(1)}, u32[]{:S(2)}, u32[]{:S(2)}) collective-permute-start(f32[72,1024]{1,0:T(8,128)S(1)} %add.150), channel_id=1, source_target_pairs={{8,0},{16,8},{24,16},{28,24},{20,28},{12,20},{4,12},{0,4},{9,1},{1... | collective-permute-start | bytes 884744 | tf_op jit(solution)/shard_map/ppermute | solution.py:544
  101.4 38.1 %copy-start.22 = (f32[64,1024]{1,0:T(8,128)S(1)}, f32[64,1024]{1,0:T(8,128)}, u32[]{:S(2)}) copy-start(f32[64,1024]{1,0:T(8,128)} %get-tuple-element.346) | copy-start | bytes 786436
  102.6 37.7 %copy-start.27 = (f32[64,1024]{1,0:T(8,128)S(1)}, f32[64,1024]{1,0:T(8,128)}, u32[]{:S(2)}) copy-start(f32[64,1024]{1,0:T(8,128)} %get-tuple-element.342) | copy-start | bytes 786436
  102.6 12.9 %collective-permute-start.12 = (f32[64,1024]{1,0:T(8,128)S(1)}, f32[64,1024]{1,0:T(8,128)S(1)}, u32[]{:S(2)}, u32[]{:S(2)}) collective-permute-start(f32[64,1024]{1,0:T(8,128)S(1)} %add.147), channel_id=1, source_target_pairs={{8,0},{16,8},{24,16},{28,24},{20,28},{12,20},{4,12},{0,4},{9,1},{1... | collective-permute-start | bytes 786440 | tf_op jit(solution)/shard_map/ppermute | solution.py:544
  102.8 12.6 %collective-permute-start.13 = (f32[64,1024]{1,0:T(8,128)S(1)}, f32[64,1024]{1,0:T(8,128)S(1)}, u32[]{:S(2)}, u32[]{:S(2)}) collective-permute-start(f32[64,1024]{1,0:T(8,128)S(1)} %add.148), channel_id=1, source_target_pairs={{0,8},{8,16},{16,24},{24,28},{28,20},{20,12},{12,4},{4,0},{1,9},{9... | collective-permute-start | bytes 786440 | tf_op jit(solution)/shard_map/ppermute | solution.py:544
  108.2 11.4 %collective-permute-start.6 = (f32[64,1024]{1,0:T(8,128)S(1)}, f32[64,1024]{1,0:T(8,128)S(1)}, u32[]{:S(2)}, u32[]{:S(2)}) collective-permute-start(f32[64,1024]{1,0:T(8,128)S(1)} %copy-done.42), channel_id=1, source_target_pairs={{8,0},{16,8},{24,16},{28,24},{20,28},{12,20},{4,12},{0,4},{9,1},{1... | collective-permute-start | bytes 786440 | tf_op jit(solution)/shard_map/ppermute | solution.py:544
  109.8 9.8 %collective-permute-start.7 = (f32[64,1024]{1,0:T(8,128)S(1)}, f32[64,1024]{1,0:T(8,128)S(1)}, u32[]{:S(2)}, u32[]{:S(2)}) collective-permute-start(f32[64,1024]{1,0:T(8,128)S(1)} %copy-done.41), channel_id=1, source_target_pairs={{0,8},{8,16},{16,24},{24,28},{28,20},{20,12},{12,4},{4,0},{1,9},{9... | collective-permute-start | bytes 786440 | tf_op jit(solution)/shard_map/ppermute | solution.py:544
  119.7 9.9 %collective-permute-start.20 = (f32[72,1024]{1,0:T(8,128)S(1)}, f32[72,1024]{1,0:T(8,128)S(1)}, u32[]{:S(2)}, u32[]{:S(2)}) collective-permute-start(f32[72,1024]{1,0:T(8,128)S(1)} %add.155), channel_id=1, source_target_pairs={{0,8},{8,16},{16,24},{24,28},{28,20},{20,12},{12,4},{4,0},{1,9},{9... | collective-permute-start | bytes 884744 | tf_op jit(solution)/shard_map/ppermute | solution.py:544
  121.5 9.7 %collective-permute-start.18 = (f32[64,1024]{1,0:T(8,128)S(1)}, f32[64,1024]{1,0:T(8,128)S(1)}, u32[]{:S(2)}, u32[]{:S(2)}) collective-permute-start(f32[64,1024]{1,0:T(8,128)S(1)} %add.153), channel_id=1, source_target_pairs={{8,0},{16,8},{24,16},{28,24},{20,28},{12,20},{4,12},{0,4},{9,1},{1... | collective-permute-start | bytes 786440 | tf_op jit(solution)/shard_map/ppermute | solution.py:544
  122.0 13.2 %collective-permute-start.19 = (f32[64,1024]{1,0:T(8,128)S(1)}, f32[64,1024]{1,0:T(8,128)S(1)}, u32[]{:S(2)}, u32[]{:S(2)}) collective-permute-start(f32[64,1024]{1,0:T(8,128)S(1)} %add.154), channel_id=1, source_target_pairs={{0,8},{8,16},{16,24},{24,28},{28,20},{20,12},{12,4},{4,0},{1,9},{9... | collective-permute-start | bytes 786440 | tf_op jit(solution)/shard_map/ppermute | solution.py:544
  123.6 11.7 %collective-permute-start.16 = (f32[64,1024]{1,0:T(8,128)S(1)}, f32[64,1024]{1,0:T(8,128)S(1)}, u32[]{:S(2)}, u32[]{:S(2)}) collective-permute-start(f32[64,1024]{1,0:T(8,128)S(1)} %add.151), channel_id=1, source_target_pairs={{8,0},{16,8},{24,16},{28,24},{20,28},{12,20},{4,12},{0,4},{9,1},{1... | collective-permute-start | bytes 786440 | tf_op jit(solution)/shard_map/ppermute | solution.py:544
  129.6 9.1 %collective-permute-start.17 = (f32[64,1024]{1,0:T(8,128)S(1)}, f32[64,1024]{1,0:T(8,128)S(1)}, u32[]{:S(2)}, u32[]{:S(2)}) collective-permute-start(f32[64,1024]{1,0:T(8,128)S(1)} %add.152), channel_id=1, source_target_pairs={{0,8},{8,16},{16,24},{24,28},{28,20},{20,12},{12,4},{4,0},{1,9},{9... | collective-permute-start | bytes 786440 | tf_op jit(solution)/shard_map/ppermute | solution.py:544
  141.0 5.6 %collective-permute-start.21 = (f32[2816,256]{1,0:T(8,128)}, f32[2816,256]{1,0:T(8,128)S(1)}, u32[]{:S(2)}, u32[]{:S(2)}) collective-permute-start(f32[2816,256]{1,0:T(8,128)} %collective-permute-done.1.refs_0_.refs_17_), channel_id=1, source_target_pairs={{0,1},{1,0},{2,3},{3,2},{4,5},{5,4},{6,7},{7,6},{8,9},{9,8},{10,11... | collective-permute-start | bytes 8650760 | tf_op jit(solution)/shard_map/ppermute | solution.py:657
  141.1 22.7 %collective-permute-start.26 = (f32[64,1024]{1,0:T(8,128)}, f32[64,1024]{1,0:T(8,128)}, u32[]{:S(2)}, u32[]{:S(2)}) collective-permute-start(f32[64,1024]{1,0:T(8,128)} %add.158), channel_id=1, source_target_pairs={{8,0},{16,8},{24,16},{28,24},{20,28},{12,20},{4,12},{0,4},{9,1},{1... | collective-permute-start | bytes 786440 | tf_op jit(solution)/shard_map/ppermute | solution.py:544
  141.6 22.2 %collective-permute-start.24 = (f32[64,1024]{1,0:T(8,128)}, f32[64,1024]{1,0:T(8,128)}, u32[]{:S(2)}, u32[]{:S(2)}) collective-permute-start(f32[64,1024]{1,0:T(8,128)} %add.156), channel_id=1, source_target_pairs={{8,0},{16,8},{24,16},{28,24},{20,28},{12,20},{4,12},{0,4},{9,1},{1... | collective-permute-start | bytes 786440 | tf_op jit(solution)/shard_map/ppermute | solution.py:544
  142.1 21.7 %collective-permute-start.25 = (f32[64,1024]{1,0:T(8,128)S(1)}, f32[64,1024]{1,0:T(8,128)}, u32[]{:S(2)}, u32[]{:S(2)}) collective-permute-start(f32[64,1024]{1,0:T(8,128)S(1)} %add.157), channel_id=1, source_target_pairs={{0,8},{8,16},{16,24},{24,28},{28,20},{20,12},{12,4},{4,0},{1,9},{9... | collective-permute-start | bytes 786440 | tf_op jit(solution)/shard_map/ppermute | solution.py:544
  166.8 9.2 %collective-permute-start.27 = (f32[64,1024]{1,0:T(8,128)S(1)}, f32[64,1024]{1,0:T(8,128)S(1)}, u32[]{:S(2)}, u32[]{:S(2)}) collective-permute-start(f32[64,1024]{1,0:T(8,128)S(1)} %add.161), channel_id=1, source_target_pairs={{8,0},{16,8},{24,16},{28,24},{20,28},{12,20},{4,12},{0,4},{9,1},{1... | collective-permute-start | bytes 786440 | tf_op jit(solution)/shard_map/ppermute | solution.py:544
  167.3 8.7 %collective-permute-start.22 = (f32[64,1024]{1,0:T(8,128)}, f32[64,1024]{1,0:T(8,128)S(1)}, u32[]{:S(2)}, u32[]{:S(2)}) collective-permute-start(f32[64,1024]{1,0:T(8,128)} %get-tuple-element.364), channel_id=1, source_target_pairs={{0,8},{8,16},{16,24},{24,28},{28,20},{20,12},{12,4},{4,0},{1,9},{9... | collective-permute-start | bytes 786440 | tf_op jit(solution)/shard_map/ppermute | solution.py:544
  168.9 11.9 %collective-permute-start.23 = (f32[64,1024]{1,0:T(8,128)}, f32[64,1024]{1,0:T(8,128)S(1)}, u32[]{:S(2)}, u32[]{:S(2)}) collective-permute-start(f32[64,1024]{1,0:T(8,128)} %get-tuple-element.365), channel_id=1, source_target_pairs={{8,0},{16,8},{24,16},{28,24},{20,28},{12,20},{4,12},{0,4},{9,1},{1... | collective-permute-start | bytes 786440 | tf_op jit(solution)/shard_map/ppermute | solution.py:544
  183.6 36.5 %copy-start.23 = (f32[64,1024]{1,0:T(8,128)S(1)}, f32[64,1024]{1,0:T(8,128)}, u32[]{:S(2)}) copy-start(f32[64,1024]{1,0:T(8,128)} %get-tuple-element.417) | copy-start | bytes 786436
  183.7 7.5 %collective-permute-start.28 = (f32[64,1024]{1,0:T(8,128)S(1)}, f32[64,1024]{1,0:T(8,128)S(1)}, u32[]{:S(2)}, u32[]{:S(2)}) collective-permute-start(f32[64,1024]{1,0:T(8,128)S(1)} %add.164), channel_id=1, source_target_pairs={{0,8},{8,16},{16,24},{24,28},{28,20},{20,12},{12,4},{4,0},{1,9},{9... | collective-permute-start | bytes 786440 | tf_op jit(solution)/shard_map/ppermute | solution.py:544
  185.3 7.2 %collective-permute-start.29 = (f32[64,1024]{1,0:T(8,128)S(1)}, f32[64,1024]{1,0:T(8,128)S(1)}, u32[]{:S(2)}, u32[]{:S(2)}) collective-permute-start(f32[64,1024]{1,0:T(8,128)S(1)} %add.165), channel_id=1, source_target_pairs={{8,0},{16,8},{24,16},{28,24},{20,28},{12,20},{4,12},{0,4},{9,1},{1... | collective-permute-start | bytes 786440 | tf_op jit(solution)/shard_map/ppermute | solution.py:544
  188.4 4.2 %collective-permute-start.30 = (f32[64,128]{1,0:T(8,128)}, f32[64,128]{1,0:T(8,128)S(1)}, u32[]{:S(2)}, u32[]{:S(2)}) collective-permute-start(f32[64,128]{1,0:T(8,128)} %stats.2.refs_4_), channel_id=1, source_target_pairs={{0,1},{1,0},{2,3},{3,2},{4,5},{5,4},{6,7},{7,6},{8,9},{9,8},{10,11... | collective-permute-start | bytes 98312 | tf_op jit(solution)/shard_map/ppermute | solution.py:657
  188.4 4.2 %collective-permute-start.31 = (f32[64,128]{1,0:T(8,128)}, f32[64,128]{1,0:T(8,128)S(1)}, u32[]{:S(2)}, u32[]{:S(2)}) collective-permute-start(f32[64,128]{1,0:T(8,128)} %stats.2.refs_4_), channel_id=1, source_target_pairs={{0,2},{1,3},{2,0},{3,1},{4,6},{5,7},{6,4},{7,5},{8,10},{9,11},{10,... | collective-permute-start | bytes 98312 | tf_op jit(solution)/shard_map/ppermute | solution.py:657
  189.9 3.6 %collective-permute-start.32 = (f32[64,128]{1,0:T(8,128)}, f32[64,128]{1,0:T(8,128)S(1)}, u32[]{:S(2)}, u32[]{:S(2)}) collective-permute-start(f32[64,128]{1,0:T(8,128)} %stats.2.refs_4_), channel_id=1, source_target_pairs={{0,3},{1,2},{2,1},{3,0},{4,7},{5,6},{6,5},{7,4},{8,11},{9,10},{10,... | collective-permute-start | bytes 98312 | tf_op jit(solution)/shard_map/ppermute | solution.py:657
  198.0 20.1 %collective-permute-start.33 = (f32[128,1024]{1,0:T(8,128)}, f32[128,1024]{1,0:T(8,128)S(1)}, u32[]{:S(2)}, u32[]{:S(2)}) collective-permute-start(f32[128,1024]{1,0:T(8,128)} %get-tuple-element.409.refs_0_), channel_id=1, source_target_pairs={{8,0},{16,8},{24,16},{28,24},{20,28},{12,20},{4,12},{0,4},{9,1},{1... | collective-permute-start | bytes 1572872 | tf_op jit(solution)/shard_map/ppermute | solution.py:544
  198.4 19.6 %collective-permute-start.34 = (f32[128,1024]{1,0:T(8,128)}, f32[128,1024]{1,0:T(8,128)S(1)}, u32[]{:S(2)}, u32[]{:S(2)}) collective-permute-start(f32[128,1024]{1,0:T(8,128)} %get-tuple-element.409.refs_0_), channel_id=1, source_target_pairs={{0,8},{8,16},{16,24},{24,28},{28,20},{20,12},{12,4},{4,0},{1,9},{9... | collective-permute-start | bytes 1572872 | tf_op jit(solution)/shard_map/ppermute | solution.py:544
  200.0 18.0 %collective-permute-start.35 = (f32[64,1024]{1,0:T(8,128)S(1)}, f32[64,1024]{1,0:T(8,128)S(1)}, u32[]{:S(2)}, u32[]{:S(2)}) collective-permute-start(f32[64,1024]{1,0:T(8,128)S(1)} %add.168), channel_id=1, source_target_pairs={{0,8},{8,16},{16,24},{24,28},{28,20},{20,12},{12,4},{4,0},{1,9},{9... | collective-permute-start | bytes 786440 | tf_op jit(solution)/shard_map/ppermute | solution.py:544
  201.6 16.4 %collective-permute-start.36 = (f32[64,1024]{1,0:T(8,128)S(1)}, f32[64,1024]{1,0:T(8,128)S(1)}, u32[]{:S(2)}, u32[]{:S(2)}) collective-permute-start(f32[64,1024]{1,0:T(8,128)S(1)} %add.169), channel_id=1, source_target_pairs={{8,0},{16,8},{24,16},{28,24},{20,28},{12,20},{4,12},{0,4},{9,1},{1... | collective-permute-start | bytes 786440 | tf_op jit(solution)/shard_map/ppermute | solution.py:544
  218.0 49.9 %copy-start.3 = (f32[128,1024]{1,0:T(8,128)}, f32[128,1024]{1,0:T(8,128)S(1)}, u32[]{:S(2)}) copy-start(f32[128,1024]{1,0:T(8,128)S(1)} %collective-permute-done.33.refs_1_) | copy-start | bytes 1572868
  218.0 49.9 %copy-start.4 = (f32[128,1024]{1,0:T(8,128)}, f32[128,1024]{1,0:T(8,128)S(1)}, u32[]{:S(2)}) copy-start(f32[128,1024]{1,0:T(8,128)S(1)} %collective-permute-done.34.refs_2_) | copy-start | bytes 1572868
  218.1 18.9 %collective-permute-start.37 = (f32[128,1024]{1,0:T(8,128)S(1)}, f32[128,1024]{1,0:T(8,128)S(1)}, u32[]{:S(2)}, u32[]{:S(2)}) collective-permute-start(f32[128,1024]{1,0:T(8,128)S(1)} %collective-permute-done.33.refs_1_), channel_id=1, source_target_pairs={{8,0},{16,8},{24,16},{28,24},{20,28},{12,20},{4,12},{0,4},{9,1},{1... | collective-permute-start | bytes 1572872 | tf_op jit(solution)/shard_map/ppermute | solution.py:544
  218.6 18.3 %collective-permute-start.38 = (f32[128,1024]{1,0:T(8,128)S(1)}, f32[128,1024]{1,0:T(8,128)S(1)}, u32[]{:S(2)}, u32[]{:S(2)}) collective-permute-start(f32[128,1024]{1,0:T(8,128)S(1)} %collective-permute-done.34.refs_2_), channel_id=1, source_target_pairs={{0,8},{8,16},{16,24},{24,28},{28,20},{20,12},{12,4},{4,0},{1,9},{9... | collective-permute-start | bytes 1572872 | tf_op jit(solution)/shard_map/ppermute | solution.py:544
  220.2 16.7 %collective-permute-start.39 = (f32[64,1024]{1,0:T(8,128)S(1)}, f32[64,1024]{1,0:T(8,128)S(1)}, u32[]{:S(2)}, u32[]{:S(2)}) collective-permute-start(f32[64,1024]{1,0:T(8,128)S(1)} %add.173), channel_id=1, source_target_pairs={{0,8},{8,16},{16,24},{24,28},{28,20},{20,12},{12,4},{4,0},{1,9},{9... | collective-permute-start | bytes 786440 | tf_op jit(solution)/shard_map/ppermute | solution.py:544
  236.9 31.1 %copy-start.5 = (f32[128,1024]{1,0:T(8,128)}, f32[128,1024]{1,0:T(8,128)S(1)}, u32[]{:S(2)}) copy-start(f32[128,1024]{1,0:T(8,128)S(1)} %collective-permute-done.37.refs_3_) | copy-start | bytes 1572868
  236.9 11.9 %collective-permute-start.40 = (f32[128,1024]{1,0:T(8,128)S(1)}, f32[128,1024]{1,0:T(8,128)S(1)}, u32[]{:S(2)}, u32[]{:S(2)}) collective-permute-start(f32[128,1024]{1,0:T(8,128)S(1)} %collective-permute-done.37.refs_3_), channel_id=1, source_target_pairs={{8,0},{16,8},{24,16},{28,24},{20,28},{12,20},{4,12},{0,4},{9,1},{1... | collective-permute-start | bytes 1572872 | tf_op jit(solution)/shard_map/ppermute | solution.py:544
  238.5 11.5 %collective-permute-start.41 = (f32[128,1024]{1,0:T(8,128)S(1)}, f32[128,1024]{1,0:T(8,128)S(1)}, u32[]{:S(2)}, u32[]{:S(2)}) collective-permute-start(f32[128,1024]{1,0:T(8,128)S(1)} %collective-permute-done.38.refs_4_), channel_id=1, source_target_pairs={{0,8},{8,16},{16,24},{24,28},{28,20},{20,12},{12,4},{4,0},{1,9},{9... | collective-permute-start | bytes 1572872 | tf_op jit(solution)/shard_map/ppermute | solution.py:544
  250.0 10.7 %collective-permute-start.42 = (f32[128,1024]{1,0:T(8,128)S(1)}, f32[128,1024]{1,0:T(8,128)S(1)}, u32[]{:S(2)}, u32[]{:S(2)}) collective-permute-start(f32[128,1024]{1,0:T(8,128)S(1)} %collective-permute-done.40.refs_5_), channel_id=1, source_target_pairs={{8,0},{16,8},{24,16},{28,24},{20,28},{12,20},{4,12},{0,4},{9,1},{1... | collective-permute-start | bytes 1572872 | tf_op jit(solution)/shard_map/ppermute | solution.py:544
  251.6 9.9 %collective-permute-start.43 = (f32[48,128]{1,0:T(8,128)}, f32[48,128]{1,0:T(8,128)S(1)}, u32[]{:S(2)}, u32[]{:S(2)}) collective-permute-start(f32[48,128]{1,0:T(8,128)} %stats.3.refs_4_), channel_id=1, source_target_pairs={{0,1},{1,0},{2,3},{3,2},{4,5},{5,4},{6,7},{7,6},{8,9},{9,8},{10,11... | collective-permute-start | bytes 73736 | tf_op jit(solution)/shard_map/ppermute | solution.py:657
  251.6 9.9 %collective-permute-start.44 = (f32[48,128]{1,0:T(8,128)}, f32[48,128]{1,0:T(8,128)S(1)}, u32[]{:S(2)}, u32[]{:S(2)}) collective-permute-start(f32[48,128]{1,0:T(8,128)} %stats.3.refs_4_), channel_id=1, source_target_pairs={{0,2},{1,3},{2,0},{3,1},{4,6},{5,7},{6,4},{7,5},{8,10},{9,11},{10,... | collective-permute-start | bytes 73736 | tf_op jit(solution)/shard_map/ppermute | solution.py:657
  252.3 9.2 %collective-permute-start.45 = (f32[48,128]{1,0:T(8,128)}, f32[48,128]{1,0:T(8,128)S(1)}, u32[]{:S(2)}, u32[]{:S(2)}) collective-permute-start(f32[48,128]{1,0:T(8,128)} %stats.3.refs_4_), channel_id=1, source_target_pairs={{0,3},{1,2},{2,1},{3,0},{4,7},{5,6},{6,5},{7,4},{8,11},{9,10},{10,... | collective-permute-start | bytes 73736 | tf_op jit(solution)/shard_map/ppermute | solution.py:657
  265.9 13.5 %collective-permute-start.46 = (f32[136,1024]{1,0:T(8,128)}, f32[136,1024]{1,0:T(8,128)}, u32[]{:S(2)}, u32[]{:S(2)}) collective-permute-start(f32[136,1024]{1,0:T(8,128)} %get-tuple-element.439.refs_7_), channel_id=1, source_target_pairs={{0,8},{8,16},{16,24},{24,28},{28,20},{20,12},{12,4},{4,0},{1,9},{9... | collective-permute-start | bytes 1671176 | tf_op jit(solution)/shard_map/ppermute | solution.py:544
  266.9 12.5 %collective-permute-start.47 = (f32[136,1024]{1,0:T(8,128)}, f32[136,1024]{1,0:T(8,128)}, u32[]{:S(2)}, u32[]{:S(2)}) collective-permute-start(f32[136,1024]{1,0:T(8,128)} %get-tuple-element.439.refs_7_), channel_id=1, source_target_pairs={{8,0},{16,8},{24,16},{28,24},{20,28},{12,20},{4,12},{0,4},{9,1},{1... | collective-permute-start | bytes 1671176 | tf_op jit(solution)/shard_map/ppermute | solution.py:544
  279.4 13.5 %collective-permute-start.48 = (f32[136,1024]{1,0:T(8,128)}, f32[136,1024]{1,0:T(8,128)S(1)}, u32[]{:S(2)}, u32[]{:S(2)}) collective-permute-start(f32[136,1024]{1,0:T(8,128)} %collective-permute-done.46.refs_8_), channel_id=1, source_target_pairs={{0,8},{8,16},{16,24},{24,28},{28,20},{20,12},{12,4},{4,0},{1,9},{9... | collective-permute-start | bytes 1671176 | tf_op jit(solution)/shard_map/ppermute | solution.py:544
  280.5 12.5 %collective-permute-start.49 = (f32[136,1024]{1,0:T(8,128)}, f32[136,1024]{1,0:T(8,128)S(1)}, u32[]{:S(2)}, u32[]{:S(2)}) collective-permute-start(f32[136,1024]{1,0:T(8,128)} %collective-permute-done.47.refs_9_), channel_id=1, source_target_pairs={{8,0},{16,8},{24,16},{28,24},{20,28},{12,20},{4,12},{0,4},{9,1},{1... | collective-permute-start | bytes 1671176 | tf_op jit(solution)/shard_map/ppermute | solution.py:544
  292.9 11.7 %collective-permute-start.50 = (f32[136,1024]{1,0:T(8,128)S(1)}, f32[136,1024]{1,0:T(8,128)S(1)}, u32[]{:S(2)}, u32[]{:S(2)}) collective-permute-start(f32[136,1024]{1,0:T(8,128)S(1)} %collective-permute-done.48.refs_10_), channel_id=1, source_target_pairs={{0,8},{8,16},{16,24},{24,28},{28,20},{20,12},{12,4},{4,0},{1,9},{9... | collective-permute-start | bytes 1671176 | tf_op jit(solution)/shard_map/ppermute | solution.py:544
  294.0 10.7 %collective-permute-start.51 = (f32[136,1024]{1,0:T(8,128)S(1)}, f32[136,1024]{1,0:T(8,128)S(1)}, u32[]{:S(2)}, u32[]{:S(2)}) collective-permute-start(f32[136,1024]{1,0:T(8,128)S(1)} %collective-permute-done.49.refs_11_), channel_id=1, source_target_pairs={{8,0},{16,8},{24,16},{28,24},{20,28},{12,20},{4,12},{0,4},{9,1},{1... | collective-permute-start | bytes 1671176 | tf_op jit(solution)/shard_map/ppermute | solution.py:544
  304.7 9.8 %collective-permute-start.52 = (f32[136,1024]{1,0:T(8,128)S(1)}, f32[136,1024]{1,0:T(8,128)S(1)}, u32[]{:S(2)}, u32[]{:S(2)}) collective-permute-start(f32[136,1024]{1,0:T(8,128)S(1)} %collective-permute-done.50.refs_12_), channel_id=1, source_target_pairs={{0,8},{8,16},{16,24},{24,28},{28,20},{20,12},{12,4},{4,0},{1,9},{9... | collective-permute-start | bytes 1671176 | tf_op jit(solution)/shard_map/ppermute | solution.py:544
  346.6 5.2 %collective-permute-start.55 = (f32[2,2816]{1,0:T(2,128)S(1)}, f32[2,2816]{1,0:T(2,128)S(1)}, u32[]{:S(2)}, u32[]{:S(2)}) collective-permute-start(f32[2,2816]{1,0:T(2,128)S(1)} %bitcast.16), channel_id=1, source_target_pairs={{0,3},{1,2},{2,1},{3,0},{4,7},{5,6},{6,5},{7,4},{8,11},{9,10},{10,... | collective-permute-start | bytes 67592 | tf_op jit(solution)/shard_map/ppermute | solution.py:657
  346.6 5.2 %collective-permute-start.54 = (f32[2,2816]{1,0:T(2,128)S(1)}, f32[2,2816]{1,0:T(2,128)S(1)}, u32[]{:S(2)}, u32[]{:S(2)}) collective-permute-start(f32[2,2816]{1,0:T(2,128)S(1)} %bitcast.17), channel_id=1, source_target_pairs={{0,2},{1,3},{2,0},{3,1},{4,6},{5,7},{6,4},{7,5},{8,10},{9,11},{10,... | collective-permute-start | bytes 67592 | tf_op jit(solution)/shard_map/ppermute | solution.py:657
  347.3 4.5 %collective-permute-start.53 = (f32[2,2816]{1,0:T(2,128)S(1)}, f32[2,2816]{1,0:T(2,128)S(1)}, u32[]{:S(2)}, u32[]{:S(2)}) collective-permute-start(f32[2,2816]{1,0:T(2,128)S(1)} %bitcast.18), channel_id=1, source_target_pairs={{0,1},{1,0},{2,3},{3,2},{4,5},{5,4},{6,7},{7,6},{8,9},{9,8},{10,11... | collective-permute-start | bytes 67592 | tf_op jit(solution)/shard_map/ppermute | solution.py:657
  (37 other events, 504.4 us)
